TPU v7x, 32 devices: a whole 2x2x4 slice. The times are simulated.
32 devices in a mesh: curve: 4 (over y, x), blk: 8 (over z, core).
Axes of the slice: x: 2, y: 2, z: 4, core: 2. Of those that a mesh axis runs over, the one named last changes fastest.
Arguments:
- anchors: bfloat16 [32768, 512], P(('curve', 'blk')), may hold values from -16 to 16
- keys: bfloat16 [4096, 512], P('blk'), may hold values from -16 to 16
- owners: int32 [32768, 1], P(('curve', 'blk')), may hold values from 0 to 7; in each aligned block of 1024 rows (0 to 1023, 1024 to 2047, ...) at most 256 rows name the same one
- key_rows: int32 [32768], P(('curve', 'blk')), may hold values from 0 to 511
Outputs:
- losses: float32 [32768], P(('curve', 'blk'))
- grad_anchors: float32 [32768, 512], P(('curve', 'blk'))
- lookup_derivative: float32 [4096, 512], P('blk')
Inputs may be any that keep to these rules, and one draw needn't show every extreme that they name: `owners`: among the rows of one device at most 256 name the same bank, a bound that some block reaches of them.
All inputs are finite; a program needn't handle non-finite values.
Results may differ from a plain program's by a relative error of at most 0.0037.
Values may be sent and summed in bfloat16 or wider, within the bound.
No kernel may reach another device: no remote copies, remote signals or barrier semaphores. Data moves between devices by JAX's collectives and lax.ppermute only.
A program may use at most 64 MiB of HBM per device.

v0:
```python
import functools

import jax
import jax.numpy as jnp
from jax import lax
from jax.experimental import pallas as pl
from jax.experimental.pallas import tpu as pltpu
from jax.sharding import PartitionSpec as P

STEPS = 4
DIVISOR = 0.07
TINY = 1e-06
LOG2E = 1.4426950408889634


F32 = jnp.float32
BF16 = jnp.bfloat16
VMEM = pl.BlockSpec(memory_space=pltpu.VMEM)
ANY = pl.BlockSpec(memory_space=pl.ANY)
SMEM = pl.BlockSpec(memory_space=pltpu.SMEM)


def call(body, outs, flops, *args, smem=1, scratch=(), placed=()):
    return pl.pallas_call(
        body,
        out_shape=[jax.ShapeDtypeStruct(s, d) for s, d in outs],
        in_specs=[SMEM] * smem + [VMEM] * (len(args) - smem),
        out_specs=[ANY if i in placed else VMEM for i in range(len(outs))],
        scratch_shapes=list(scratch),
        compiler_params=pltpu.CompilerParams(vmem_limit_bytes=48 * 1024 * 1024),
        cost_estimate=pl.CostEstimate(flops=flops, transcendentals=0, bytes_accessed=1 << 20),
    )(*args)


def unit(values):
    wide = values.astype(F32)
    length = jnp.sqrt(jnp.sum(wide * wide, axis=1, keepdims=True) + TINY)
    return wide / length, length


def nt_dot(left, right):
    return lax.dot_general(left, right, (((1,), (1,)), ((), ())), preferred_element_type=F32)


def nn_dot(left, right):
    return lax.dot_general(left, right, (((1,), (0,)), ((), ())), preferred_element_type=F32)


def sizes(whole, most):
    step = min(whole, most)
    while whole % step:
        step -= 1
    return step


def span(index, step):
    return pl.ds(pl.multiple_of(index * step, step), step)


def loop(count, body):
    lax.fori_loop(0, count, lambda index, carry: (body(index), carry)[1], 0)


def normalize_body(x_ref, o_ref):
    rows = x_ref.shape[0]
    step = sizes(rows, 128)

    def some(index):
        o_ref[span(index, step), :] = unit(x_ref[span(index, step), :])[0].astype(BF16)

    loop(rows // step, some)


def first_key(info_ref, distance, bank_rows, peers):
    return (info_ref[1] + 2 * distance) % peers * bank_rows


def scores_body(info_ref, *refs, distance, peers, curve, own_neg, par_neg, raw):
    pieces = 1 if raw else curve
    key_refs, refs = refs[:pieces], list(refs[pieces:])
    p_own, p_par, q_own, q_par, before, stats, turned = refs[:7]
    bank, refs = refs[-1], refs[7:-1]
    e_own = refs.pop(0) if own_neg else None
    e_par = refs.pop(0) if par_neg else None
    bank_rows = bank.shape[0]
    anchors = q_own.shape[0]
    step = sizes(anchors, 256)
    if raw:
        part = sizes(bank_rows, 128)

        def some(index):
            at = span(index, part)
            bank[at, :] = unit(key_refs[0][at, :])[0].astype(BF16)

        loop(bank_rows // part, some)
    else:
        for turn, key_ref in enumerate(key_refs):
            bank[span(info_ref[0] ^ turn, key_ref.shape[0]), :] = key_ref[...]
    turned[...] = bank[...].T
    base = first_key(info_ref, distance, bank_rows, peers)

    def side(row, q_ref, p_ref, e_ref, negative):
        def some(index):
            at = span(index, step)
            logits = nt_dot(bank[...], q_ref[at, :])
            ids = lax.broadcasted_iota(jnp.int32, (bank_rows, step), 0)
            found = jnp.sum(
                jnp.where(ids == p_ref[:, at] - base, logits, 0.0), axis=0, keepdims=True
            )
            total = before[row : row + 1, at]
            if negative:
                grown = jnp.exp2(logits * (LOG2E / DIVISOR))
                total = total + jnp.sum(grown, axis=0, keepdims=True)
                e_ref[:, at] = grown.astype(BF16)
            stats[row : row + 1, at] = total
            stats[row + 1 : row + 2, at] = before[row + 1 : row + 2, at] + found * (1.0 / DIVISOR)

        loop(anchors // step, some)

    side(0, q_own, p_own, e_own, own_neg)
    if par_neg:
        negative = (2 * distance + 2 * info_ref[2] - 1 + peers) % peers <= STEPS

        @pl.when(negative)
        def _():
            side(2, q_par, p_par, e_par, True)

        @pl.when(jnp.logical_not(negative))
        def _():
            e_par[...] = jnp.zeros_like(e_par)
            side(2, q_par, p_par, e_par, False)

    else:
        side(2, q_par, p_par, e_par, False)


def scalings(mine, other, row, at=slice(None)):
    score = mine[row + 1 : row + 2, at] + other[3 - row : 4 - row, at]
    grown = jnp.exp2(score * LOG2E)
    total = mine[row : row + 1, at] + other[2 - row : 3 - row, at] + grown
    inverse = 1.0 / total
    return inverse, grown * inverse - 1.0, total, score


def weights_of(e_ref, at, bank_rows, place, inverse, coef):
    ids = lax.broadcasted_iota(jnp.int32, (bank_rows, place.shape[1]), 0)
    weights = jnp.where(ids == place, coef, 0.0)
    if e_ref is not None:
        weights = weights + e_ref[:, at].astype(F32) * inverse
    return weights.astype(BF16)


def bank_grad_body(info_ref, *refs, distances, peers, curve, own_neg, par_neg):
    p_own, p_par, q_own, q_par, mine, other = refs[:6]
    refs = list(refs[6:])
    e_own = {d: refs.pop(0) if own_neg[d] else None for d in distances}
    e_par = {d: refs.pop(0) if par_neg[d] else None for d in distances}
    outs, grads = refs[:-1], refs[-1]
    bank_rows = grads.shape[0]
    rows = bank_rows // curve
    anchors = q_own.shape[0]
    step = sizes(anchors, 512)
    for number, d in enumerate(distances):
        base = first_key(info_ref, d, bank_rows, peers)
        grads[...] = jnp.zeros_like(grads)

        def side(row, q_ref, p_ref, e_ref):
            def some(index):
                at = span(index, step)
                inverse, coef, _, _ = scalings(mine, other, row, at)
                weights = weights_of(e_ref, at, bank_rows, p_ref[:, at] - base, inverse, coef)
                grads[...] += nn_dot(weights, q_ref[at, :])

            loop(anchors // step, some)

        side(0, q_own, p_own, e_own[d])
        side(2, q_par, p_par, e_par[d])
        for turn in range(curve):
            cut = grads[span(info_ref[0] ^ turn, rows), :]
            outs[turn][number * rows : (number + 1) * rows, :] = cut.astype(outs[turn].dtype)


def query_grad(info_ref, banks, grown, p_ref, mine, other, at, peers, row):
    bank_rows = banks[0].shape[1]
    inverse, coef, _, _ = scalings(mine, other, row, at)
    total = None
    for d, bank in enumerate(banks):
        place = p_ref[:, at] - first_key(info_ref, d, bank_rows, peers)
        part = nn_dot(bank[...], weights_of(grown[d], at, bank_rows, place, inverse, coef))
        total = part if total is None else total + part
    return total


def partner_grad_body(info_ref, p_ref, mine, other, *refs, negatives, peers):
    refs = list(refs)
    banks = [refs.pop(0) for _ in negatives]
    grown = [refs.pop(0) if negative else None for negative in negatives]
    out = refs.pop(0)
    anchors = p_ref.shape[1]
    step = sizes(anchors, 256)

    def some(index):
        at = span(index, step)
        out[:, at] = query_grad(info_ref, banks, grown, p_ref, mine, other, at, peers, 2)

    loop(anchors // step, some)


def anchor_body(info_ref, p_ref, mine, other, x_ref, received, *refs, negatives, peers):
    refs = list(refs)
    banks = [refs.pop(0) for _ in negatives]
    grown = [refs.pop(0) if negative else None for negative in negatives]
    out, loss, held, sems = refs
    anchors = p_ref.shape[1]
    step = sizes(anchors, 256)

    def copy(index):
        return pltpu.make_async_copy(
            held.at[span(index, step), :], out.at[span(index, step), :], sems.at[index]
        )

    def some(index):
        at = span(index, step)
        grad = query_grad(info_ref, banks, grown, p_ref, mine, other, at, peers, 0)
        grad = (grad + received[:, at]).T * (1.0 / DIVISOR)
        unit_vec, length = unit(x_ref[at, :])
        along = jnp.sum(unit_vec * grad, axis=1, keepdims=True)
        held[at, :] = (grad - unit_vec * along) / length
        copy(index).start()

    loop(anchors // step, some)
    _, _, total, score = scalings(mine, other, 0)
    loss[...] = jnp.log(total) - score
    loop(anchors // step, lambda index: copy(index).wait())


def key_body(x_ref, *refs):
    grads, out = refs[:-1], refs[-1]
    total = grads[0][...].astype(F32)
    for part in grads[1:]:
        total = total + part[...].astype(F32)
    grad = total * (1.0 / DIVISOR)
    unit_vec, length = unit(x_ref[...])
    along = jnp.sum(unit_vec * grad, axis=1, keepdims=True)
    out[...] = ((grad - unit_vec * along) / length).astype(out.dtype)


def add_body(*refs, count):
    grads, outs = refs[:-count], refs[-count:]
    rows = outs[0].shape[0]
    for number, out in enumerate(outs):
        at = slice(number * rows, (number + 1) * rows)
        total = grads[0][at, :].astype(F32)
        for part in grads[1:]:
            total = total + part[at, :].astype(F32)
        out[...] = total.astype(out.dtype)


def place_body(info_ref, *refs):
    parts, (out, held, sems) = refs[:-3], refs[-3:]
    rows = parts[0].shape[0]

    def copy(turn):
        at = span(info_ref[0] ^ turn, rows)
        return pltpu.make_async_copy(held.at[turn], out.at[at, :], sems.at[turn])

    for turn, part in enumerate(parts):
        held[turn] = part[...].astype(F32)
        copy(turn).start()
    for turn in range(len(parts)):
        copy(turn).wait()


def shards(anchors, keys, owners, key_rows):
    anchor_rows, width = anchors.shape
    bank_rows = keys.shape[0]
    curve = lax.axis_size("curve")
    peers = lax.axis_size("blk")
    pairs = peers // 2
    rows = bank_rows // curve
    at_curve = lax.axis_index("curve")
    at_blk = lax.axis_index("blk")
    lane = jnp.arange(4, dtype=jnp.int32)
    info = jnp.where(lane == 0, at_curve, jnp.where(lane == 1, at_blk, at_blk % 2)).astype(jnp.int32)
    block = 2 * bank_rows * anchor_rows * width

    def across(x):
        moved = [x]
        for turn in range(1, curve):
            moved.append(lax.ppermute(x, "curve", [(i, i ^ turn) for i in range(curve)]))
        return moved

    def exchange(parts):
        moved = [parts[0]]
        for turn in range(1, curve):
            route = [(i, i ^ turn) for i in range(curve)]
            moved.append(lax.ppermute(parts[turn], "curve", route))
        return moved

    def partner(x):
        return lax.ppermute(x, "blk", [(i, i ^ 1) for i in range(peers)])

    def from_ahead(x, distance):
        return lax.ppermute(x, "blk", [((i + 2 * distance) % peers, i) for i in range(peers)])

    def to_ahead(x, distance):
        return lax.ppermute(x, "blk", [(i, (i + 2 * distance) % peers) for i in range(peers)])

    far = far_order(pairs)
    neg_own = [2 * d % peers <= STEPS for d in range(pairs)]
    neg_par = [min((2 * d - 1) % peers, (2 * d + 1) % peers) <= STEPS for d in range(pairs)]

    own_keys = lax.dynamic_slice_in_dim(keys, at_curve * rows, rows, 0)
    (piece,) = call(normalize_body, [((rows, width), BF16)], 1 << 20, own_keys, smem=0)
    arrived = {d: from_ahead(piece, d) for d in far}
    (queries,) = call(normalize_body, [((anchor_rows, width), BF16)], 1 << 20, anchors, smem=0)
    queries_par = partner(queries)
    positive = (owners[:, 0] * bank_rows + key_rows).reshape(1, anchor_rows)
    positive_par = partner(positive)
    shared = (positive, positive_par, queries, queries_par)

    stats = jnp.zeros((4, anchor_rows), F32)
    banks, own_grown, par_grown = {}, {}, {}
    for d in [0] + far:
        parts = [keys] if d == 0 else across(arrived[d])
        outs = [((4, anchor_rows), F32), ((width, bank_rows), BF16)]
        outs += [((bank_rows, anchor_rows), BF16)] * (neg_own[d] + neg_par[d])
        results = call(
            functools.partial(
                scores_body,
                distance=d,
                peers=peers,
                curve=curve,
                own_neg=neg_own[d],
                par_neg=neg_par[d],
                raw=d == 0,
            ),
            outs,
            2 * block,
            info,
            *parts,
            *shared,
            stats,
            scratch=[pltpu.VMEM((bank_rows, width), BF16)],
        )
        stats, banks[d] = results[:2]
        results = list(results[2:])
        if neg_own[d]:
            own_grown[d] = results.pop(0)
        if neg_par[d]:
            par_grown[d] = results.pop(0)
    other = partner(stats)

    returned, final = [], []
    for group in grad_groups(pairs):
        parts = call(
            functools.partial(
                bank_grad_body,
                distances=group,
                peers=peers,
                curve=curve,
                own_neg=neg_own,
                par_neg=neg_par,
            ),
            [((len(group) * rows, width), F32)]
            + [((len(group) * rows, width), BF16)] * (curve - 1),
            2 * block * len(group),
            info,
            *shared,
            stats,
            other,
            *[own_grown[d] for d in group if neg_own[d]],
            *[par_grown[d] for d in group if neg_par[d]],
            scratch=[pltpu.VMEM((bank_rows, width), F32)],
        )
        parts = exchange(parts)
        if group == (0,):
            final = parts
            continue
        sums = call(
            functools.partial(add_body, count=len(group)),
            [((rows, width), BF16)] * len(group),
            1 << 20,
            *parts,
            smem=0,
        )
        returned += [to_ahead(x, d) for x, d in zip(sums, group)]

    own_banks = [banks[d] for d in range(pairs)]
    (sent,) = call(
        functools.partial(partner_grad_body, negatives=neg_par, peers=peers),
        [((width, anchor_rows), F32)],
        pairs * block,
        info,
        positive_par,
        stats,
        other,
        *own_banks,
        *[par_grown[d] for d in range(pairs) if neg_par[d]],
    )
    received = partner(sent)

    (mine,) = call(key_body, [((rows, width), BF16)], 1 << 20, own_keys, *final, *returned, smem=0)
    step = sizes(anchor_rows, 256)
    grad_anchors, losses = call(
        functools.partial(anchor_body, negatives=neg_own, peers=peers),
        [((anchor_rows, width), F32), ((1, anchor_rows), F32)],
        pairs * block,
        info,
        positive,
        stats,
        other,
        anchors,
        received,
        *own_banks,
        *[own_grown[d] for d in range(pairs) if neg_own[d]],
        scratch=[
            pltpu.VMEM((anchor_rows, width), F32),
            pltpu.SemaphoreType.DMA((anchor_rows // step,)),
        ],
        placed=(0,),
    )
    (lookup_derivative,) = call(
        place_body,
        [((bank_rows, width), F32)],
        1 << 20,
        info,
        *across(mine),
        scratch=[pltpu.VMEM((curve, rows, width), F32), pltpu.SemaphoreType.DMA((curve,))],
        placed=(0,),
    )
    return losses.reshape(anchor_rows), grad_anchors, lookup_derivative


def far_order(pairs):
    return sorted(range(1, pairs), key=lambda d: (min(d, pairs - d), d))


def grad_groups(pairs):
    return [tuple(sorted({d, pairs - d})) for d in range(pairs // 2, 0, -1)] + [(0,)]


def solution(mesh):
    return jax.shard_map(
        shards,
        mesh=mesh,
        in_specs=(
            P(("curve", "blk"), None),
            P("blk", None),
            P(("curve", "blk"), None),
            P(("curve", "blk")),
        ),
        out_specs=(P(("curve", "blk")), P(("curve", "blk"), None), P("blk", None)),
        check_vma=False,
    )
```

profile of v0, /device:TPU:0, one launch (start us, length us, event | category | flops | bytes accessed | tf_op | source)
XLA Modules:
  0.0 107.6 jit_solution(10474752336819169650)
XLA Ops:
  3.6 4.7 %collective-permute-start.10 = (bf16[128,512]{1,0:T(8,128)(2,1)S(1)}, bf16[128,512]{1,0:T(8,128)(2,1)S(1)}, u32[]{:S(2)}, u32[]{:S(2)}) collective-permute-start(bf16[128,512]{1,0:T(8,128)(2,1)S(1)} %shard_map.67), channel_id=1, source_target_pairs={{2,0},{3,1},{4,2},{5,3},{6,4},{7,5},{0,6},{1,7},{10,8},{11,9},{12,... | collective-permute-start | bytes 393224 | tf_op jit(solution)/shard_map/ppermute | solution.py:304
  9.3 2.9 %collective-permute-done.10.refs_0_ = bf16[128,512]{1,0:T(8,128)(2,1)S(1)} collective-permute-done((bf16[128,512]{1,0:T(8,128)(2,1)S(1)}, bf16[128,512]{1,0:T(8,128)(2,1)S(1)}, u32[]{:S(2)}, u32[]{:S(2)}) %collective-permute-start.10) | collective-permute-done | bytes 131104 | tf_op jit(solution)/shard_map/ppermute | solution.py:304
  14.9 1.5 %collective-permute-start.12 = (bf16[128,512]{1,0:T(8,128)(2,1)S(1)}, bf16[128,512]{1,0:T(8,128)(2,1)S(1)}, u32[]{:S(2)}, u32[]{:S(2)}) collective-permute-start(bf16[128,512]{1,0:T(8,128)(2,1)S(1)} %collective-permute-done.10.refs_0_), channel_id=1, source_target_pairs={{0,16},{8,24},{16,0},{24,8},{1,17},{9,25},{17,1},{25,9},{2,18},{10... | collective-permute-start | bytes 393224 | tf_op jit(solution)/shard_map/ppermute | solution.py:290
  16.5 2.4 %collective-permute-start.13 = (bf16[128,512]{1,0:T(8,128)(2,1)S(1)}, bf16[128,512]{1,0:T(8,128)(2,1)S(1)}, u32[]{:S(2)}, u32[]{:S(2)}) collective-permute-start(bf16[128,512]{1,0:T(8,128)(2,1)S(1)} %collective-permute-done.10.refs_0_), channel_id=1, source_target_pairs={{0,24},{8,16},{16,8},{24,0},{1,25},{9,17},{17,9},{25,1},{2,26},{10... | collective-permute-start | bytes 393224 | tf_op jit(solution)/shard_map/ppermute | solution.py:290
  21.9 1.5 %collective-permute-start.8 = (bf16[128,512]{1,0:T(8,128)(2,1)S(1)}, bf16[128,512]{1,0:T(8,128)(2,1)S(1)}, u32[]{:S(2)}, u32[]{:S(2)}) collective-permute-start(bf16[128,512]{1,0:T(8,128)(2,1)S(1)} %collective-permute-done.6.refs_0_), channel_id=1, source_target_pairs={{0,16},{8,24},{16,0},{24,8},{1,17},{9,25},{17,1},{25,9},{2,18},{10... | collective-permute-start | bytes 393224 | tf_op jit(solution)/shard_map/ppermute | solution.py:290
  23.9 4.1 %shard_map.69 = (f32[4,1024]{1,0:T(4,128)S(1)}, bf16[512,512]{1,0:T(8,128)(2,1)S(1)}, bf16[512,1024]{1,0:T(8,128)(2,1)S(1)}, bf16[512,1024]{1,0:T(8,128)(2,1)S(1)}) custom-call(s32[4]{0:T(128)S(1)} %compare_select_fusion.1.info_ref, bf16[512,512]{1,0:T(8,128)(2,1)S(1)} %copy-done.3, s32[1,1024]{1,0:T(1,128)S(1)} %bitcast.4, ...), custom_call_target="tpu_custom_call" | custom-call | flops 1073741824 | bytes 1048576 | tf_op jit(solution)/shard_map/pallas_call | solution.py:24
  28.0 1.5 %collective-permute-start.1 = (bf16[128,512]{1,0:T(8,128)(2,1)S(1)}, bf16[128,512]{1,0:T(8,128)(2,1)S(1)}, u32[]{:S(2)}, u32[]{:S(2)}) collective-permute-start(bf16[128,512]{1,0:T(8,128)(2,1)S(1)} %collective-permute-done.refs_0_), channel_id=1, source_target_pairs={{0,8},{8,0},{16,24},{24,16},{1,9},{9,1},{17,25},{25,17},{2,10},{10... | collective-permute-start | bytes 393224 | tf_op jit(solution)/shard_map/ppermute | solution.py:290
  29.5 1.5 %collective-permute-start.2 = (bf16[128,512]{1,0:T(8,128)(2,1)S(1)}, bf16[128,512]{1,0:T(8,128)(2,1)S(1)}, u32[]{:S(2)}, u32[]{:S(2)}) collective-permute-start(bf16[128,512]{1,0:T(8,128)(2,1)S(1)} %collective-permute-done.refs_0_), channel_id=1, source_target_pairs={{0,16},{8,24},{16,0},{24,8},{1,17},{9,25},{17,1},{25,9},{2,18},{10... | collective-permute-start | bytes 393224 | tf_op jit(solution)/shard_map/ppermute | solution.py:290
  31.5 3.6 %shard_map.70 = (f32[4,1024]{1,0:T(4,128)S(1)}, bf16[512,512]{1,0:T(8,128)(2,1)S(1)}, bf16[512,1024]{1,0:T(8,128)(2,1)S(1)}, bf16[512,1024]{1,0:T(8,128)(2,1)S(1)}) custom-call(s32[4]{0:T(128)S(1)} %compare_select_fusion.1.info_ref, bf16[128,512]{1,0:T(8,128)(2,1)S(1)} %collective-permute-done.10.refs_0_, ...), custom_call_target="tpu_custom_call" | custom-call | flops 1073741824 | bytes 1048576 | tf_op jit(solution)/shard_map/pallas_call | solution.py:24
  35.1 3.5 %shard_map.71 = (f32[4,1024]{1,0:T(4,128)S(1)}, bf16[512,512]{1,0:T(8,128)(2,1)S(1)}) custom-call(s32[4]{0:T(128)S(1)} %compare_select_fusion.1.info_ref, bf16[128,512]{1,0:T(8,128)(2,1)S(1)} %collective-permute-done.6.refs_0_, bf16[128,512]{1,0:T(8,128)(2,1)S(1)} %collective-permute-done.7.refs_1_, bf16[128,512]{1,0:T(8,128)(2,1)S(1)} %collective-permute-done.8.refs_2_, ...), custom_call_target="tpu_custom_call" | custom-call | flops 1073741824 | bytes 1048576 | tf_op jit(solution)/shard_map/pallas_call | solution.py:24
  38.7 3.6 %shard_map.72 = (f32[4,1024]{1,0:T(4,128)S(1)}, bf16[512,512]{1,0:T(8,128)(2,1)S(1)}, bf16[512,1024]{1,0:T(8,128)(2,1)S(1)}, bf16[512,1024]{1,0:T(8,128)(2,1)S(1)}) custom-call(s32[4]{0:T(128)S(1)} %compare_select_fusion.1.info_ref, bf16[128,512]{1,0:T(8,128)(2,1)S(1)} %collective-permute-done.refs_0_, bf16[128,512]{1,0:T(8,128)(2,1)S(1)} %collective-permute-done.1.refs_1_, ...), custom_call_target="tpu_custom_call" | custom-call | flops 1073741824 | bytes 1048576 | tf_op jit(solution)/shard_map/pallas_call | solution.py:24
  43.6 5.1 %shard_map.73 = f32[512,1024]{1,0:T(8,128)} custom-call(s32[4]{0:T(128)S(1)} %compare_select_fusion.1.info_ref, s32[1,1024]{1,0:T(1,128)S(1)} %collective-permute-done.4.refs_2_.refs_5_.p_ref.refs_1_, f32[4,1024]{1,0:T(4,128)S(1)} %get-tuple-element.36.mine.refs_4_, f32[4,1024]{1,0:T(4,128)S(1)} %collective-permute-done.14.other.refs_5_, ...), custom_call_target="tpu_custom_call" | custom-call | flops 2147483648 | bytes 1048576 | tf_op jit(solution)/shard_map/pallas_call | solution.py:24
  48.8 2.5 %shard_map.76 = (f32[128,512]{1,0:T(8,128)S(1)}, bf16[128,512]{1,0:T(8,128)(2,1)S(1)}, bf16[128,512]{1,0:T(8,128)(2,1)S(1)}, bf16[128,512]{1,0:T(8,128)(2,1)S(1)}) custom-call(s32[4]{0:T(128)S(1)} %compare_select_fusion.1.info_ref, s32[1,1024]{1,0:T(1,128)S(1)} %bitcast.8, s32[1,1024]{1,0:T(1,128)S(1)} %collective-permute-done.4.refs_2_.refs_5_.p_ref.refs_1_, ...), custom_call_target="tpu_custom_call" | custom-call | flops 1073741824 | bytes 1048576 | tf_op jit(solution)/shard_map/pallas_call | solution.py:24
  52.9 1.5 %collective-permute-start.20 = (bf16[128,512]{1,0:T(8,128)(2,1)S(1)}, bf16[128,512]{1,0:T(8,128)(2,1)S(1)}, u32[]{:S(2)}, u32[]{:S(2)}) collective-permute-start(bf16[128,512]{1,0:T(8,128)(2,1)S(1)} %get-tuple-element.55), channel_id=1, source_target_pairs={{0,16},{8,24},{16,0},{24,8},{1,17},{9,25},{17,1},{25,9},{2,18},{10... | collective-permute-start | bytes 393224 | tf_op jit(solution)/shard_map/ppermute | solution.py:297
  54.4 4.3 %shard_map.78 = (f32[256,512]{1,0:T(8,128)S(1)}, bf16[256,512]{1,0:T(8,128)(2,1)S(1)}, bf16[256,512]{1,0:T(8,128)(2,1)S(1)}, bf16[256,512]{1,0:T(8,128)(2,1)S(1)}) custom-call(s32[4]{0:T(128)S(1)} %compare_select_fusion.1.info_ref, s32[1,1024]{1,0:T(1,128)S(1)} %bitcast.9, s32[1,1024]{1,0:T(1,128)S(1)} %collective-permute-done.4.refs_2_.refs_5_.p_ref.refs_1_, ...), custom_call_target="tpu_custom_call" | custom-call | flops 2147483648 | bytes 1048576 | tf_op jit(solution)/shard_map/pallas_call | solution.py:24
  59.9 2.4 %collective-permute-start.25 = (bf16[256,512]{1,0:T(8,128)(2,1)S(1)}, bf16[256,512]{1,0:T(8,128)(2,1)S(1)}, u32[]{:S(2)}, u32[]{:S(2)}) collective-permute-start(bf16[256,512]{1,0:T(8,128)(2,1)S(1)} %get-tuple-element.60), channel_id=1, source_target_pairs={{0,24},{8,16},{16,8},{24,0},{1,25},{9,17},{17,9},{25,1},{2,26},{10... | collective-permute-start | bytes 786440 | tf_op jit(solution)/shard_map/ppermute | solution.py:297
  62.8 2.5 %shard_map.75 = (f32[128,512]{1,0:T(8,128)S(1)}, bf16[128,512]{1,0:T(8,128)(2,1)S(1)}, bf16[128,512]{1,0:T(8,128)(2,1)S(1)}, bf16[128,512]{1,0:T(8,128)(2,1)S(1)}) custom-call(s32[4]{0:T(128)S(1)} %compare_select_fusion.1.info_ref, s32[1,1024]{1,0:T(1,128)S(1)} %bitcast.10, s32[1,1024]{1,0:T(1,128)S(1)} %collective-permute-done.4.refs_2_.refs_5_.p_ref.refs_1_, ...), custom_call_target="tpu_custom_call" | custom-call | flops 1073741824 | bytes 1048576 | tf_op jit(solution)/shard_map/pallas_call | solution.py:24
  65.4 9.9 %collective-permute-done.21.refs_3_ = bf16[128,512]{1,0:T(8,128)(2,1)S(1)} collective-permute-done((bf16[128,512]{1,0:T(8,128)(2,1)S(1)}, bf16[128,512]{1,0:T(8,128)(2,1)S(1)}, u32[]{:S(2)}, u32[]{:S(2)}) %collective-permute-start.21) | collective-permute-done | bytes 131104 | tf_op jit(solution)/shard_map/ppermute | solution.py:297
  79.5 1.7 %collective-permute-done.16.refs_1_ = bf16[128,512]{1,0:T(8,128)(2,1)S(1)} collective-permute-done((bf16[128,512]{1,0:T(8,128)(2,1)S(1)}, bf16[128,512]{1,0:T(8,128)(2,1)S(1)}, u32[]{:S(2)}, u32[]{:S(2)}) %collective-permute-start.16) | collective-permute-done | bytes 131104 | tf_op jit(solution)/shard_map/ppermute | solution.py:297
  82.1 2.9 %collective-permute-start.27 = (bf16[128,512]{1,0:T(8,128)(2,1)S(1)}, bf16[128,512]{1,0:T(8,128)(2,1)S(1)}, u32[]{:S(2)}, u32[]{:S(2)}) collective-permute-start(bf16[128,512]{1,0:T(8,128)(2,1)S(1)} %get-tuple-element.62), channel_id=1, source_target_pairs={{0,6},{1,7},{2,0},{3,1},{4,2},{5,3},{6,4},{7,5},{8,14},{9,15},{10,... | collective-permute-start | bytes 393224 | tf_op jit(solution)/shard_map/ppermute | solution.py:307
  85.0 4.5 %collective-permute-done.22.refs_4_ = bf16[128,512]{1,0:T(8,128)(2,1)S(1)} collective-permute-done((bf16[128,512]{1,0:T(8,128)(2,1)S(1)}, bf16[128,512]{1,0:T(8,128)(2,1)S(1)}, u32[]{:S(2)}, u32[]{:S(2)}) %collective-permute-start.22) | collective-permute-done | bytes 131104 | tf_op jit(solution)/shard_map/ppermute | solution.py:307
  96.1 2.4 %collective-permute-done.30.refs_3_ = bf16[128,512]{1,0:T(8,128)(2,1)S(1)} collective-permute-done((bf16[128,512]{1,0:T(8,128)(2,1)S(1)}, bf16[128,512]{1,0:T(8,128)(2,1)S(1)}, u32[]{:S(2)}, u32[]{:S(2)}) %collective-permute-start.30) | collective-permute-done | bytes 131104 | tf_op jit(solution)/shard_map/ppermute | solution.py:290
  98.5 1.6 %shard_map.81 = f32[512,512]{1,0:T(8,128)} custom-call(s32[4]{0:T(128)S(1)} %compare_select_fusion.1.info_ref, bf16[128,512]{1,0:T(8,128)(2,1)S(1)} %shard_map.80.refs_0_, bf16[128,512]{1,0:T(8,128)(2,1)S(1)} %collective-permute-done.28.refs_1_, bf16[128,512]{1,0:T(8,128)(2,1)S(1)} %collective-permute-done.29.refs_2_, ...), custom_call_target="tpu_custom_call" | custom-call | flops 1048576 | bytes 1048576 | tf_op jit(solution)/shard_map/pallas_call | solution.py:24
  100.1 7.5 %shard_map.74 = (f32[1024,512]{1,0:T(8,128)}, f32[1,1024]{1,0:T(1,128)}) custom-call(s32[4]{0:T(128)S(1)} %compare_select_fusion.1.info_ref, s32[1,1024]{1,0:T(1,128)S(1)} %bitcast.11, f32[4,1024]{1,0:T(4,128)S(1)} %get-tuple-element.36.mine.refs_4_, f32[4,1024]{1,0:T(4,128)S(1)} %collective-permute-done.14.other.refs_5_, bf16[1024,512]{1,0:T(8,128)(2,1)S(1)} %copy-done.2, ...), custom_call_target="tpu_custom_call" | custom-call | flops 2147483648 | bytes 1048576 | tf_op jit(solution)/shard_map/pallas_call | solution.py:24
  (70 shorter events, 26.9 us)
Async XLA Ops:
  2.9 20.5 %collective-permute-start.5 = (bf16[1024,512]{1,0:T(8,128)(2,1)S(1)}, bf16[1024,512]{1,0:T(8,128)(2,1)S(1)}, u32[]{:S(2)}, u32[]{:S(2)}) collective-permute-start(bf16[1024,512]{1,0:T(8,128)(2,1)S(1)} %shard_map.68.refs_3_.refs_6_.refs_2_), channel_id=1, source_target_pairs={{0,1},{1,0},{2,3},{3,2},{4,5},{5,4},{6,7},{7,6},{8,9},{9,8},{10,11... | collective-permute-start | bytes 3145736 | tf_op jit(solution)/shard_map/ppermute | solution.py:301
  3.6 8.6 %collective-permute-start.10 = (bf16[128,512]{1,0:T(8,128)(2,1)S(1)}, bf16[128,512]{1,0:T(8,128)(2,1)S(1)}, u32[]{:S(2)}, u32[]{:S(2)}) collective-permute-start(bf16[128,512]{1,0:T(8,128)(2,1)S(1)} %shard_map.67), channel_id=1, source_target_pairs={{2,0},{3,1},{4,2},{5,3},{6,4},{7,5},{0,6},{1,7},{10,8},{11,9},{12,... | collective-permute-start | bytes 393224 | tf_op jit(solution)/shard_map/ppermute | solution.py:304
  8.3 8.3 %collective-permute-start.6 = (bf16[128,512]{1,0:T(8,128)(2,1)S(1)}, bf16[128,512]{1,0:T(8,128)(2,1)S(1)}, u32[]{:S(2)}, u32[]{:S(2)}) collective-permute-start(bf16[128,512]{1,0:T(8,128)(2,1)S(1)} %shard_map.67), channel_id=1, source_target_pairs={{6,0},{7,1},{0,2},{1,3},{2,4},{3,5},{4,6},{5,7},{14,8},{15,9},{8,1... | collective-permute-start | bytes 393224 | tf_op jit(solution)/shard_map/ppermute | solution.py:304
  8.3 12.1 %collective-permute-start = (bf16[128,512]{1,0:T(8,128)(2,1)S(1)}, bf16[128,512]{1,0:T(8,128)(2,1)S(1)}, u32[]{:S(2)}, u32[]{:S(2)}) collective-permute-start(bf16[128,512]{1,0:T(8,128)(2,1)S(1)} %shard_map.67), channel_id=1, source_target_pairs={{4,0},{5,1},{6,2},{7,3},{0,4},{1,5},{2,6},{3,7},{12,8},{13,9},{14,... | collective-permute-start | bytes 393224 | tf_op jit(solution)/shard_map/ppermute | solution.py:304
  12.2 9.7 %collective-permute-start.11 = (bf16[128,512]{1,0:T(8,128)(2,1)S(1)}, bf16[128,512]{1,0:T(8,128)(2,1)S(1)}, u32[]{:S(2)}, u32[]{:S(2)}) collective-permute-start(bf16[128,512]{1,0:T(8,128)(2,1)S(1)} %collective-permute-done.10.refs_0_), channel_id=1, source_target_pairs={{0,8},{8,0},{16,24},{24,16},{1,9},{9,1},{17,25},{25,17},{2,10},{10... | collective-permute-start | bytes 393224 | tf_op jit(solution)/shard_map/ppermute | solution.py:290
  14.9 13.0 %collective-permute-start.12 = (bf16[128,512]{1,0:T(8,128)(2,1)S(1)}, bf16[128,512]{1,0:T(8,128)(2,1)S(1)}, u32[]{:S(2)}, u32[]{:S(2)}) collective-permute-start(bf16[128,512]{1,0:T(8,128)(2,1)S(1)} %collective-permute-done.10.refs_0_), channel_id=1, source_target_pairs={{0,16},{8,24},{16,0},{24,8},{1,17},{9,25},{17,1},{25,9},{2,18},{10... | collective-permute-start | bytes 393224 | tf_op jit(solution)/shard_map/ppermute | solution.py:290
  16.5 13.0 %collective-permute-start.13 = (bf16[128,512]{1,0:T(8,128)(2,1)S(1)}, bf16[128,512]{1,0:T(8,128)(2,1)S(1)}, u32[]{:S(2)}, u32[]{:S(2)}) collective-permute-start(bf16[128,512]{1,0:T(8,128)(2,1)S(1)} %collective-permute-done.10.refs_0_), channel_id=1, source_target_pairs={{0,24},{8,16},{16,8},{24,0},{1,25},{9,17},{17,9},{25,1},{2,26},{10... | collective-permute-start | bytes 393224 | tf_op jit(solution)/shard_map/ppermute | solution.py:290
  20.4 10.7 %collective-permute-start.7 = (bf16[128,512]{1,0:T(8,128)(2,1)S(1)}, bf16[128,512]{1,0:T(8,128)(2,1)S(1)}, u32[]{:S(2)}, u32[]{:S(2)}) collective-permute-start(bf16[128,512]{1,0:T(8,128)(2,1)S(1)} %collective-permute-done.6.refs_0_), channel_id=1, source_target_pairs={{0,8},{8,0},{16,24},{24,16},{1,9},{9,1},{17,25},{25,17},{2,10},{10... | collective-permute-start | bytes 393224 | tf_op jit(solution)/shard_map/ppermute | solution.py:290
  21.9 13.3 %collective-permute-start.8 = (bf16[128,512]{1,0:T(8,128)(2,1)S(1)}, bf16[128,512]{1,0:T(8,128)(2,1)S(1)}, u32[]{:S(2)}, u32[]{:S(2)}) collective-permute-start(bf16[128,512]{1,0:T(8,128)(2,1)S(1)} %collective-permute-done.6.refs_0_), channel_id=1, source_target_pairs={{0,16},{8,24},{16,0},{24,8},{1,17},{9,25},{17,1},{25,9},{2,18},{10... | collective-permute-start | bytes 393224 | tf_op jit(solution)/shard_map/ppermute | solution.py:290
  23.4 11.7 %collective-permute-start.9 = (bf16[128,512]{1,0:T(8,128)(2,1)S(1)}, bf16[128,512]{1,0:T(8,128)(2,1)S(1)}, u32[]{:S(2)}, u32[]{:S(2)}) collective-permute-start(bf16[128,512]{1,0:T(8,128)(2,1)S(1)} %collective-permute-done.6.refs_0_), channel_id=1, source_target_pairs={{0,24},{8,16},{16,8},{24,0},{1,25},{9,17},{17,9},{25,1},{2,26},{10... | collective-permute-start | bytes 393224 | tf_op jit(solution)/shard_map/ppermute | solution.py:290
  28.0 10.7 %collective-permute-start.1 = (bf16[128,512]{1,0:T(8,128)(2,1)S(1)}, bf16[128,512]{1,0:T(8,128)(2,1)S(1)}, u32[]{:S(2)}, u32[]{:S(2)}) collective-permute-start(bf16[128,512]{1,0:T(8,128)(2,1)S(1)} %collective-permute-done.refs_0_), channel_id=1, source_target_pairs={{0,8},{8,0},{16,24},{24,16},{1,9},{9,1},{17,25},{25,17},{2,10},{10... | collective-permute-start | bytes 393224 | tf_op jit(solution)/shard_map/ppermute | solution.py:290
  29.5 9.2 %collective-permute-start.2 = (bf16[128,512]{1,0:T(8,128)(2,1)S(1)}, bf16[128,512]{1,0:T(8,128)(2,1)S(1)}, u32[]{:S(2)}, u32[]{:S(2)}) collective-permute-start(bf16[128,512]{1,0:T(8,128)(2,1)S(1)} %collective-permute-done.refs_0_), channel_id=1, source_target_pairs={{0,16},{8,24},{16,0},{24,8},{1,17},{9,25},{17,1},{25,9},{2,18},{10... | collective-permute-start | bytes 393224 | tf_op jit(solution)/shard_map/ppermute | solution.py:290
  31.0 7.7 %collective-permute-start.3 = (bf16[128,512]{1,0:T(8,128)(2,1)S(1)}, bf16[128,512]{1,0:T(8,128)(2,1)S(1)}, u32[]{:S(2)}, u32[]{:S(2)}) collective-permute-start(bf16[128,512]{1,0:T(8,128)(2,1)S(1)} %collective-permute-done.refs_0_), channel_id=1, source_target_pairs={{0,24},{8,16},{16,8},{24,0},{1,25},{9,17},{17,9},{25,1},{2,26},{10... | collective-permute-start | bytes 393224 | tf_op jit(solution)/shard_map/ppermute | solution.py:290
  48.7 51.4 %collective-permute-start.15 = (f32[512,1024]{1,0:T(8,128)}, f32[512,1024]{1,0:T(8,128)}, u32[]{:S(2)}, u32[]{:S(2)}) collective-permute-start(f32[512,1024]{1,0:T(8,128)} %shard_map.73), channel_id=1, source_target_pairs={{0,1},{1,0},{2,3},{3,2},{4,5},{5,4},{6,7},{7,6},{8,9},{9,8},{10,11... | collective-permute-start | bytes 6291464 | tf_op jit(solution)/shard_map/ppermute | solution.py:301
  51.4 8.5 %collective-permute-start.19 = (bf16[128,512]{1,0:T(8,128)(2,1)S(1)}, bf16[128,512]{1,0:T(8,128)(2,1)S(1)}, u32[]{:S(2)}, u32[]{:S(2)}) collective-permute-start(bf16[128,512]{1,0:T(8,128)(2,1)S(1)} %get-tuple-element.54), channel_id=1, source_target_pairs={{0,8},{8,0},{16,24},{24,16},{1,9},{9,1},{17,25},{25,17},{2,10},{10... | collective-permute-start | bytes 393224 | tf_op jit(solution)/shard_map/ppermute | solution.py:297
  52.9 9.5 %collective-permute-start.20 = (bf16[128,512]{1,0:T(8,128)(2,1)S(1)}, bf16[128,512]{1,0:T(8,128)(2,1)S(1)}, u32[]{:S(2)}, u32[]{:S(2)}) collective-permute-start(bf16[128,512]{1,0:T(8,128)(2,1)S(1)} %get-tuple-element.55), channel_id=1, source_target_pairs={{0,16},{8,24},{16,0},{24,8},{1,17},{9,25},{17,1},{25,9},{2,18},{10... | collective-permute-start | bytes 393224 | tf_op jit(solution)/shard_map/ppermute | solution.py:297
  58.8 17.1 %collective-permute-start.23 = (bf16[256,512]{1,0:T(8,128)(2,1)S(1)}, bf16[256,512]{1,0:T(8,128)(2,1)S(1)}, u32[]{:S(2)}, u32[]{:S(2)}) collective-permute-start(bf16[256,512]{1,0:T(8,128)(2,1)S(1)} %get-tuple-element.58), channel_id=1, source_target_pairs={{0,8},{8,0},{16,24},{24,16},{1,9},{9,1},{17,25},{25,17},{2,10},{10... | collective-permute-start | bytes 786440 | tf_op jit(solution)/shard_map/ppermute | solution.py:297
  59.4 18.1 %collective-permute-start.24 = (bf16[256,512]{1,0:T(8,128)(2,1)S(1)}, bf16[256,512]{1,0:T(8,128)(2,1)S(1)}, u32[]{:S(2)}, u32[]{:S(2)}) collective-permute-start(bf16[256,512]{1,0:T(8,128)(2,1)S(1)} %get-tuple-element.59), channel_id=1, source_target_pairs={{0,16},{8,24},{16,0},{24,8},{1,17},{9,25},{17,1},{25,9},{2,18},{10... | collective-permute-start | bytes 786440 | tf_op jit(solution)/shard_map/ppermute | solution.py:297
  59.9 19.0 %collective-permute-start.25 = (bf16[256,512]{1,0:T(8,128)(2,1)S(1)}, bf16[256,512]{1,0:T(8,128)(2,1)S(1)}, u32[]{:S(2)}, u32[]{:S(2)}) collective-permute-start(bf16[256,512]{1,0:T(8,128)(2,1)S(1)} %get-tuple-element.60), channel_id=1, source_target_pairs={{0,24},{8,16},{16,8},{24,0},{1,25},{9,17},{17,9},{25,1},{2,26},{10... | collective-permute-start | bytes 786440 | tf_op jit(solution)/shard_map/ppermute | solution.py:297
  62.3 13.0 %collective-permute-start.21 = (bf16[128,512]{1,0:T(8,128)(2,1)S(1)}, bf16[128,512]{1,0:T(8,128)(2,1)S(1)}, u32[]{:S(2)}, u32[]{:S(2)}) collective-permute-start(bf16[128,512]{1,0:T(8,128)(2,1)S(1)} %get-tuple-element.56), channel_id=1, source_target_pairs={{0,24},{8,16},{16,8},{24,0},{1,25},{9,17},{17,9},{25,1},{2,26},{10... | collective-permute-start | bytes 393224 | tf_op jit(solution)/shard_map/ppermute | solution.py:297
  77.5 7.6 %collective-permute-start.18 = (bf16[128,512]{1,0:T(8,128)(2,1)S(1)}, bf16[128,512]{1,0:T(8,128)(2,1)S(1)}, u32[]{:S(2)}, u32[]{:S(2)}) collective-permute-start(bf16[128,512]{1,0:T(8,128)(2,1)S(1)} %get-tuple-element.52), channel_id=1, source_target_pairs={{0,24},{8,16},{16,8},{24,0},{1,25},{9,17},{17,9},{25,1},{2,26},{10... | collective-permute-start | bytes 393224 | tf_op jit(solution)/shard_map/ppermute | solution.py:297
  78.9 10.6 %collective-permute-start.22 = (bf16[128,512]{1,0:T(8,128)(2,1)S(1)}, bf16[128,512]{1,0:T(8,128)(2,1)S(1)}, u32[]{:S(2)}, u32[]{:S(2)}) collective-permute-start(bf16[128,512]{1,0:T(8,128)(2,1)S(1)} %shard_map.77), channel_id=1, source_target_pairs={{0,4},{1,5},{2,6},{3,7},{4,0},{5,1},{6,2},{7,3},{8,12},{9,13},{10,... | collective-permute-start | bytes 393224 | tf_op jit(solution)/shard_map/ppermute | solution.py:307
  81.2 8.3 %collective-permute-start.26 = (bf16[128,512]{1,0:T(8,128)(2,1)S(1)}, bf16[128,512]{1,0:T(8,128)(2,1)S(1)}, u32[]{:S(2)}, u32[]{:S(2)}) collective-permute-start(bf16[128,512]{1,0:T(8,128)(2,1)S(1)} %get-tuple-element.61), channel_id=1, source_target_pairs={{0,2},{1,3},{2,4},{3,5},{4,6},{5,7},{6,0},{7,1},{8,10},{9,11},{10,... | collective-permute-start | bytes 393224 | tf_op jit(solution)/shard_map/ppermute | solution.py:307
  82.1 7.8 %collective-permute-start.27 = (bf16[128,512]{1,0:T(8,128)(2,1)S(1)}, bf16[128,512]{1,0:T(8,128)(2,1)S(1)}, u32[]{:S(2)}, u32[]{:S(2)}) collective-permute-start(bf16[128,512]{1,0:T(8,128)(2,1)S(1)} %get-tuple-element.62), channel_id=1, source_target_pairs={{0,6},{1,7},{2,0},{3,1},{4,2},{5,3},{6,4},{7,5},{8,14},{9,15},{10,... | collective-permute-start | bytes 393224 | tf_op jit(solution)/shard_map/ppermute | solution.py:307
  (13 other events, 84.2 us)
where the time goes:
time: 108 us
  Pallas kernels  40 us (37%)
  starting transfers between devices  37.3 us (35%)
  waiting for transfers between devices  28.2 us (26%)
  local copies, waits for them, and re-layouts  1.25 us (1%)
    pallas_call x15, Pallas kernels, call(): pl.pallas_call(body, out_shape=[jax.ShapeDtypeStruct(s, d) for s, d in ou...  40 us
    ppermute x12, starting transfers between devices, across(): lax.ppermute(x, 'curve', [(i, i ^ turn) for i in range(curve)])  16 us
    ppermute x9, waiting for transfers between devices, exchange(): moved.append(lax.ppermute(parts[turn], 'curve', route))  11.8 us
    ppermute x9, starting transfers between devices, exchange(): moved.append(lax.ppermute(parts[turn], 'curve', route))  10.7 us
    ppermute x3, starting transfers between devices, from_ahead(): lax.ppermute(x, 'blk', [((i + 2 * distance) % peers, i) for i in range(pe...  5.69 us
    ppermute x3, waiting for transfers between devices, to_ahead(): lax.ppermute(x, 'blk', [(i, (i + 2 * distance) % peers) for i in range(pe...  4.87 us
    ppermute x12, waiting for transfers between devices, across(): lax.ppermute(x, 'curve', [(i, i ^ turn) for i in range(curve)])  4.8 us
    ppermute x3, waiting for transfers between devices, from_ahead(): lax.ppermute(x, 'blk', [((i + 2 * distance) % peers, i) for i in range(pe...  4.38 us
  transfers between devices with their start and end apart: 31, of which 13 were waited for; matrix products, arithmetic and copies ran while one was open for 0% of the time, Pallas kernels for 21%

commit v1 on v0

--- a/solution.py
+++ b/solution.py
@@ -17,14 +17,13 @@
 BF16 = jnp.bfloat16
 VMEM = pl.BlockSpec(memory_space=pltpu.VMEM)
 ANY = pl.BlockSpec(memory_space=pl.ANY)
-SMEM = pl.BlockSpec(memory_space=pltpu.SMEM)
-
-
-def call(body, outs, flops, *args, smem=1, scratch=(), placed=()):
+
+
+def call(body, outs, flops, *args, scratch=(), placed=()):
     return pl.pallas_call(
         body,
         out_shape=[jax.ShapeDtypeStruct(s, d) for s, d in outs],
-        in_specs=[SMEM] * smem + [VMEM] * (len(args) - smem),
+        in_specs=[VMEM] * len(args),
         out_specs=[ANY if i in placed else VMEM for i in range(len(outs))],
         scratch_shapes=list(scratch),
         compiler_params=pltpu.CompilerParams(vmem_limit_bytes=48 * 1024 * 1024),
@@ -54,11 +53,14 @@
 
 
 def span(index, step):
+    if isinstance(index, int):
+        return slice(index * step, (index + 1) * step)
     return pl.ds(pl.multiple_of(index * step, step), step)
 
 
 def loop(count, body):
-    lax.fori_loop(0, count, lambda index, carry: (body(index), carry)[1], 0)
+    for index in range(count):
+        body(index)
 
 
 def normalize_body(x_ref, o_ref):
@@ -71,11 +73,11 @@
     loop(rows // step, some)
 
 
-def first_key(info_ref, distance, bank_rows, peers):
-    return (info_ref[1] + 2 * distance) % peers * bank_rows
-
-
-def scores_body(info_ref, *refs, distance, peers, curve, own_neg, par_neg, raw):
+def first_key(distance, bank_rows, peers):
+    return (lax.axis_index("blk") + 2 * distance) % peers * bank_rows
+
+
+def scores_body(*refs, distance, peers, curve, own_neg, par_neg, raw):
     pieces = 1 if raw else curve
     key_refs, refs = refs[:pieces], list(refs[pieces:])
     p_own, p_par, q_own, q_par, before, stats, turned = refs[:7]
@@ -95,9 +97,9 @@
         loop(bank_rows // part, some)
     else:
         for turn, key_ref in enumerate(key_refs):
-            bank[span(info_ref[0] ^ turn, key_ref.shape[0]), :] = key_ref[...]
+            bank[span(lax.axis_index("curve") ^ turn, key_ref.shape[0]), :] = key_ref[...]
     turned[...] = bank[...].T
-    base = first_key(info_ref, distance, bank_rows, peers)
+    base = first_key(distance, bank_rows, peers)
 
     def side(row, q_ref, p_ref, e_ref, negative):
         def some(index):
@@ -119,7 +121,7 @@
 
     side(0, q_own, p_own, e_own, own_neg)
     if par_neg:
-        negative = (2 * distance + 2 * info_ref[2] - 1 + peers) % peers <= STEPS
+        negative = (2 * distance + 2 * (lax.axis_index("blk") % 2) - 1 + peers) % peers <= STEPS
 
         @pl.when(negative)
         def _():
@@ -150,7 +152,7 @@
     return weights.astype(BF16)
 
 
-def bank_grad_body(info_ref, *refs, distances, peers, curve, own_neg, par_neg):
+def bank_grad_body(*refs, distances, peers, curve, own_neg, par_neg):
     p_own, p_par, q_own, q_par, mine, other = refs[:6]
     refs = list(refs[6:])
     e_own = {d: refs.pop(0) if own_neg[d] else None for d in distances}
@@ -161,7 +163,7 @@
     anchors = q_own.shape[0]
     step = sizes(anchors, 512)
     for number, d in enumerate(distances):
-        base = first_key(info_ref, d, bank_rows, peers)
+        base = first_key(d, bank_rows, peers)
         grads[...] = jnp.zeros_like(grads)
 
         def side(row, q_ref, p_ref, e_ref):
@@ -176,22 +178,22 @@
         side(0, q_own, p_own, e_own[d])
         side(2, q_par, p_par, e_par[d])
         for turn in range(curve):
-            cut = grads[span(info_ref[0] ^ turn, rows), :]
+            cut = grads[span(lax.axis_index("curve") ^ turn, rows), :]
             outs[turn][number * rows : (number + 1) * rows, :] = cut.astype(outs[turn].dtype)
 
 
-def query_grad(info_ref, banks, grown, p_ref, mine, other, at, peers, row):
+def query_grad(banks, grown, p_ref, mine, other, at, peers, row):
     bank_rows = banks[0].shape[1]
     inverse, coef, _, _ = scalings(mine, other, row, at)
     total = None
     for d, bank in enumerate(banks):
-        place = p_ref[:, at] - first_key(info_ref, d, bank_rows, peers)
+        place = p_ref[:, at] - first_key(d, bank_rows, peers)
         part = nn_dot(bank[...], weights_of(grown[d], at, bank_rows, place, inverse, coef))
         total = part if total is None else total + part
     return total
 
 
-def partner_grad_body(info_ref, p_ref, mine, other, *refs, negatives, peers):
+def partner_grad_body(p_ref, mine, other, *refs, negatives, peers):
     refs = list(refs)
     banks = [refs.pop(0) for _ in negatives]
     grown = [refs.pop(0) if negative else None for negative in negatives]
@@ -201,12 +203,12 @@
 
     def some(index):
         at = span(index, step)
-        out[:, at] = query_grad(info_ref, banks, grown, p_ref, mine, other, at, peers, 2)
+        out[:, at] = query_grad(banks, grown, p_ref, mine, other, at, peers, 2)
 
     loop(anchors // step, some)
 
 
-def anchor_body(info_ref, p_ref, mine, other, x_ref, received, *refs, negatives, peers):
+def anchor_body(p_ref, mine, other, x_ref, received, *refs, negatives, peers):
     refs = list(refs)
     banks = [refs.pop(0) for _ in negatives]
     grown = [refs.pop(0) if negative else None for negative in negatives]
@@ -221,7 +223,7 @@
 
     def some(index):
         at = span(index, step)
-        grad = query_grad(info_ref, banks, grown, p_ref, mine, other, at, peers, 0)
+        grad = query_grad(banks, grown, p_ref, mine, other, at, peers, 0)
         grad = (grad + received[:, at]).T * (1.0 / DIVISOR)
         unit_vec, length = unit(x_ref[at, :])
         along = jnp.sum(unit_vec * grad, axis=1, keepdims=True)
@@ -256,12 +258,12 @@
         out[...] = total.astype(out.dtype)
 
 
-def place_body(info_ref, *refs):
+def place_body(*refs):
     parts, (out, held, sems) = refs[:-3], refs[-3:]
     rows = parts[0].shape[0]
 
     def copy(turn):
-        at = span(info_ref[0] ^ turn, rows)
+        at = span(lax.axis_index("curve") ^ turn, rows)
         return pltpu.make_async_copy(held.at[turn], out.at[at, :], sems.at[turn])
 
     for turn, part in enumerate(parts):
@@ -279,9 +281,6 @@
     pairs = peers // 2
     rows = bank_rows // curve
     at_curve = lax.axis_index("curve")
-    at_blk = lax.axis_index("blk")
-    lane = jnp.arange(4, dtype=jnp.int32)
-    info = jnp.where(lane == 0, at_curve, jnp.where(lane == 1, at_blk, at_blk % 2)).astype(jnp.int32)
     block = 2 * bank_rows * anchor_rows * width
 
     def across(x):
@@ -311,9 +310,9 @@
     neg_par = [min((2 * d - 1) % peers, (2 * d + 1) % peers) <= STEPS for d in range(pairs)]
 
     own_keys = lax.dynamic_slice_in_dim(keys, at_curve * rows, rows, 0)
-    (piece,) = call(normalize_body, [((rows, width), BF16)], 1 << 20, own_keys, smem=0)
+    (piece,) = call(normalize_body, [((rows, width), BF16)], 1 << 20, own_keys)
     arrived = {d: from_ahead(piece, d) for d in far}
-    (queries,) = call(normalize_body, [((anchor_rows, width), BF16)], 1 << 20, anchors, smem=0)
+    (queries,) = call(normalize_body, [((anchor_rows, width), BF16)], 1 << 20, anchors)
     queries_par = partner(queries)
     positive = (owners[:, 0] * bank_rows + key_rows).reshape(1, anchor_rows)
     positive_par = partner(positive)
@@ -337,7 +336,6 @@
             ),
             outs,
             2 * block,
-            info,
             *parts,
             *shared,
             stats,
@@ -365,7 +363,6 @@
             [((len(group) * rows, width), F32)]
             + [((len(group) * rows, width), BF16)] * (curve - 1),
             2 * block * len(group),
-            info,
             *shared,
             stats,
             other,
@@ -382,7 +379,6 @@
             [((rows, width), BF16)] * len(group),
             1 << 20,
             *parts,
-            smem=0,
         )
         returned += [to_ahead(x, d) for x, d in zip(sums, group)]
 
@@ -391,7 +387,6 @@
         functools.partial(partner_grad_body, negatives=neg_par, peers=peers),
         [((width, anchor_rows), F32)],
         pairs * block,
-        info,
         positive_par,
         stats,
         other,
@@ -400,13 +395,12 @@
     )
     received = partner(sent)
 
-    (mine,) = call(key_body, [((rows, width), BF16)], 1 << 20, own_keys, *final, *returned, smem=0)
+    (mine,) = call(key_body, [((rows, width), BF16)], 1 << 20, own_keys, *final, *returned)
     step = sizes(anchor_rows, 256)
     grad_anchors, losses = call(
         functools.partial(anchor_body, negatives=neg_own, peers=peers),
         [((anchor_rows, width), F32), ((1, anchor_rows), F32)],
         pairs * block,
-        info,
         positive,
         stats,
         other,
@@ -424,7 +418,6 @@
         place_body,
         [((bank_rows, width), F32)],
         1 << 20,
-        info,
         *across(mine),
         scratch=[pltpu.VMEM((curve, rows, width), F32), pltpu.SemaphoreType.DMA((curve,))],
         placed=(0,),

time: 108 us -> 98.9 us (0.916)
  Pallas kernels: 40 us -> 25.1 us
  starting transfers between devices: 37.3 us -> 40.7 us
  local copies, waits for them, and re-layouts: 1.25 us -> 2.59 us
  waiting for transfers between devices: 28.2 us -> 29.3 us
    pallas_call x15, Pallas kernels: 40 us -> 25.1 us  [call(): pl.pallas_call(body, out_shape=[jax.ShapeDtypeStruct(s, d) for s, d in ou...]
    ppermute x12, waiting for transfers between devices: 4.8 us -> 7.88 us  [across(): lax.ppermute(x, 'curve', [(i, i ^ turn) for i in range(curve)])]
    ppermute x3, starting transfers between devices: 4.1 us -> 7 us  [to_ahead(): lax.ppermute(x, 'blk', [(i, (i + 2 * distance) % peers) for i in range(pe...]
    ppermute x3, waiting for transfers between devices: 4.87 us -> 2.52 us  [to_ahead(): lax.ppermute(x, 'blk', [(i, (i + 2 * distance) % peers) for i in range(pe...]
    unnamed x12 -> x14, local copies, waits for them, and re-layouts: 1.24 us -> 2.58 us
  transfers between devices with their start and end apart: 31 -> 31, of which waited for: 13 -> 13; matrix products, arithmetic and copies ran while one was open for 0% -> 0% of each run, Pallas kernels for 21% -> 12%
where the time goes in v1:
time: 98.9 us; the launch traced here: 98.8 us
  starting transfers between devices  40.7 us (41%)
  waiting for transfers between devices  29.3 us (30%)
  Pallas kernels  25.1 us (25%)
  local copies, waits for them, and re-layouts  2.59 us (3%)
  between operations  1.01 us (1%)
    pallas_call x15, Pallas kernels, call(): pl.pallas_call(body, out_shape=[jax.ShapeDtypeStruct(s, d) for s, d in ou...  25.1 us
    ppermute x12, starting transfers between devices, across(): lax.ppermute(x, 'curve', [(i, i ^ turn) for i in range(curve)])  16 us
    ppermute x9, waiting for transfers between devices, exchange(): moved.append(lax.ppermute(parts[turn], 'curve', route))  12.6 us
    ppermute x9, starting transfers between devices, exchange(): moved.append(lax.ppermute(parts[turn], 'curve', route))  10.7 us
    ppermute x12, waiting for transfers between devices, across(): lax.ppermute(x, 'curve', [(i, i ^ turn) for i in range(curve)])  7.88 us
    ppermute x3, starting transfers between devices, to_ahead(): lax.ppermute(x, 'blk', [(i, (i + 2 * distance) % peers) for i in range(pe...  7 us
    ppermute x3, starting transfers between devices, from_ahead(): lax.ppermute(x, 'blk', [((i + 2 * distance) % peers, i) for i in range(pe...  6.12 us
    ppermute x3, waiting for transfers between devices, from_ahead(): lax.ppermute(x, 'blk', [((i + 2 * distance) % peers, i) for i in range(pe...  3.95 us
  transfers between devices with their start and end apart: 31, of which 13 were waited for; matrix products, arithmetic and copies ran while one was open for 0% of the time, Pallas kernels for 12%

profile of v1, /device:TPU:0, one launch (start us, length us, event | category | flops | bytes accessed | tf_op | source)
XLA Modules:
  0.0 98.8 jit_solution(15994386134313833669)
XLA Ops:
  3.1 5.1 %collective-permute-start.10 = (bf16[128,512]{1,0:T(8,128)(2,1)S(1)}, bf16[128,512]{1,0:T(8,128)(2,1)S(1)}, u32[]{:S(2)}, u32[]{:S(2)}) collective-permute-start(bf16[128,512]{1,0:T(8,128)(2,1)S(1)} %shard_map.67), channel_id=1, source_target_pairs={{2,0},{3,1},{4,2},{5,3},{6,4},{7,5},{0,6},{1,7},{10,8},{11,9},{12,... | collective-permute-start | bytes 393224 | tf_op jit(solution)/shard_map/ppermute | solution.py:303
  9.2 2.9 %collective-permute-done.10.refs_0_ = bf16[128,512]{1,0:T(8,128)(2,1)S(1)} collective-permute-done((bf16[128,512]{1,0:T(8,128)(2,1)S(1)}, bf16[128,512]{1,0:T(8,128)(2,1)S(1)}, u32[]{:S(2)}, u32[]{:S(2)}) %collective-permute-start.10) | collective-permute-done | bytes 131104 | tf_op jit(solution)/shard_map/ppermute | solution.py:303
  14.9 1.5 %collective-permute-start.12 = (bf16[128,512]{1,0:T(8,128)(2,1)S(1)}, bf16[128,512]{1,0:T(8,128)(2,1)S(1)}, u32[]{:S(2)}, u32[]{:S(2)}) collective-permute-start(bf16[128,512]{1,0:T(8,128)(2,1)S(1)} %collective-permute-done.10.refs_0_), channel_id=1, source_target_pairs={{0,16},{8,24},{16,0},{24,8},{1,17},{9,25},{17,1},{25,9},{2,18},{10... | collective-permute-start | bytes 393224 | tf_op jit(solution)/shard_map/ppermute | solution.py:289
  16.4 2.4 %collective-permute-start.13 = (bf16[128,512]{1,0:T(8,128)(2,1)S(1)}, bf16[128,512]{1,0:T(8,128)(2,1)S(1)}, u32[]{:S(2)}, u32[]{:S(2)}) collective-permute-start(bf16[128,512]{1,0:T(8,128)(2,1)S(1)} %collective-permute-done.10.refs_0_), channel_id=1, source_target_pairs={{0,24},{8,16},{16,8},{24,0},{1,25},{9,17},{17,9},{25,1},{2,26},{10... | collective-permute-start | bytes 393224 | tf_op jit(solution)/shard_map/ppermute | solution.py:289
  19.9 1.5 %collective-permute-start.7 = (bf16[128,512]{1,0:T(8,128)(2,1)S(1)}, bf16[128,512]{1,0:T(8,128)(2,1)S(1)}, u32[]{:S(2)}, u32[]{:S(2)}) collective-permute-start(bf16[128,512]{1,0:T(8,128)(2,1)S(1)} %collective-permute-done.6.refs_0_), channel_id=1, source_target_pairs={{0,8},{8,0},{16,24},{24,16},{1,9},{9,1},{17,25},{25,17},{2,10},{10... | collective-permute-start | bytes 393224 | tf_op jit(solution)/shard_map/ppermute | solution.py:289
  21.3 1.5 %collective-permute-start.8 = (bf16[128,512]{1,0:T(8,128)(2,1)S(1)}, bf16[128,512]{1,0:T(8,128)(2,1)S(1)}, u32[]{:S(2)}, u32[]{:S(2)}) collective-permute-start(bf16[128,512]{1,0:T(8,128)(2,1)S(1)} %collective-permute-done.6.refs_0_), channel_id=1, source_target_pairs={{0,16},{8,24},{16,0},{24,8},{1,17},{9,25},{17,1},{25,9},{2,18},{10... | collective-permute-start | bytes 393224 | tf_op jit(solution)/shard_map/ppermute | solution.py:289
  23.4 1.8 %shard_map.69 = (f32[4,1024]{1,0:T(4,128)S(1)}, bf16[512,512]{1,0:T(8,128)(2,1)S(1)}, bf16[512,1024]{1,0:T(8,128)(2,1)S(1)}, bf16[512,1024]{1,0:T(8,128)(2,1)S(1)}) custom-call(bf16[512,512]{1,0:T(8,128)(2,1)S(1)} %copy-done.3, s32[1,1024]{1,0:T(1,128)S(1)} %bitcast.4, s32[1,1024]{1,0:T(1,128)S(1)} %collective-permute-done.4.refs_2_.refs_5_.p_ref.refs_1_, ...), custom_call_target="tpu_custom_call" | custom-call | flops 1073741824 | bytes 1048576 | tf_op jit(solution)/shard_map/pallas_call | solution.py:23
  25.2 1.6 %collective-permute-start.1 = (bf16[128,512]{1,0:T(8,128)(2,1)S(1)}, bf16[128,512]{1,0:T(8,128)(2,1)S(1)}, u32[]{:S(2)}, u32[]{:S(2)}) collective-permute-start(bf16[128,512]{1,0:T(8,128)(2,1)S(1)} %collective-permute-done.refs_0_), channel_id=1, source_target_pairs={{0,8},{8,0},{16,24},{24,16},{1,9},{9,1},{17,25},{25,17},{2,10},{10... | collective-permute-start | bytes 393224 | tf_op jit(solution)/shard_map/ppermute | solution.py:289
  26.7 1.5 %collective-permute-start.2 = (bf16[128,512]{1,0:T(8,128)(2,1)S(1)}, bf16[128,512]{1,0:T(8,128)(2,1)S(1)}, u32[]{:S(2)}, u32[]{:S(2)}) collective-permute-start(bf16[128,512]{1,0:T(8,128)(2,1)S(1)} %collective-permute-done.refs_0_), channel_id=1, source_target_pairs={{0,16},{8,24},{16,0},{24,8},{1,17},{9,25},{17,1},{25,9},{2,18},{10... | collective-permute-start | bytes 393224 | tf_op jit(solution)/shard_map/ppermute | solution.py:289
  28.7 1.9 %shard_map.70 = (f32[4,1024]{1,0:T(4,128)S(1)}, bf16[512,512]{1,0:T(8,128)(2,1)S(1)}, bf16[512,1024]{1,0:T(8,128)(2,1)S(1)}, bf16[512,1024]{1,0:T(8,128)(2,1)S(1)}) custom-call(bf16[128,512]{1,0:T(8,128)(2,1)S(1)} %collective-permute-done.10.refs_0_, bf16[128,512]{1,0:T(8,128)(2,1)S(1)} %collective-permute-done.11.refs_1_, ...), custom_call_target="tpu_custom_call" | custom-call | flops 1073741824 | bytes 1048576 | tf_op jit(solution)/shard_map/pallas_call | solution.py:23
  32.0 2.7 %collective-permute-done.2.refs_2_ = bf16[128,512]{1,0:T(8,128)(2,1)S(1)} collective-permute-done((bf16[128,512]{1,0:T(8,128)(2,1)S(1)}, bf16[128,512]{1,0:T(8,128)(2,1)S(1)}, u32[]{:S(2)}, u32[]{:S(2)}) %collective-permute-start.2) | collective-permute-done | bytes 131104 | tf_op jit(solution)/shard_map/ppermute | solution.py:289
  34.7 2.1 %shard_map.72 = (f32[4,1024]{1,0:T(4,128)S(1)}, bf16[512,512]{1,0:T(8,128)(2,1)S(1)}, bf16[512,1024]{1,0:T(8,128)(2,1)S(1)}, bf16[512,1024]{1,0:T(8,128)(2,1)S(1)}) custom-call(bf16[128,512]{1,0:T(8,128)(2,1)S(1)} %collective-permute-done.refs_0_, bf16[128,512]{1,0:T(8,128)(2,1)S(1)} %collective-permute-done.1.refs_1_, ...), custom_call_target="tpu_custom_call" | custom-call | flops 1073741824 | bytes 1048576 | tf_op jit(solution)/shard_map/pallas_call | solution.py:23
  38.1 3.8 %shard_map.73 = f32[512,1024]{1,0:T(8,128)} custom-call(s32[1,1024]{1,0:T(1,128)S(1)} %collective-permute-done.4.refs_2_.refs_5_.p_ref.refs_1_, f32[4,1024]{1,0:T(4,128)S(1)} %get-tuple-element.36.mine.refs_4_, f32[4,1024]{1,0:T(4,128)S(1)} %collective-permute-done.14.other.refs_5_, bf16[512,512]{1,0:T(8,128)(2,1)S(1)} %get-tuple-element.37.refs_0_, ...), custom_call_target="tpu_custom_call" | custom-call | flops 2147483648 | bytes 1048576 | tf_op jit(solution)/shard_map/pallas_call | solution.py:23
  44.0 1.5 %collective-permute-start.20 = (bf16[128,512]{1,0:T(8,128)(2,1)S(1)}, bf16[128,512]{1,0:T(8,128)(2,1)S(1)}, u32[]{:S(2)}, u32[]{:S(2)}) collective-permute-start(bf16[128,512]{1,0:T(8,128)(2,1)S(1)} %get-tuple-element.55), channel_id=1, source_target_pairs={{0,16},{8,24},{16,0},{24,8},{1,17},{9,25},{17,1},{25,9},{2,18},{10... | collective-permute-start | bytes 393224 | tf_op jit(solution)/shard_map/ppermute | solution.py:296
  45.5 2.5 %shard_map.78 = (f32[256,512]{1,0:T(8,128)S(1)}, bf16[256,512]{1,0:T(8,128)(2,1)S(1)}, bf16[256,512]{1,0:T(8,128)(2,1)S(1)}, bf16[256,512]{1,0:T(8,128)(2,1)S(1)}) custom-call(s32[1,1024]{1,0:T(1,128)S(1)} %bitcast.9, s32[1,1024]{1,0:T(1,128)S(1)} %collective-permute-done.4.refs_2_.refs_5_.p_ref.refs_1_, ...), custom_call_target="tpu_custom_call" | custom-call | flops 2147483648 | bytes 1048576 | tf_op jit(solution)/shard_map/pallas_call | solution.py:23
  50.1 1.5 %collective-permute-start.25 = (bf16[256,512]{1,0:T(8,128)(2,1)S(1)}, bf16[256,512]{1,0:T(8,128)(2,1)S(1)}, u32[]{:S(2)}, u32[]{:S(2)}) collective-permute-start(bf16[256,512]{1,0:T(8,128)(2,1)S(1)} %get-tuple-element.60), channel_id=1, source_target_pairs={{0,24},{8,16},{16,8},{24,0},{1,25},{9,17},{17,9},{25,1},{2,26},{10... | collective-permute-start | bytes 786440 | tf_op jit(solution)/shard_map/ppermute | solution.py:296
  54.4 10.2 %collective-permute-done.21.refs_3_ = bf16[128,512]{1,0:T(8,128)(2,1)S(1)} collective-permute-done((bf16[128,512]{1,0:T(8,128)(2,1)S(1)}, bf16[128,512]{1,0:T(8,128)(2,1)S(1)}, u32[]{:S(2)}, u32[]{:S(2)}) %collective-permute-start.21) | collective-permute-done | bytes 131104 | tf_op jit(solution)/shard_map/ppermute | solution.py:296
  64.6 1.5 %collective-permute-start.16 = (bf16[128,512]{1,0:T(8,128)(2,1)S(1)}, bf16[128,512]{1,0:T(8,128)(2,1)S(1)}, u32[]{:S(2)}, u32[]{:S(2)}) collective-permute-start(bf16[128,512]{1,0:T(8,128)(2,1)S(1)} %get-tuple-element.50), channel_id=1, source_target_pairs={{0,8},{8,0},{16,24},{24,16},{1,9},{9,1},{17,25},{25,17},{2,10},{10... | collective-permute-start | bytes 393224 | tf_op jit(solution)/shard_map/ppermute | solution.py:296
  68.7 1.8 %collective-permute-done.16.refs_1_ = bf16[128,512]{1,0:T(8,128)(2,1)S(1)} collective-permute-done((bf16[128,512]{1,0:T(8,128)(2,1)S(1)}, bf16[128,512]{1,0:T(8,128)(2,1)S(1)}, u32[]{:S(2)}, u32[]{:S(2)}) %collective-permute-start.16) | collective-permute-done | bytes 131104 | tf_op jit(solution)/shard_map/ppermute | solution.py:296
  70.5 2.5 %collective-permute-start.26 = (bf16[128,512]{1,0:T(8,128)(2,1)S(1)}, bf16[128,512]{1,0:T(8,128)(2,1)S(1)}, u32[]{:S(2)}, u32[]{:S(2)}) collective-permute-start(bf16[128,512]{1,0:T(8,128)(2,1)S(1)} %get-tuple-element.61), channel_id=1, source_target_pairs={{0,2},{1,3},{2,4},{3,5},{4,6},{5,7},{6,0},{7,1},{8,10},{9,11},{10,... | collective-permute-start | bytes 393224 | tf_op jit(solution)/shard_map/ppermute | solution.py:306
  73.7 4.1 %collective-permute-start.27 = (bf16[128,512]{1,0:T(8,128)(2,1)S(1)}, bf16[128,512]{1,0:T(8,128)(2,1)S(1)}, u32[]{:S(2)}, u32[]{:S(2)}) collective-permute-start(bf16[128,512]{1,0:T(8,128)(2,1)S(1)} %get-tuple-element.62), channel_id=1, source_target_pairs={{0,6},{1,7},{2,0},{3,1},{4,2},{5,3},{6,4},{7,5},{8,14},{9,15},{10,... | collective-permute-start | bytes 393224 | tf_op jit(solution)/shard_map/ppermute | solution.py:306
  77.8 1.8 %collective-permute-done.22.refs_4_ = bf16[128,512]{1,0:T(8,128)(2,1)S(1)} collective-permute-done((bf16[128,512]{1,0:T(8,128)(2,1)S(1)}, bf16[128,512]{1,0:T(8,128)(2,1)S(1)}, u32[]{:S(2)}, u32[]{:S(2)}) %collective-permute-start.22) | collective-permute-done | bytes 131104 | tf_op jit(solution)/shard_map/ppermute | solution.py:306
  87.0 2.3 %collective-permute-done.30.refs_3_ = bf16[128,512]{1,0:T(8,128)(2,1)S(1)} collective-permute-done((bf16[128,512]{1,0:T(8,128)(2,1)S(1)}, bf16[128,512]{1,0:T(8,128)(2,1)S(1)}, u32[]{:S(2)}, u32[]{:S(2)}) %collective-permute-start.30) | collective-permute-done | bytes 131104 | tf_op jit(solution)/shard_map/ppermute | solution.py:289
  91.6 7.0 %shard_map.74 = (f32[1024,512]{1,0:T(8,128)}, f32[1,1024]{1,0:T(1,128)}) custom-call(s32[1,1024]{1,0:T(1,128)S(1)} %bitcast.11, f32[4,1024]{1,0:T(4,128)S(1)} %get-tuple-element.36.mine.refs_4_, f32[4,1024]{1,0:T(4,128)S(1)} %collective-permute-done.14.other.refs_5_, bf16[1024,512]{1,0:T(8,128)(2,1)S(1)} %copy-done.1, f32[512,1024]{1,0:T(8,128)} %copy-done.4, ...), custom_call_target="tpu_custom_call" | custom-call | flops 2147483648 | bytes 1048576 | tf_op jit(solution)/shard_map/pallas_call | solution.py:23
  (71 shorter events, 30.8 us)
Async XLA Ops:
  2.4 20.5 %collective-permute-start.5 = (bf16[1024,512]{1,0:T(8,128)(2,1)S(1)}, bf16[1024,512]{1,0:T(8,128)(2,1)S(1)}, u32[]{:S(2)}, u32[]{:S(2)}) collective-permute-start(bf16[1024,512]{1,0:T(8,128)(2,1)S(1)} %shard_map.68.refs_3_.refs_6_.refs_2_), channel_id=1, source_target_pairs={{0,1},{1,0},{2,3},{3,2},{4,5},{5,4},{6,7},{7,6},{8,9},{9,8},{10,11... | collective-permute-start | bytes 3145736 | tf_op jit(solution)/shard_map/ppermute | solution.py:300
  3.1 9.0 %collective-permute-start.10 = (bf16[128,512]{1,0:T(8,128)(2,1)S(1)}, bf16[128,512]{1,0:T(8,128)(2,1)S(1)}, u32[]{:S(2)}, u32[]{:S(2)}) collective-permute-start(bf16[128,512]{1,0:T(8,128)(2,1)S(1)} %shard_map.67), channel_id=1, source_target_pairs={{2,0},{3,1},{4,2},{5,3},{6,4},{7,5},{0,6},{1,7},{10,8},{11,9},{12,... | collective-permute-start | bytes 393224 | tf_op jit(solution)/shard_map/ppermute | solution.py:303
  8.2 8.2 %collective-permute-start.6 = (bf16[128,512]{1,0:T(8,128)(2,1)S(1)}, bf16[128,512]{1,0:T(8,128)(2,1)S(1)}, u32[]{:S(2)}, u32[]{:S(2)}) collective-permute-start(bf16[128,512]{1,0:T(8,128)(2,1)S(1)} %shard_map.67), channel_id=1, source_target_pairs={{6,0},{7,1},{0,2},{1,3},{2,4},{3,5},{4,6},{5,7},{14,8},{15,9},{8,1... | collective-permute-start | bytes 393224 | tf_op jit(solution)/shard_map/ppermute | solution.py:303
  8.2 11.7 %collective-permute-start = (bf16[128,512]{1,0:T(8,128)(2,1)S(1)}, bf16[128,512]{1,0:T(8,128)(2,1)S(1)}, u32[]{:S(2)}, u32[]{:S(2)}) collective-permute-start(bf16[128,512]{1,0:T(8,128)(2,1)S(1)} %shard_map.67), channel_id=1, source_target_pairs={{4,0},{5,1},{6,2},{7,3},{0,4},{1,5},{2,6},{3,7},{12,8},{13,9},{14,... | collective-permute-start | bytes 393224 | tf_op jit(solution)/shard_map/ppermute | solution.py:303
  12.1 9.2 %collective-permute-start.11 = (bf16[128,512]{1,0:T(8,128)(2,1)S(1)}, bf16[128,512]{1,0:T(8,128)(2,1)S(1)}, u32[]{:S(2)}, u32[]{:S(2)}) collective-permute-start(bf16[128,512]{1,0:T(8,128)(2,1)S(1)} %collective-permute-done.10.refs_0_), channel_id=1, source_target_pairs={{0,8},{8,0},{16,24},{24,16},{1,9},{9,1},{17,25},{25,17},{2,10},{10... | collective-permute-start | bytes 393224 | tf_op jit(solution)/shard_map/ppermute | solution.py:289
  14.9 10.3 %collective-permute-start.12 = (bf16[128,512]{1,0:T(8,128)(2,1)S(1)}, bf16[128,512]{1,0:T(8,128)(2,1)S(1)}, u32[]{:S(2)}, u32[]{:S(2)}) collective-permute-start(bf16[128,512]{1,0:T(8,128)(2,1)S(1)} %collective-permute-done.10.refs_0_), channel_id=1, source_target_pairs={{0,16},{8,24},{16,0},{24,8},{1,17},{9,25},{17,1},{25,9},{2,18},{10... | collective-permute-start | bytes 393224 | tf_op jit(solution)/shard_map/ppermute | solution.py:289
  16.4 10.3 %collective-permute-start.13 = (bf16[128,512]{1,0:T(8,128)(2,1)S(1)}, bf16[128,512]{1,0:T(8,128)(2,1)S(1)}, u32[]{:S(2)}, u32[]{:S(2)}) collective-permute-start(bf16[128,512]{1,0:T(8,128)(2,1)S(1)} %collective-permute-done.10.refs_0_), channel_id=1, source_target_pairs={{0,24},{8,16},{16,8},{24,0},{1,25},{9,17},{17,9},{25,1},{2,26},{10... | collective-permute-start | bytes 393224 | tf_op jit(solution)/shard_map/ppermute | solution.py:289
  19.9 8.4 %collective-permute-start.7 = (bf16[128,512]{1,0:T(8,128)(2,1)S(1)}, bf16[128,512]{1,0:T(8,128)(2,1)S(1)}, u32[]{:S(2)}, u32[]{:S(2)}) collective-permute-start(bf16[128,512]{1,0:T(8,128)(2,1)S(1)} %collective-permute-done.6.refs_0_), channel_id=1, source_target_pairs={{0,8},{8,0},{16,24},{24,16},{1,9},{9,1},{17,25},{25,17},{2,10},{10... | collective-permute-start | bytes 393224 | tf_op jit(solution)/shard_map/ppermute | solution.py:289
  21.3 9.3 %collective-permute-start.8 = (bf16[128,512]{1,0:T(8,128)(2,1)S(1)}, bf16[128,512]{1,0:T(8,128)(2,1)S(1)}, u32[]{:S(2)}, u32[]{:S(2)}) collective-permute-start(bf16[128,512]{1,0:T(8,128)(2,1)S(1)} %collective-permute-done.6.refs_0_), channel_id=1, source_target_pairs={{0,16},{8,24},{16,0},{24,8},{1,17},{9,25},{17,1},{25,9},{2,18},{10... | collective-permute-start | bytes 393224 | tf_op jit(solution)/shard_map/ppermute | solution.py:289
  22.9 7.8 %collective-permute-start.9 = (bf16[128,512]{1,0:T(8,128)(2,1)S(1)}, bf16[128,512]{1,0:T(8,128)(2,1)S(1)}, u32[]{:S(2)}, u32[]{:S(2)}) collective-permute-start(bf16[128,512]{1,0:T(8,128)(2,1)S(1)} %collective-permute-done.6.refs_0_), channel_id=1, source_target_pairs={{0,24},{8,16},{16,8},{24,0},{1,25},{9,17},{17,9},{25,1},{2,26},{10... | collective-permute-start | bytes 393224 | tf_op jit(solution)/shard_map/ppermute | solution.py:289
  25.2 6.8 %collective-permute-start.1 = (bf16[128,512]{1,0:T(8,128)(2,1)S(1)}, bf16[128,512]{1,0:T(8,128)(2,1)S(1)}, u32[]{:S(2)}, u32[]{:S(2)}) collective-permute-start(bf16[128,512]{1,0:T(8,128)(2,1)S(1)} %collective-permute-done.refs_0_), channel_id=1, source_target_pairs={{0,8},{8,0},{16,24},{24,16},{1,9},{9,1},{17,25},{25,17},{2,10},{10... | collective-permute-start | bytes 393224 | tf_op jit(solution)/shard_map/ppermute | solution.py:289
  26.7 8.0 %collective-permute-start.2 = (bf16[128,512]{1,0:T(8,128)(2,1)S(1)}, bf16[128,512]{1,0:T(8,128)(2,1)S(1)}, u32[]{:S(2)}, u32[]{:S(2)}) collective-permute-start(bf16[128,512]{1,0:T(8,128)(2,1)S(1)} %collective-permute-done.refs_0_), channel_id=1, source_target_pairs={{0,16},{8,24},{16,0},{24,8},{1,17},{9,25},{17,1},{25,9},{2,18},{10... | collective-permute-start | bytes 393224 | tf_op jit(solution)/shard_map/ppermute | solution.py:289
  41.9 48.3 %collective-permute-start.15 = (f32[512,1024]{1,0:T(8,128)}, f32[512,1024]{1,0:T(8,128)S(1)}, u32[]{:S(2)}, u32[]{:S(2)}) collective-permute-start(f32[512,1024]{1,0:T(8,128)} %shard_map.73), channel_id=1, source_target_pairs={{0,1},{1,0},{2,3},{3,2},{4,5},{5,4},{6,7},{7,6},{8,9},{9,8},{10,11... | collective-permute-start | bytes 6291464 | tf_op jit(solution)/shard_map/ppermute | solution.py:300
  43.4 6.7 %collective-permute-start.19 = (bf16[128,512]{1,0:T(8,128)(2,1)S(1)}, bf16[128,512]{1,0:T(8,128)(2,1)S(1)}, u32[]{:S(2)}, u32[]{:S(2)}) collective-permute-start(bf16[128,512]{1,0:T(8,128)(2,1)S(1)} %get-tuple-element.54), channel_id=1, source_target_pairs={{0,8},{8,0},{16,24},{24,16},{1,9},{9,1},{17,25},{25,17},{2,10},{10... | collective-permute-start | bytes 393224 | tf_op jit(solution)/shard_map/ppermute | solution.py:296
  44.0 7.6 %collective-permute-start.20 = (bf16[128,512]{1,0:T(8,128)(2,1)S(1)}, bf16[128,512]{1,0:T(8,128)(2,1)S(1)}, u32[]{:S(2)}, u32[]{:S(2)}) collective-permute-start(bf16[128,512]{1,0:T(8,128)(2,1)S(1)} %get-tuple-element.55), channel_id=1, source_target_pairs={{0,16},{8,24},{16,0},{24,8},{1,17},{9,25},{17,1},{25,9},{2,18},{10... | collective-permute-start | bytes 393224 | tf_op jit(solution)/shard_map/ppermute | solution.py:296
  48.1 18.0 %collective-permute-start.23 = (bf16[256,512]{1,0:T(8,128)(2,1)S(1)}, bf16[256,512]{1,0:T(8,128)(2,1)S(1)}, u32[]{:S(2)}, u32[]{:S(2)}) collective-permute-start(bf16[256,512]{1,0:T(8,128)(2,1)S(1)} %get-tuple-element.58), channel_id=1, source_target_pairs={{0,8},{8,0},{16,24},{24,16},{1,9},{9,1},{17,25},{25,17},{2,10},{10... | collective-permute-start | bytes 786440 | tf_op jit(solution)/shard_map/ppermute | solution.py:296
  49.3 18.0 %collective-permute-start.24 = (bf16[256,512]{1,0:T(8,128)(2,1)S(1)}, bf16[256,512]{1,0:T(8,128)(2,1)S(1)}, u32[]{:S(2)}, u32[]{:S(2)}) collective-permute-start(bf16[256,512]{1,0:T(8,128)(2,1)S(1)} %get-tuple-element.59), channel_id=1, source_target_pairs={{0,16},{8,24},{16,0},{24,8},{1,17},{9,25},{17,1},{25,9},{2,18},{10... | collective-permute-start | bytes 786440 | tf_op jit(solution)/shard_map/ppermute | solution.py:296
  50.1 18.1 %collective-permute-start.25 = (bf16[256,512]{1,0:T(8,128)(2,1)S(1)}, bf16[256,512]{1,0:T(8,128)(2,1)S(1)}, u32[]{:S(2)}, u32[]{:S(2)}) collective-permute-start(bf16[256,512]{1,0:T(8,128)(2,1)S(1)} %get-tuple-element.60), channel_id=1, source_target_pairs={{0,24},{8,16},{16,8},{24,0},{1,25},{9,17},{17,9},{25,1},{2,26},{10... | collective-permute-start | bytes 786440 | tf_op jit(solution)/shard_map/ppermute | solution.py:296
  51.6 13.0 %collective-permute-start.21 = (bf16[128,512]{1,0:T(8,128)(2,1)S(1)}, bf16[128,512]{1,0:T(8,128)(2,1)S(1)}, u32[]{:S(2)}, u32[]{:S(2)}) collective-permute-start(bf16[128,512]{1,0:T(8,128)(2,1)S(1)} %get-tuple-element.56), channel_id=1, source_target_pairs={{0,24},{8,16},{16,8},{24,0},{1,25},{9,17},{17,9},{25,1},{2,26},{10... | collective-permute-start | bytes 393224 | tf_op jit(solution)/shard_map/ppermute | solution.py:296
  66.1 7.6 %collective-permute-start.17 = (bf16[128,512]{1,0:T(8,128)(2,1)S(1)}, bf16[128,512]{1,0:T(8,128)(2,1)S(1)}, u32[]{:S(2)}, u32[]{:S(2)}) collective-permute-start(bf16[128,512]{1,0:T(8,128)(2,1)S(1)} %get-tuple-element.51), channel_id=1, source_target_pairs={{0,16},{8,24},{16,0},{24,8},{1,17},{9,25},{17,1},{25,9},{2,18},{10... | collective-permute-start | bytes 393224 | tf_op jit(solution)/shard_map/ppermute | solution.py:296
  67.3 10.5 %collective-permute-start.18 = (bf16[128,512]{1,0:T(8,128)(2,1)S(1)}, bf16[128,512]{1,0:T(8,128)(2,1)S(1)}, u32[]{:S(2)}, u32[]{:S(2)}) collective-permute-start(bf16[128,512]{1,0:T(8,128)(2,1)S(1)} %get-tuple-element.52), channel_id=1, source_target_pairs={{0,24},{8,16},{16,8},{24,0},{1,25},{9,17},{17,9},{25,1},{2,26},{10... | collective-permute-start | bytes 393224 | tf_op jit(solution)/shard_map/ppermute | solution.py:296
  68.2 11.3 %collective-permute-start.22 = (bf16[128,512]{1,0:T(8,128)(2,1)S(1)}, bf16[128,512]{1,0:T(8,128)(2,1)S(1)}, u32[]{:S(2)}, u32[]{:S(2)}) collective-permute-start(bf16[128,512]{1,0:T(8,128)(2,1)S(1)} %shard_map.77), channel_id=1, source_target_pairs={{0,4},{1,5},{2,6},{3,7},{4,0},{5,1},{6,2},{7,3},{8,12},{9,13},{10,... | collective-permute-start | bytes 393224 | tf_op jit(solution)/shard_map/ppermute | solution.py:306
  70.5 9.1 %collective-permute-start.26 = (bf16[128,512]{1,0:T(8,128)(2,1)S(1)}, bf16[128,512]{1,0:T(8,128)(2,1)S(1)}, u32[]{:S(2)}, u32[]{:S(2)}) collective-permute-start(bf16[128,512]{1,0:T(8,128)(2,1)S(1)} %get-tuple-element.61), channel_id=1, source_target_pairs={{0,2},{1,3},{2,4},{3,5},{4,6},{5,7},{6,0},{7,1},{8,10},{9,11},{10,... | collective-permute-start | bytes 393224 | tf_op jit(solution)/shard_map/ppermute | solution.py:306
  73.7 6.6 %collective-permute-start.27 = (bf16[128,512]{1,0:T(8,128)(2,1)S(1)}, bf16[128,512]{1,0:T(8,128)(2,1)S(1)}, u32[]{:S(2)}, u32[]{:S(2)}) collective-permute-start(bf16[128,512]{1,0:T(8,128)(2,1)S(1)} %get-tuple-element.62), channel_id=1, source_target_pairs={{0,6},{1,7},{2,0},{3,1},{4,2},{5,3},{6,4},{7,5},{8,14},{9,15},{10,... | collective-permute-start | bytes 393224 | tf_op jit(solution)/shard_map/ppermute | solution.py:306
  (14 other events, 86.1 us)

commit v2 on v1

--- a/solution.py
+++ b/solution.py
@@ -157,7 +157,10 @@
     refs = list(refs[6:])
     e_own = {d: refs.pop(0) if own_neg[d] else None for d in distances}
     e_par = {d: refs.pop(0) if par_neg[d] else None for d in distances}
-    outs, grads = refs[:-1], refs[-1]
+    grads = refs.pop()
+    outs = [refs.pop(0) for _ in range(curve)]
+    w_own = {d: refs.pop(0) if own_neg[d] else None for d in distances}
+    w_par = {d: refs.pop(0) if par_neg[d] else None for d in distances}
     bank_rows = grads.shape[0]
     rows = bank_rows // curve
     anchors = q_own.shape[0]
@@ -166,54 +169,52 @@
         base = first_key(d, bank_rows, peers)
         grads[...] = jnp.zeros_like(grads)
 
-        def side(row, q_ref, p_ref, e_ref):
+        def side(row, q_ref, p_ref, e_ref, w_ref):
             def some(index):
                 at = span(index, step)
                 inverse, coef, _, _ = scalings(mine, other, row, at)
                 weights = weights_of(e_ref, at, bank_rows, p_ref[:, at] - base, inverse, coef)
+                if w_ref is not None:
+                    w_ref[:, at] = weights
                 grads[...] += nn_dot(weights, q_ref[at, :])
 
             loop(anchors // step, some)
 
-        side(0, q_own, p_own, e_own[d])
-        side(2, q_par, p_par, e_par[d])
+        side(0, q_own, p_own, e_own[d], w_own[d])
+        side(2, q_par, p_par, e_par[d], w_par[d])
         for turn in range(curve):
             cut = grads[span(lax.axis_index("curve") ^ turn, rows), :]
             outs[turn][number * rows : (number + 1) * rows, :] = cut.astype(outs[turn].dtype)
 
 
-def query_grad(banks, grown, p_ref, mine, other, at, peers, row):
-    bank_rows = banks[0].shape[1]
-    inverse, coef, _, _ = scalings(mine, other, row, at)
-    total = None
-    for d, bank in enumerate(banks):
-        place = p_ref[:, at] - first_key(d, bank_rows, peers)
-        part = nn_dot(bank[...], weights_of(grown[d], at, bank_rows, place, inverse, coef))
-        total = part if total is None else total + part
-    return total
-
-
-def partner_grad_body(p_ref, mine, other, *refs, negatives, peers):
+def query_grad_body(p_ref, mine, other, *refs, negatives, peers, row):
     refs = list(refs)
     banks = [refs.pop(0) for _ in negatives]
-    grown = [refs.pop(0) if negative else None for negative in negatives]
+    kept = [refs.pop(0) if negative else None for negative in negatives]
     out = refs.pop(0)
+    bank_rows = banks[0].shape[1]
     anchors = p_ref.shape[1]
     step = sizes(anchors, 256)
 
     def some(index):
         at = span(index, step)
-        out[:, at] = query_grad(banks, grown, p_ref, mine, other, at, peers, 2)
+        inverse, coef, _, _ = scalings(mine, other, row, at)
+        total = None
+        for d, bank in enumerate(banks):
+            if kept[d] is None:
+                place = p_ref[:, at] - first_key(d, bank_rows, peers)
+                weights = weights_of(None, at, bank_rows, place, inverse, coef)
+            else:
+                weights = kept[d][:, at]
+            part = nn_dot(bank[...], weights)
+            total = part if total is None else total + part
+        out[:, at] = total.astype(out.dtype)
 
     loop(anchors // step, some)
 
 
-def anchor_body(p_ref, mine, other, x_ref, received, *refs, negatives, peers):
-    refs = list(refs)
-    banks = [refs.pop(0) for _ in negatives]
-    grown = [refs.pop(0) if negative else None for negative in negatives]
-    out, loss, held, sems = refs
-    anchors = p_ref.shape[1]
+def anchor_body(mine, other, x_ref, left, right, out, loss, held, sems):
+    anchors = x_ref.shape[0]
     step = sizes(anchors, 256)
 
     def copy(index):
@@ -223,8 +224,7 @@
 
     def some(index):
         at = span(index, step)
-        grad = query_grad(banks, grown, p_ref, mine, other, at, peers, 0)
-        grad = (grad + received[:, at]).T * (1.0 / DIVISOR)
+        grad = (left[:, at] + right[:, at].astype(F32)).T * (1.0 / DIVISOR)
         unit_vec, length = unit(x_ref[at, :])
         along = jnp.sum(unit_vec * grad, axis=1, keepdims=True)
         held[at, :] = (grad - unit_vec * along) / length
@@ -350,6 +350,7 @@
     other = partner(stats)
 
     returned, final = [], []
+    own_kept, par_kept = {}, {}
     for group in grad_groups(pairs):
         parts = call(
             functools.partial(
@@ -361,7 +362,8 @@
                 par_neg=neg_par,
             ),
             [((len(group) * rows, width), F32)]
-            + [((len(group) * rows, width), BF16)] * (curve - 1),
+            + [((len(group) * rows, width), BF16)] * (curve - 1)
+            + [((bank_rows, anchor_rows), BF16)] * sum(neg_own[d] + neg_par[d] for d in group),
             2 * block * len(group),
             *shared,
             stats,
@@ -370,7 +372,10 @@
             *[par_grown[d] for d in group if neg_par[d]],
             scratch=[pltpu.VMEM((bank_rows, width), F32)],
         )
-        parts = exchange(parts)
+        weights = list(parts[curve:])
+        own_kept.update({d: weights.pop(0) for d in group if neg_own[d]})
+        par_kept.update({d: weights.pop(0) for d in group if neg_par[d]})
+        parts = exchange(parts[:curve])
         if group == (0,):
             final = parts
             continue
@@ -382,32 +387,33 @@
         )
         returned += [to_ahead(x, d) for x, d in zip(sums, group)]
 
-    own_banks = [banks[d] for d in range(pairs)]
-    (sent,) = call(
-        functools.partial(partner_grad_body, negatives=neg_par, peers=peers),
-        [((width, anchor_rows), F32)],
-        pairs * block,
-        positive_par,
-        stats,
-        other,
-        *own_banks,
-        *[par_grown[d] for d in range(pairs) if neg_par[d]],
-    )
+    def query_grad(dtype, row, p, kept, negatives):
+        return call(
+            functools.partial(query_grad_body, negatives=negatives, peers=peers, row=row),
+            [((width, anchor_rows), dtype)],
+            pairs * block,
+            p,
+            stats,
+            other,
+            *[banks[d] for d in range(pairs)],
+            *[kept[d] for d in range(pairs) if negatives[d]],
+        )[0]
+
+    sent = query_grad(F32, 2, positive_par, par_kept, neg_par)
     received = partner(sent)
+    own_part = query_grad(F32, 0, positive, own_kept, neg_own)
 
     (mine,) = call(key_body, [((rows, width), BF16)], 1 << 20, own_keys, *final, *returned)
     step = sizes(anchor_rows, 256)
     grad_anchors, losses = call(
-        functools.partial(anchor_body, negatives=neg_own, peers=peers),
+        anchor_body,
         [((anchor_rows, width), F32), ((1, anchor_rows), F32)],
-        pairs * block,
-        positive,
+        1 << 22,
         stats,
         other,
         anchors,
+        own_part,
         received,
-        *own_banks,
-        *[own_grown[d] for d in range(pairs) if neg_own[d]],
         scratch=[
             pltpu.VMEM((anchor_rows, width), F32),
             pltpu.SemaphoreType.DMA((anchor_rows // step,)),

time: 98.9 us -> 103 us (1.041)
  local copies, waits for them, and re-layouts: 2.59 us -> 6.15 us
  Pallas kernels: 25.1 us -> 28.6 us
  waiting for transfers between devices: 29.3 us -> 26.2 us
    ppermute x12, waiting for transfers between devices: 7.88 us -> 1.32 us  [across(): lax.ppermute(x, 'curve', [(i, i ^ turn) for i in range(curve)])]
    unnamed x14 -> x36, local copies, waits for them, and re-layouts: 2.58 us -> 6.14 us
    pallas_call x15 -> x16, Pallas kernels: 25.1 us -> 28.6 us  [call(): pl.pallas_call(body, out_shape=[jax.ShapeDtypeStruct(s, d) for s, d in ou...]
    ppermute x9, waiting for transfers between devices: 12.6 us -> 14.9 us  [exchange(): moved.append(lax.ppermute(parts[turn], 'curve', route))]
    ppermute x3, waiting for transfers between devices: 2.52 us -> 3.73 us  [to_ahead(): lax.ppermute(x, 'blk', [(i, (i + 2 * distance) % peers) for i in range(pe...]
  transfers between devices with their start and end apart: 31 -> 31, of which waited for: 13 -> 11; matrix products, arithmetic and copies ran while one was open for 0% -> 0% of each run, Pallas kernels for 12% -> 10%
where the time goes in v2:
time: 103 us; the launch traced here: 102 us
  starting transfers between devices  40.4 us (39%)
  Pallas kernels  28.6 us (28%)
  waiting for transfers between devices  26.2 us (25%)
  local copies, waits for them, and re-layouts  6.15 us (6%)
  between operations  1.05 us (1%)
    pallas_call x16, Pallas kernels, call(): pl.pallas_call(body, out_shape=[jax.ShapeDtypeStruct(s, d) for s, d in ou...  28.6 us
    ppermute x12, starting transfers between devices, across(): lax.ppermute(x, 'curve', [(i, i ^ turn) for i in range(curve)])  16 us
    ppermute x9, waiting for transfers between devices, exchange(): moved.append(lax.ppermute(parts[turn], 'curve', route))  14.9 us
    ppermute x9, starting transfers between devices, exchange(): moved.append(lax.ppermute(parts[turn], 'curve', route))  10.5 us
    ppermute x3, starting transfers between devices, to_ahead(): lax.ppermute(x, 'blk', [(i, (i + 2 * distance) % peers) for i in range(pe...  6.9 us
    unnamed x36, local copies, waits for them, and re-layouts  6.14 us
    ppermute x3, starting transfers between devices, from_ahead(): lax.ppermute(x, 'blk', [((i + 2 * distance) % peers, i) for i in range(pe...  6.13 us
    ppermute x3, waiting for transfers between devices, from_ahead(): lax.ppermute(x, 'blk', [((i + 2 * distance) % peers, i) for i in range(pe...  3.94 us
  transfers between devices with their start and end apart: 31, of which 11 were waited for; matrix products, arithmetic and copies ran while one was open for 0% of the time, Pallas kernels for 10%

profile of v2, /device:TPU:0, one launch (start us, length us, event | category | flops | bytes accessed | tf_op | source)
XLA Modules:
  0.0 102.4 jit_solution(6686326875446150259)
XLA Ops:
  3.1 5.1 %collective-permute-start.10 = (bf16[128,512]{1,0:T(8,128)(2,1)S(1)}, bf16[128,512]{1,0:T(8,128)(2,1)S(1)}, u32[]{:S(2)}, u32[]{:S(2)}) collective-permute-start(bf16[128,512]{1,0:T(8,128)(2,1)S(1)} %shard_map.67), channel_id=1, source_target_pairs={{2,0},{3,1},{4,2},{5,3},{6,4},{7,5},{0,6},{1,7},{10,8},{11,9},{12,... | collective-permute-start | bytes 393224 | tf_op jit(solution)/shard_map/ppermute | solution.py:303
  9.2 2.9 %collective-permute-done.10.refs_0_ = bf16[128,512]{1,0:T(8,128)(2,1)S(1)} collective-permute-done((bf16[128,512]{1,0:T(8,128)(2,1)S(1)}, bf16[128,512]{1,0:T(8,128)(2,1)S(1)}, u32[]{:S(2)}, u32[]{:S(2)}) %collective-permute-start.10) | collective-permute-done | bytes 131104 | tf_op jit(solution)/shard_map/ppermute | solution.py:303
  14.9 1.5 %collective-permute-start.12 = (bf16[128,512]{1,0:T(8,128)(2,1)S(1)}, bf16[128,512]{1,0:T(8,128)(2,1)S(1)}, u32[]{:S(2)}, u32[]{:S(2)}) collective-permute-start(bf16[128,512]{1,0:T(8,128)(2,1)S(1)} %collective-permute-done.10.refs_0_), channel_id=1, source_target_pairs={{0,16},{8,24},{16,0},{24,8},{1,17},{9,25},{17,1},{25,9},{2,18},{10... | collective-permute-start | bytes 393224 | tf_op jit(solution)/shard_map/ppermute | solution.py:289
  16.4 2.4 %collective-permute-start.13 = (bf16[128,512]{1,0:T(8,128)(2,1)S(1)}, bf16[128,512]{1,0:T(8,128)(2,1)S(1)}, u32[]{:S(2)}, u32[]{:S(2)}) collective-permute-start(bf16[128,512]{1,0:T(8,128)(2,1)S(1)} %collective-permute-done.10.refs_0_), channel_id=1, source_target_pairs={{0,24},{8,16},{16,8},{24,0},{1,25},{9,17},{17,9},{25,1},{2,26},{10... | collective-permute-start | bytes 393224 | tf_op jit(solution)/shard_map/ppermute | solution.py:289
  21.3 1.5 %collective-permute-start.8 = (bf16[128,512]{1,0:T(8,128)(2,1)S(1)}, bf16[128,512]{1,0:T(8,128)(2,1)S(1)}, u32[]{:S(2)}, u32[]{:S(2)}) collective-permute-start(bf16[128,512]{1,0:T(8,128)(2,1)S(1)} %collective-permute-done.6.refs_0_), channel_id=1, source_target_pairs={{0,16},{8,24},{16,0},{24,8},{1,17},{9,25},{17,1},{25,9},{2,18},{10... | collective-permute-start | bytes 393224 | tf_op jit(solution)/shard_map/ppermute | solution.py:289
  23.3 1.8 %shard_map.69 = (f32[4,1024]{1,0:T(4,128)S(1)}, bf16[512,512]{1,0:T(8,128)(2,1)S(1)}, bf16[512,1024]{1,0:T(8,128)(2,1)S(1)}, bf16[512,1024]{1,0:T(8,128)(2,1)S(1)}) custom-call(bf16[512,512]{1,0:T(8,128)(2,1)S(1)} %copy-done.5, s32[1,1024]{1,0:T(1,128)S(1)} %bitcast.4, s32[1,1024]{1,0:T(1,128)S(1)} %collective-permute-done.4.refs_2_.refs_5_.refs_1_.p_ref, ...), custom_call_target="tpu_custom_call" | custom-call | flops 1073741824 | bytes 1048576 | tf_op jit(solution)/shard_map/pallas_call | solution.py:23
  29.6 1.9 %shard_map.70 = (f32[4,1024]{1,0:T(4,128)S(1)}, bf16[512,512]{1,0:T(8,128)(2,1)S(1)}, bf16[512,1024]{1,0:T(8,128)(2,1)S(1)}, bf16[512,1024]{1,0:T(8,128)(2,1)S(1)}) custom-call(bf16[128,512]{1,0:T(8,128)(2,1)S(1)} %collective-permute-done.10.refs_0_, bf16[128,512]{1,0:T(8,128)(2,1)S(1)} %collective-permute-done.11.refs_1_, ...), custom_call_target="tpu_custom_call" | custom-call | flops 1073741824 | bytes 1048576 | tf_op jit(solution)/shard_map/pallas_call | solution.py:23
  35.0 2.0 %shard_map.72 = (f32[4,1024]{1,0:T(4,128)S(1)}, bf16[512,512]{1,0:T(8,128)(2,1)S(1)}, bf16[512,1024]{1,0:T(8,128)(2,1)S(1)}, bf16[512,1024]{1,0:T(8,128)(2,1)S(1)}) custom-call(bf16[128,512]{1,0:T(8,128)(2,1)S(1)} %collective-permute-done.refs_0_, bf16[128,512]{1,0:T(8,128)(2,1)S(1)} %collective-permute-done.1.refs_1_, ...), custom_call_target="tpu_custom_call" | custom-call | flops 1073741824 | bytes 1048576 | tf_op jit(solution)/shard_map/pallas_call | solution.py:23
  39.3 4.0 %shard_map.74 = (f32[256,512]{1,0:T(8,128)S(1)}, bf16[256,512]{1,0:T(8,128)(2,1)S(1)}, bf16[256,512]{1,0:T(8,128)(2,1)S(1)}, bf16[256,512]{1,0:T(8,128)(2,1)S(1)...) custom-call(s32[1,1024]{1,0:T(1,128)S(1)} %bitcast.8, ...), custom_call_target="tpu_custom_call" | custom-call | flops 2147483648 | bytes 1048576 | tf_op jit(solution)/shard_map/pallas_call | solution.py:23
  43.3 2.6 %shard_map.75 = (f32[128,512]{1,0:T(8,128)S(1)}, bf16[128,512]{1,0:T(8,128)(2,1)S(1)}, bf16[128,512]{1,0:T(8,128)(2,1)S(1)}, bf16[128,512]{1,0:T(8,128)(2,1)S(1)...) custom-call(s32[1,1024]{1,0:T(1,128)S(1)} %bitcast.9, ...), custom_call_target="tpu_custom_call" | custom-call | flops 1073741824 | bytes 1048576 | tf_op jit(solution)/shard_map/pallas_call | solution.py:23
  45.9 2.6 %shard_map.73 = (f32[128,512]{1,0:T(8,128)S(1)}, bf16[128,512]{1,0:T(8,128)(2,1)S(1)}, bf16[128,512]{1,0:T(8,128)(2,1)S(1)}, bf16[128,512]{1,0:T(8,128)(2,1)S(1)...) custom-call(s32[1,1024]{1,0:T(1,128)S(1)} %bitcast.10, ...), custom_call_target="tpu_custom_call" | custom-call | flops 1073741824 | bytes 1048576 | tf_op jit(solution)/shard_map/pallas_call | solution.py:23
  48.5 3.7 %shard_map.77 = f32[512,1024]{1,0:T(8,128)} custom-call(s32[1,1024]{1,0:T(1,128)S(1)} %collective-permute-done.4.refs_2_.refs_5_.refs_1_.p_ref, f32[4,1024]{1,0:T(4,128)S(1)} %get-tuple-element.42.refs_4_.mine, f32[4,1024]{1,0:T(4,128)S(1)} %collective-permute-done.14.refs_5_.other, bf16[512,512]{1,0:T(8,128)(2,1)S(1)} %get-tuple-element.43.refs_0_, ...), custom_call_target="tpu_custom_call" | custom-call | flops 2147483648 | bytes 1048576 | tf_op jit(solution)/shard_map/pallas_call | solution.py:23
  56.4 2.3 %collective-permute-done.19.refs_1_ = bf16[128,512]{1,0:T(8,128)(2,1)S(1)} collective-permute-done((bf16[128,512]{1,0:T(8,128)(2,1)S(1)}, bf16[128,512]{1,0:T(8,128)(2,1)S(1)}, u32[]{:S(2)}, u32[]{:S(2)}) %collective-permute-start.19) | collective-permute-done | bytes 131104 | tf_op jit(solution)/shard_map/ppermute | solution.py:296
  60.1 1.6 %collective-permute-start.21 = (bf16[128,512]{1,0:T(8,128)(2,1)S(1)}, bf16[128,512]{1,0:T(8,128)(2,1)S(1)}, u32[]{:S(2)}, u32[]{:S(2)}) collective-permute-start(bf16[128,512]{1,0:T(8,128)(2,1)S(1)} %get-tuple-element.68), channel_id=1, source_target_pairs={{0,24},{8,16},{16,8},{24,0},{1,25},{9,17},{17,9},{25,1},{2,26},{10... | collective-permute-start | bytes 393224 | tf_op jit(solution)/shard_map/ppermute | solution.py:296
  61.7 10.9 %collective-permute-done.21.refs_3_ = bf16[128,512]{1,0:T(8,128)(2,1)S(1)} collective-permute-done((bf16[128,512]{1,0:T(8,128)(2,1)S(1)}, bf16[128,512]{1,0:T(8,128)(2,1)S(1)}, u32[]{:S(2)}, u32[]{:S(2)}) %collective-permute-start.21) | collective-permute-done | bytes 131104 | tf_op jit(solution)/shard_map/ppermute | solution.py:296
  74.3 1.9 %collective-permute-start.18 = (bf16[128,512]{1,0:T(8,128)(2,1)S(1)}, bf16[128,512]{1,0:T(8,128)(2,1)S(1)}, u32[]{:S(2)}, u32[]{:S(2)}) collective-permute-start(bf16[128,512]{1,0:T(8,128)(2,1)S(1)} %get-tuple-element.64), channel_id=1, source_target_pairs={{0,24},{8,16},{16,8},{24,0},{1,25},{9,17},{17,9},{25,1},{2,26},{10... | collective-permute-start | bytes 393224 | tf_op jit(solution)/shard_map/ppermute | solution.py:296
  76.8 1.6 %collective-permute-done.16.refs_1_ = bf16[128,512]{1,0:T(8,128)(2,1)S(1)} collective-permute-done((bf16[128,512]{1,0:T(8,128)(2,1)S(1)}, bf16[128,512]{1,0:T(8,128)(2,1)S(1)}, u32[]{:S(2)}, u32[]{:S(2)}) %collective-permute-start.16) | collective-permute-done | bytes 131104 | tf_op jit(solution)/shard_map/ppermute | solution.py:296
  78.5 2.8 %collective-permute-start.26 = (bf16[128,512]{1,0:T(8,128)(2,1)S(1)}, bf16[128,512]{1,0:T(8,128)(2,1)S(1)}, u32[]{:S(2)}, u32[]{:S(2)}) collective-permute-start(bf16[128,512]{1,0:T(8,128)(2,1)S(1)} %get-tuple-element.73), channel_id=1, source_target_pairs={{0,2},{1,3},{2,4},{3,5},{4,6},{5,7},{6,0},{7,1},{8,10},{9,11},{10,... | collective-permute-start | bytes 393224 | tf_op jit(solution)/shard_map/ppermute | solution.py:306
  81.2 3.7 %collective-permute-start.27 = (bf16[128,512]{1,0:T(8,128)(2,1)S(1)}, bf16[128,512]{1,0:T(8,128)(2,1)S(1)}, u32[]{:S(2)}, u32[]{:S(2)}) collective-permute-start(bf16[128,512]{1,0:T(8,128)(2,1)S(1)} %get-tuple-element.74), channel_id=1, source_target_pairs={{0,6},{1,7},{2,0},{3,1},{4,2},{5,3},{6,4},{7,5},{8,14},{9,15},{10,... | collective-permute-start | bytes 393224 | tf_op jit(solution)/shard_map/ppermute | solution.py:306
  84.9 3.4 %collective-permute-done.22.refs_4_ = bf16[128,512]{1,0:T(8,128)(2,1)S(1)} collective-permute-done((bf16[128,512]{1,0:T(8,128)(2,1)S(1)}, bf16[128,512]{1,0:T(8,128)(2,1)S(1)}, u32[]{:S(2)}, u32[]{:S(2)}) %collective-permute-start.22) | collective-permute-done | bytes 131104 | tf_op jit(solution)/shard_map/ppermute | solution.py:306
  90.4 2.0 %collective-permute-start.30 = (bf16[128,512]{1,0:T(8,128)(2,1)S(1)}, bf16[128,512]{1,0:T(8,128)(2,1)S(1)}, u32[]{:S(2)}, u32[]{:S(2)}) collective-permute-start(bf16[128,512]{1,0:T(8,128)(2,1)S(1)} %shard_map.81.refs_0_), channel_id=1, source_target_pairs={{0,24},{8,16},{16,8},{24,0},{1,25},{9,17},{17,9},{25,1},{2,26},{10... | collective-permute-start | bytes 393224 | tf_op jit(solution)/shard_map/ppermute | solution.py:289
  92.5 3.7 %shard_map.76.left = f32[512,1024]{1,0:T(8,128)} custom-call(s32[1,1024]{1,0:T(1,128)S(1)} %bitcast.11, f32[4,1024]{1,0:T(4,128)S(1)} %get-tuple-element.42.refs_4_.mine, f32[4,1024]{1,0:T(4,128)S(1)} %collective-permute-done.14.refs_5_.other, bf16[512,512]{1,0:T(8,128)(2,1)S(1)} %copy-done.7, bf16[512,512]{1,0:T(8,128)(2,1)S(1)} %copy-done.9, ...), custom_call_target="tpu_custom_call" | custom-call | flops 2147483648 | bytes 1048576 | tf_op jit(solution)/shard_map/pallas_call | solution.py:23
  97.7 1.6 %copy-done.2 = f32[512,1024]{1,0:T(8,128)S(1)} copy-done((f32[512,1024]{1,0:T(8,128)S(1)}, f32[512,1024]{1,0:T(8,128)}, u32[]{:S(2)}) %copy-start.2) | copy-done | bytes 2097176
  99.3 3.0 %shard_map.78 = (f32[1024,512]{1,0:T(8,128)}, f32[1,1024]{1,0:T(1,128)}) custom-call(f32[4,1024]{1,0:T(4,128)S(1)} %get-tuple-element.42.refs_4_.mine, f32[4,1024]{1,0:T(4,128)S(1)} %collective-permute-done.14.refs_5_.other, bf16[1024,512]{1,0:T(8,128)(2,1)S(1)} %copy-done.1, f32[512,1024]{1,0:T(8,128)S(1)} %copy-done.2, ...), custom_call_target="tpu_custom_call" | custom-call | flops 4194304 | bytes 1048576 | tf_op jit(solution)/shard_map/pallas_call | solution.py:23
  (94 shorter events, 30.8 us)
Async XLA Ops:
  2.4 20.5 %collective-permute-start.5 = (bf16[1024,512]{1,0:T(8,128)(2,1)S(1)}, bf16[1024,512]{1,0:T(8,128)(2,1)S(1)}, u32[]{:S(2)}, u32[]{:S(2)}) collective-permute-start(bf16[1024,512]{1,0:T(8,128)(2,1)S(1)} %shard_map.68.refs_3_.refs_6_.refs_2_), channel_id=1, source_target_pairs={{0,1},{1,0},{2,3},{3,2},{4,5},{5,4},{6,7},{7,6},{8,9},{9,8},{10,11... | collective-permute-start | bytes 3145736 | tf_op jit(solution)/shard_map/ppermute | solution.py:300
  3.1 9.0 %collective-permute-start.10 = (bf16[128,512]{1,0:T(8,128)(2,1)S(1)}, bf16[128,512]{1,0:T(8,128)(2,1)S(1)}, u32[]{:S(2)}, u32[]{:S(2)}) collective-permute-start(bf16[128,512]{1,0:T(8,128)(2,1)S(1)} %shard_map.67), channel_id=1, source_target_pairs={{2,0},{3,1},{4,2},{5,3},{6,4},{7,5},{0,6},{1,7},{10,8},{11,9},{12,... | collective-permute-start | bytes 393224 | tf_op jit(solution)/shard_map/ppermute | solution.py:303
  8.2 8.2 %collective-permute-start.6 = (bf16[128,512]{1,0:T(8,128)(2,1)S(1)}, bf16[128,512]{1,0:T(8,128)(2,1)S(1)}, u32[]{:S(2)}, u32[]{:S(2)}) collective-permute-start(bf16[128,512]{1,0:T(8,128)(2,1)S(1)} %shard_map.67), channel_id=1, source_target_pairs={{6,0},{7,1},{0,2},{1,3},{2,4},{3,5},{4,6},{5,7},{14,8},{15,9},{8,1... | collective-permute-start | bytes 393224 | tf_op jit(solution)/shard_map/ppermute | solution.py:303
  8.2 11.7 %collective-permute-start = (bf16[128,512]{1,0:T(8,128)(2,1)S(1)}, bf16[128,512]{1,0:T(8,128)(2,1)S(1)}, u32[]{:S(2)}, u32[]{:S(2)}) collective-permute-start(bf16[128,512]{1,0:T(8,128)(2,1)S(1)} %shard_map.67), channel_id=1, source_target_pairs={{4,0},{5,1},{6,2},{7,3},{0,4},{1,5},{2,6},{3,7},{12,8},{13,9},{14,... | collective-permute-start | bytes 393224 | tf_op jit(solution)/shard_map/ppermute | solution.py:303
  12.1 9.2 %collective-permute-start.11 = (bf16[128,512]{1,0:T(8,128)(2,1)S(1)}, bf16[128,512]{1,0:T(8,128)(2,1)S(1)}, u32[]{:S(2)}, u32[]{:S(2)}) collective-permute-start(bf16[128,512]{1,0:T(8,128)(2,1)S(1)} %collective-permute-done.10.refs_0_), channel_id=1, source_target_pairs={{0,8},{8,0},{16,24},{24,16},{1,9},{9,1},{17,25},{25,17},{2,10},{10... | collective-permute-start | bytes 393224 | tf_op jit(solution)/shard_map/ppermute | solution.py:289
  14.9 11.3 %collective-permute-start.12 = (bf16[128,512]{1,0:T(8,128)(2,1)S(1)}, bf16[128,512]{1,0:T(8,128)(2,1)S(1)}, u32[]{:S(2)}, u32[]{:S(2)}) collective-permute-start(bf16[128,512]{1,0:T(8,128)(2,1)S(1)} %collective-permute-done.10.refs_0_), channel_id=1, source_target_pairs={{0,16},{8,24},{16,0},{24,8},{1,17},{9,25},{17,1},{25,9},{2,18},{10... | collective-permute-start | bytes 393224 | tf_op jit(solution)/shard_map/ppermute | solution.py:289
  16.4 11.2 %collective-permute-start.13 = (bf16[128,512]{1,0:T(8,128)(2,1)S(1)}, bf16[128,512]{1,0:T(8,128)(2,1)S(1)}, u32[]{:S(2)}, u32[]{:S(2)}) collective-permute-start(bf16[128,512]{1,0:T(8,128)(2,1)S(1)} %collective-permute-done.10.refs_0_), channel_id=1, source_target_pairs={{0,24},{8,16},{16,8},{24,0},{1,25},{9,17},{17,9},{25,1},{2,26},{10... | collective-permute-start | bytes 393224 | tf_op jit(solution)/shard_map/ppermute | solution.py:289
  19.8 9.3 %collective-permute-start.7 = (bf16[128,512]{1,0:T(8,128)(2,1)S(1)}, bf16[128,512]{1,0:T(8,128)(2,1)S(1)}, u32[]{:S(2)}, u32[]{:S(2)}) collective-permute-start(bf16[128,512]{1,0:T(8,128)(2,1)S(1)} %collective-permute-done.6.refs_0_), channel_id=1, source_target_pairs={{0,8},{8,0},{16,24},{24,16},{1,9},{9,1},{17,25},{25,17},{2,10},{10... | collective-permute-start | bytes 393224 | tf_op jit(solution)/shard_map/ppermute | solution.py:289
  21.3 11.2 %collective-permute-start.8 = (bf16[128,512]{1,0:T(8,128)(2,1)S(1)}, bf16[128,512]{1,0:T(8,128)(2,1)S(1)}, u32[]{:S(2)}, u32[]{:S(2)}) collective-permute-start(bf16[128,512]{1,0:T(8,128)(2,1)S(1)} %collective-permute-done.6.refs_0_), channel_id=1, source_target_pairs={{0,16},{8,24},{16,0},{24,8},{1,17},{9,25},{17,1},{25,9},{2,18},{10... | collective-permute-start | bytes 393224 | tf_op jit(solution)/shard_map/ppermute | solution.py:289
  22.9 9.6 %collective-permute-start.9 = (bf16[128,512]{1,0:T(8,128)(2,1)S(1)}, bf16[128,512]{1,0:T(8,128)(2,1)S(1)}, u32[]{:S(2)}, u32[]{:S(2)}) collective-permute-start(bf16[128,512]{1,0:T(8,128)(2,1)S(1)} %collective-permute-done.6.refs_0_), channel_id=1, source_target_pairs={{0,24},{8,16},{16,8},{24,0},{1,25},{9,17},{17,9},{25,1},{2,26},{10... | collective-permute-start | bytes 393224 | tf_op jit(solution)/shard_map/ppermute | solution.py:289
  26.1 7.7 %collective-permute-start.1 = (bf16[128,512]{1,0:T(8,128)(2,1)S(1)}, bf16[128,512]{1,0:T(8,128)(2,1)S(1)}, u32[]{:S(2)}, u32[]{:S(2)}) collective-permute-start(bf16[128,512]{1,0:T(8,128)(2,1)S(1)} %collective-permute-done.refs_0_), channel_id=1, source_target_pairs={{0,8},{8,0},{16,24},{24,16},{1,9},{9,1},{17,25},{25,17},{2,10},{10... | collective-permute-start | bytes 393224 | tf_op jit(solution)/shard_map/ppermute | solution.py:289
  52.2 45.2 %collective-permute-start.15 = (f32[512,1024]{1,0:T(8,128)}, f32[512,1024]{1,0:T(8,128)S(1)}, u32[]{:S(2)}, u32[]{:S(2)}) collective-permute-start(f32[512,1024]{1,0:T(8,128)} %shard_map.77), channel_id=1, source_target_pairs={{0,1},{1,0},{2,3},{3,2},{4,5},{5,4},{6,7},{7,6},{8,9},{9,8},{10,11... | collective-permute-start | bytes 6291464 | tf_op jit(solution)/shard_map/ppermute | solution.py:300
  52.4 6.4 %collective-permute-start.19 = (bf16[128,512]{1,0:T(8,128)(2,1)S(1)}, bf16[128,512]{1,0:T(8,128)(2,1)S(1)}, u32[]{:S(2)}, u32[]{:S(2)}) collective-permute-start(bf16[128,512]{1,0:T(8,128)(2,1)S(1)} %get-tuple-element.66), channel_id=1, source_target_pairs={{0,8},{8,0},{16,24},{24,16},{1,9},{9,1},{17,25},{25,17},{2,10},{10... | collective-permute-start | bytes 393224 | tf_op jit(solution)/shard_map/ppermute | solution.py:296
  52.9 7.2 %collective-permute-start.20 = (bf16[128,512]{1,0:T(8,128)(2,1)S(1)}, bf16[128,512]{1,0:T(8,128)(2,1)S(1)}, u32[]{:S(2)}, u32[]{:S(2)}) collective-permute-start(bf16[128,512]{1,0:T(8,128)(2,1)S(1)} %get-tuple-element.67), channel_id=1, source_target_pairs={{0,16},{8,24},{16,0},{24,8},{1,17},{9,25},{17,1},{25,9},{2,18},{10... | collective-permute-start | bytes 393224 | tf_op jit(solution)/shard_map/ppermute | solution.py:296
  54.3 19.3 %collective-permute-start.23 = (bf16[256,512]{1,0:T(8,128)(2,1)S(1)}, bf16[256,512]{1,0:T(8,128)(2,1)S(1)}, u32[]{:S(2)}, u32[]{:S(2)}) collective-permute-start(bf16[256,512]{1,0:T(8,128)(2,1)S(1)} %get-tuple-element.70), channel_id=1, source_target_pairs={{0,8},{8,0},{16,24},{24,16},{1,9},{9,1},{17,25},{25,17},{2,10},{10... | collective-permute-start | bytes 786440 | tf_op jit(solution)/shard_map/ppermute | solution.py:296
  55.4 18.9 %collective-permute-start.24 = (bf16[256,512]{1,0:T(8,128)(2,1)S(1)}, bf16[256,512]{1,0:T(8,128)(2,1)S(1)}, u32[]{:S(2)}, u32[]{:S(2)}) collective-permute-start(bf16[256,512]{1,0:T(8,128)(2,1)S(1)} %get-tuple-element.71), channel_id=1, source_target_pairs={{0,16},{8,24},{16,0},{24,8},{1,17},{9,25},{17,1},{25,9},{2,18},{10... | collective-permute-start | bytes 786440 | tf_op jit(solution)/shard_map/ppermute | solution.py:296
  58.8 17.5 %collective-permute-start.25 = (bf16[256,512]{1,0:T(8,128)(2,1)S(1)}, bf16[256,512]{1,0:T(8,128)(2,1)S(1)}, u32[]{:S(2)}, u32[]{:S(2)}) collective-permute-start(bf16[256,512]{1,0:T(8,128)(2,1)S(1)} %get-tuple-element.72), channel_id=1, source_target_pairs={{0,24},{8,16},{16,8},{24,0},{1,25},{9,17},{17,9},{25,1},{2,26},{10... | collective-permute-start | bytes 786440 | tf_op jit(solution)/shard_map/ppermute | solution.py:296
  60.1 12.5 %collective-permute-start.21 = (bf16[128,512]{1,0:T(8,128)(2,1)S(1)}, bf16[128,512]{1,0:T(8,128)(2,1)S(1)}, u32[]{:S(2)}, u32[]{:S(2)}) collective-permute-start(bf16[128,512]{1,0:T(8,128)(2,1)S(1)} %get-tuple-element.68), channel_id=1, source_target_pairs={{0,24},{8,16},{16,8},{24,0},{1,25},{9,17},{17,9},{25,1},{2,26},{10... | collective-permute-start | bytes 393224 | tf_op jit(solution)/shard_map/ppermute | solution.py:296
  73.7 7.6 %collective-permute-start.17 = (bf16[128,512]{1,0:T(8,128)(2,1)S(1)}, bf16[128,512]{1,0:T(8,128)(2,1)S(1)}, u32[]{:S(2)}, u32[]{:S(2)}) collective-permute-start(bf16[128,512]{1,0:T(8,128)(2,1)S(1)} %get-tuple-element.63), channel_id=1, source_target_pairs={{0,16},{8,24},{16,0},{24,8},{1,17},{9,25},{17,1},{25,9},{2,18},{10... | collective-permute-start | bytes 393224 | tf_op jit(solution)/shard_map/ppermute | solution.py:296
  74.3 10.6 %collective-permute-start.18 = (bf16[128,512]{1,0:T(8,128)(2,1)S(1)}, bf16[128,512]{1,0:T(8,128)(2,1)S(1)}, u32[]{:S(2)}, u32[]{:S(2)}) collective-permute-start(bf16[128,512]{1,0:T(8,128)(2,1)S(1)} %get-tuple-element.64), channel_id=1, source_target_pairs={{0,24},{8,16},{16,8},{24,0},{1,25},{9,17},{17,9},{25,1},{2,26},{10... | collective-permute-start | bytes 393224 | tf_op jit(solution)/shard_map/ppermute | solution.py:296
  76.3 12.1 %collective-permute-start.22 = (bf16[128,512]{1,0:T(8,128)(2,1)S(1)}, bf16[128,512]{1,0:T(8,128)(2,1)S(1)}, u32[]{:S(2)}, u32[]{:S(2)}) collective-permute-start(bf16[128,512]{1,0:T(8,128)(2,1)S(1)} %shard_map.79), channel_id=1, source_target_pairs={{0,4},{1,5},{2,6},{3,7},{4,0},{5,1},{6,2},{7,3},{8,12},{9,13},{10,... | collective-permute-start | bytes 393224 | tf_op jit(solution)/shard_map/ppermute | solution.py:306
  78.5 9.9 %collective-permute-start.26 = (bf16[128,512]{1,0:T(8,128)(2,1)S(1)}, bf16[128,512]{1,0:T(8,128)(2,1)S(1)}, u32[]{:S(2)}, u32[]{:S(2)}) collective-permute-start(bf16[128,512]{1,0:T(8,128)(2,1)S(1)} %get-tuple-element.73), channel_id=1, source_target_pairs={{0,2},{1,3},{2,4},{3,5},{4,6},{5,7},{6,0},{7,1},{8,10},{9,11},{10,... | collective-permute-start | bytes 393224 | tf_op jit(solution)/shard_map/ppermute | solution.py:306
  81.2 7.4 %collective-permute-start.27 = (bf16[128,512]{1,0:T(8,128)(2,1)S(1)}, bf16[128,512]{1,0:T(8,128)(2,1)S(1)}, u32[]{:S(2)}, u32[]{:S(2)}) collective-permute-start(bf16[128,512]{1,0:T(8,128)(2,1)S(1)} %get-tuple-element.74), channel_id=1, source_target_pairs={{0,6},{1,7},{2,0},{3,1},{4,2},{5,3},{6,4},{7,5},{8,14},{9,15},{10,... | collective-permute-start | bytes 393224 | tf_op jit(solution)/shard_map/ppermute | solution.py:306
  88.9 7.2 %collective-permute-start.28 = (bf16[128,512]{1,0:T(8,128)(2,1)S(1)}, bf16[128,512]{1,0:T(8,128)(2,1)S(1)}, u32[]{:S(2)}, u32[]{:S(2)}) collective-permute-start(bf16[128,512]{1,0:T(8,128)(2,1)S(1)} %shard_map.81.refs_0_), channel_id=1, source_target_pairs={{0,8},{8,0},{16,24},{24,16},{1,9},{9,1},{17,25},{25,17},{2,10},{10... | collective-permute-start | bytes 393224 | tf_op jit(solution)/shard_map/ppermute | solution.py:289
  (25 other events, 291.4 us)

commit v3 on v2

--- a/solution.py
+++ b/solution.py
@@ -1,4 +1,5 @@
 import functools
+import math
 
 import jax
 import jax.numpy as jnp
@@ -10,6 +11,7 @@
 STEPS = 4
 DIVISOR = 0.07
 TINY = 1e-06
+SLACK = 4
 LOG2E = 1.4426950408889634
 
 
@@ -20,13 +22,16 @@
 
 
 def call(body, outs, flops, *args, scratch=(), placed=()):
+    held = sum(math.prod(x.shape) * x.dtype.itemsize for x in args)
+    held += sum(math.prod(shape) * jnp.dtype(dtype).itemsize for shape, dtype in outs)
+    held += sum(math.prod(x.shape) * 4 for x in scratch if x.memory_space == pltpu.VMEM)
     return pl.pallas_call(
         body,
         out_shape=[jax.ShapeDtypeStruct(s, d) for s, d in outs],
         in_specs=[VMEM] * len(args),
         out_specs=[ANY if i in placed else VMEM for i in range(len(outs))],
         scratch_shapes=list(scratch),
-        compiler_params=pltpu.CompilerParams(vmem_limit_bytes=48 * 1024 * 1024),
+        compiler_params=pltpu.CompilerParams(vmem_limit_bytes=held + (SLACK << 20)),
         cost_estimate=pl.CostEstimate(flops=flops, transcendentals=0, bytes_accessed=1 << 20),
     )(*args)
 
@@ -73,21 +78,46 @@
     loop(rows // step, some)
 
 
+def cuts(bank_rows, curve):
+    parts = min(2, curve.bit_length() - 1)
+    size = bank_rows // parts
+    return [(bit, bit * size, size // 2) for bit in range(parts)]
+
+
+def own_cut(bit, start, rows):
+    return pl.ds(start + (lax.axis_index("curve") >> bit) % 2 * rows, rows)
+
+
+def other_cut(bit, start, rows):
+    return pl.ds(start + (1 - (lax.axis_index("curve") >> bit) % 2) * rows, rows)
+
+
+def pieces_body(keys_ref, piece_ref, near_ref, *, curve):
+    rows = piece_ref.shape[0]
+    at = span(lax.axis_index("curve"), rows)
+    piece_ref[...] = unit(keys_ref[at, :])[0].astype(BF16)
+    filled = 0
+    for bit, start, half in cuts(keys_ref.shape[0], curve):
+        part = unit(keys_ref[own_cut(bit, start, half), :])[0].astype(BF16)
+        near_ref[filled : filled + half, :] = part
+        filled += half
+
+
 def first_key(distance, bank_rows, peers):
     return (lax.axis_index("blk") + 2 * distance) % peers * bank_rows
 
 
-def scores_body(*refs, distance, peers, curve, own_neg, par_neg, raw):
-    pieces = 1 if raw else curve
+def scores_body(*refs, distance, bank_rows, peers, curve, own_neg, par_neg):
+    near = cuts(bank_rows, curve) if distance == 1 else None
+    pieces = 1 if distance == 0 else 1 + len(near) if near else curve
     key_refs, refs = refs[:pieces], list(refs[pieces:])
     p_own, p_par, q_own, q_par, before, stats, turned = refs[:7]
     bank, refs = refs[-1], refs[7:-1]
     e_own = refs.pop(0) if own_neg else None
     e_par = refs.pop(0) if par_neg else None
-    bank_rows = bank.shape[0]
     anchors = q_own.shape[0]
     step = sizes(anchors, 256)
-    if raw:
+    if distance == 0:
         part = sizes(bank_rows, 128)
 
         def some(index):
@@ -95,6 +125,12 @@
             bank[at, :] = unit(key_refs[0][at, :])[0].astype(BF16)
 
         loop(bank_rows // part, some)
+    elif near:
+        filled = 0
+        for part, key_ref in zip(near, key_refs[1:]):
+            bank[own_cut(*part), :] = key_refs[0][filled : filled + part[2], :]
+            bank[other_cut(*part), :] = key_ref[...]
+            filled += part[2]
     else:
         for turn, key_ref in enumerate(key_refs):
             bank[span(lax.axis_index("curve") ^ turn, key_ref.shape[0]), :] = key_ref[...]
@@ -158,9 +194,7 @@
     e_own = {d: refs.pop(0) if own_neg[d] else None for d in distances}
     e_par = {d: refs.pop(0) if par_neg[d] else None for d in distances}
     grads = refs.pop()
-    outs = [refs.pop(0) for _ in range(curve)]
-    w_own = {d: refs.pop(0) if own_neg[d] else None for d in distances}
-    w_par = {d: refs.pop(0) if par_neg[d] else None for d in distances}
+    outs = refs
     bank_rows = grads.shape[0]
     rows = bank_rows // curve
     anchors = q_own.shape[0]
@@ -169,19 +203,17 @@
         base = first_key(d, bank_rows, peers)
         grads[...] = jnp.zeros_like(grads)
 
-        def side(row, q_ref, p_ref, e_ref, w_ref):
+        def side(row, q_ref, p_ref, e_ref):
             def some(index):
                 at = span(index, step)
                 inverse, coef, _, _ = scalings(mine, other, row, at)
                 weights = weights_of(e_ref, at, bank_rows, p_ref[:, at] - base, inverse, coef)
-                if w_ref is not None:
-                    w_ref[:, at] = weights
                 grads[...] += nn_dot(weights, q_ref[at, :])
 
             loop(anchors // step, some)
 
-        side(0, q_own, p_own, e_own[d], w_own[d])
-        side(2, q_par, p_par, e_par[d], w_par[d])
+        side(0, q_own, p_own, e_own[d])
+        side(2, q_par, p_par, e_par[d])
         for turn in range(curve):
             cut = grads[span(lax.axis_index("curve") ^ turn, rows), :]
             outs[turn][number * rows : (number + 1) * rows, :] = cut.astype(outs[turn].dtype)
@@ -190,7 +222,7 @@
 def query_grad_body(p_ref, mine, other, *refs, negatives, peers, row):
     refs = list(refs)
     banks = [refs.pop(0) for _ in negatives]
-    kept = [refs.pop(0) if negative else None for negative in negatives]
+    grown = [refs.pop(0) if negative else None for negative in negatives]
     out = refs.pop(0)
     bank_rows = banks[0].shape[1]
     anchors = p_ref.shape[1]
@@ -201,12 +233,8 @@
         inverse, coef, _, _ = scalings(mine, other, row, at)
         total = None
         for d, bank in enumerate(banks):
-            if kept[d] is None:
-                place = p_ref[:, at] - first_key(d, bank_rows, peers)
-                weights = weights_of(None, at, bank_rows, place, inverse, coef)
-            else:
-                weights = kept[d][:, at]
-            part = nn_dot(bank[...], weights)
+            place = p_ref[:, at] - first_key(d, bank_rows, peers)
+            part = nn_dot(bank[...], weights_of(grown[d], at, bank_rows, place, inverse, coef))
             total = part if total is None else total + part
         out[:, at] = total.astype(out.dtype)
 
@@ -236,13 +264,14 @@
     loop(anchors // step, lambda index: copy(index).wait())
 
 
-def key_body(x_ref, *refs):
+def key_body(keys_ref, *refs):
     grads, out = refs[:-1], refs[-1]
+    x = keys_ref[span(lax.axis_index("curve"), out.shape[0]), :]
     total = grads[0][...].astype(F32)
     for part in grads[1:]:
         total = total + part[...].astype(F32)
     grad = total * (1.0 / DIVISOR)
-    unit_vec, length = unit(x_ref[...])
+    unit_vec, length = unit(x)
     along = jnp.sum(unit_vec * grad, axis=1, keepdims=True)
     out[...] = ((grad - unit_vec * along) / length).astype(out.dtype)
 
@@ -280,21 +309,17 @@
     peers = lax.axis_size("blk")
     pairs = peers // 2
     rows = bank_rows // curve
-    at_curve = lax.axis_index("curve")
     block = 2 * bank_rows * anchor_rows * width
 
+    def neighbour(x, turn):
+        return lax.ppermute(x, "curve", [(i, i ^ turn) for i in range(curve)])
+
+    def exchange(parts):
+        rest = [neighbour(parts[turn], turn) for turn in range(1, curve)]
+        return [parts[0], *rest]
+
     def across(x):
-        moved = [x]
-        for turn in range(1, curve):
-            moved.append(lax.ppermute(x, "curve", [(i, i ^ turn) for i in range(curve)]))
-        return moved
-
-    def exchange(parts):
-        moved = [parts[0]]
-        for turn in range(1, curve):
-            route = [(i, i ^ turn) for i in range(curve)]
-            moved.append(lax.ppermute(parts[turn], "curve", route))
-        return moved
+        return exchange([x] * curve)
 
     def partner(x):
         return lax.ppermute(x, "blk", [(i, i ^ 1) for i in range(peers)])
@@ -309,9 +334,14 @@
     neg_own = [2 * d % peers <= STEPS for d in range(pairs)]
     neg_par = [min((2 * d - 1) % peers, (2 * d + 1) % peers) <= STEPS for d in range(pairs)]
 
-    own_keys = lax.dynamic_slice_in_dim(keys, at_curve * rows, rows, 0)
-    (piece,) = call(normalize_body, [((rows, width), BF16)], 1 << 20, own_keys)
-    arrived = {d: from_ahead(piece, d) for d in far}
+    near = cuts(bank_rows, curve)
+    piece, near_piece = call(
+        functools.partial(pieces_body, curve=curve),
+        [((rows, width), BF16), ((bank_rows // 2, width), BF16)],
+        1 << 20,
+        keys,
+    )
+    arrived = {d: from_ahead(near_piece if d == 1 else piece, d) for d in far}
     (queries,) = call(normalize_body, [((anchor_rows, width), BF16)], 1 << 20, anchors)
     queries_par = partner(queries)
     positive = (owners[:, 0] * bank_rows + key_rows).reshape(1, anchor_rows)
@@ -321,7 +351,16 @@
     stats = jnp.zeros((4, anchor_rows), F32)
     banks, own_grown, par_grown = {}, {}, {}
     for d in [0] + far:
-        parts = [keys] if d == 0 else across(arrived[d])
+        if d == 0:
+            parts = [keys]
+        elif d == 1:
+            parts, filled = [arrived[d]], 0
+            for bit, _, half in near:
+                sent = arrived[d][filled : filled + half]
+                parts.append(neighbour(sent, 1 << bit))
+                filled += half
+        else:
+            parts = across(arrived[d])
         outs = [((4, anchor_rows), F32), ((width, bank_rows), BF16)]
         outs += [((bank_rows, anchor_rows), BF16)] * (neg_own[d] + neg_par[d])
         results = call(
@@ -332,7 +371,7 @@
                 curve=curve,
                 own_neg=neg_own[d],
                 par_neg=neg_par[d],
-                raw=d == 0,
+                bank_rows=bank_rows,
             ),
             outs,
             2 * block,
@@ -350,7 +389,6 @@
     other = partner(stats)
 
     returned, final = [], []
-    own_kept, par_kept = {}, {}
     for group in grad_groups(pairs):
         parts = call(
             functools.partial(
@@ -362,8 +400,7 @@
                 par_neg=neg_par,
             ),
             [((len(group) * rows, width), F32)]
-            + [((len(group) * rows, width), BF16)] * (curve - 1)
-            + [((bank_rows, anchor_rows), BF16)] * sum(neg_own[d] + neg_par[d] for d in group),
+            + [((len(group) * rows, width), BF16)] * (curve - 1),
             2 * block * len(group),
             *shared,
             stats,
@@ -372,10 +409,7 @@
             *[par_grown[d] for d in group if neg_par[d]],
             scratch=[pltpu.VMEM((bank_rows, width), F32)],
         )
-        weights = list(parts[curve:])
-        own_kept.update({d: weights.pop(0) for d in group if neg_own[d]})
-        par_kept.update({d: weights.pop(0) for d in group if neg_par[d]})
-        parts = exchange(parts[:curve])
+        parts = exchange(parts)
         if group == (0,):
             final = parts
             continue
@@ -387,7 +421,7 @@
         )
         returned += [to_ahead(x, d) for x, d in zip(sums, group)]
 
-    def query_grad(dtype, row, p, kept, negatives):
+    def query_grad(dtype, row, p, grown, negatives):
         return call(
             functools.partial(query_grad_body, negatives=negatives, peers=peers, row=row),
             [((width, anchor_rows), dtype)],
@@ -396,14 +430,14 @@
             stats,
             other,
             *[banks[d] for d in range(pairs)],
-            *[kept[d] for d in range(pairs) if negatives[d]],
+            *[grown[d] for d in range(pairs) if negatives[d]],
         )[0]
 
-    sent = query_grad(F32, 2, positive_par, par_kept, neg_par)
+    sent = query_grad(BF16, 2, positive_par, par_grown, neg_par)
     received = partner(sent)
-    own_part = query_grad(F32, 0, positive, own_kept, neg_own)
-
-    (mine,) = call(key_body, [((rows, width), BF16)], 1 << 20, own_keys, *final, *returned)
+    own_part = query_grad(F32, 0, positive, own_grown, neg_own)
+
+    (mine,) = call(key_body, [((rows, width), BF16)], 1 << 20, keys, *final, *returned)
     step = sizes(anchor_rows, 256)
     grad_anchors, losses = call(
         anchor_body,
@@ -432,7 +466,7 @@
 
 
 def far_order(pairs):
-    return sorted(range(1, pairs), key=lambda d: (min(d, pairs - d), d))
+    return sorted(range(1, pairs), key=lambda d: (d == 1, min(d, pairs - d), d))
 
 
 def grad_groups(pairs):

time: 103 us -> 92.8 us (0.901)
  waiting for transfers between devices: 26.2 us -> 33.1 us
  Pallas kernels: 28.6 us -> 22.3 us
  starting transfers between devices: 40.4 us -> 35 us
  local copies, waits for them, and re-layouts: 6.15 us -> 1.26 us
    pallas_call x16, Pallas kernels: 28.6 us -> 22.3 us  [call(): pl.pallas_call(body, out_shape=[jax.ShapeDtypeStruct(s, d) for s, d in ou...]
    ppermute x3, waiting for transfers between devices: 3.94 us -> 9.38 us  [from_ahead(): lax.ppermute(x, 'blk', [((i + 2 * distance) % peers, i) for i in range(pe...]
    unnamed x36 -> x10, local copies, waits for them, and re-layouts: 6.14 us -> 1.24 us
    ppermute x3, starting transfers between devices: 6.9 us -> 3.54 us  [to_ahead(): lax.ppermute(x, 'blk', [(i, (i + 2 * distance) % peers) for i in range(pe...]
    ppermute x21 -> x20, starting transfers between devices: 26.5 us -> 24.3 us  [neighbour(): return lax.ppermute(x, 'curve', [(i, i ^ turn) for i in range(curve)])]
    ppermute x3, waiting for transfers between devices: 3.73 us -> 5.22 us  [to_ahead(): lax.ppermute(x, 'blk', [(i, (i + 2 * distance) % peers) for i in range(pe...]
    ppermute x4, waiting for transfers between devices: 2.34 us -> 1.18 us  [partner(): return lax.ppermute(x, 'blk', [(i, i ^ 1) for i in range(peers)])]
    ppermute x21 -> x20, waiting for transfers between devices: 16.2 us -> 17.3 us  [neighbour(): return lax.ppermute(x, 'curve', [(i, i ^ turn) for i in range(curve)])]
  transfers between devices with their start and end apart: 31 -> 30, of which waited for: 11 -> 13; matrix products, arithmetic and copies ran while one was open for 0% -> 0% of each run, Pallas kernels for 10% -> 15%
where the time goes in v3:
time: 92.8 us; the launch traced here: 92.6 us
  starting transfers between devices  35 us (38%)
  waiting for transfers between devices  33.1 us (36%)
  Pallas kernels  22.3 us (24%)
  local copies, waits for them, and re-layouts  1.26 us (1%)
  between operations  1.05 us (1%)
    ppermute x20, starting transfers between devices, neighbour(): return lax.ppermute(x, 'curve', [(i, i ^ turn) for i in range(curve)])  24.3 us
    pallas_call x16, Pallas kernels, call(): pl.pallas_call(body, out_shape=[jax.ShapeDtypeStruct(s, d) for s, d in ou...  22.3 us
    ppermute x20, waiting for transfers between devices, neighbour(): return lax.ppermute(x, 'curve', [(i, i ^ turn) for i in range(curve)])  17.3 us
    ppermute x3, waiting for transfers between devices, from_ahead(): lax.ppermute(x, 'blk', [((i + 2 * distance) % peers, i) for i in range(pe...  9.38 us
    ppermute x3, starting transfers between devices, from_ahead(): lax.ppermute(x, 'blk', [((i + 2 * distance) % peers, i) for i in range(pe...  6.19 us
    ppermute x3, waiting for transfers between devices, to_ahead(): lax.ppermute(x, 'blk', [(i, (i + 2 * distance) % peers) for i in range(pe...  5.22 us
    ppermute x3, starting transfers between devices, to_ahead(): lax.ppermute(x, 'blk', [(i, (i + 2 * distance) % peers) for i in range(pe...  3.54 us
  transfers between devices with their start and end apart: 30, of which 13 were waited for; matrix products, arithmetic and copies ran while one was open for 0% of the time, Pallas kernels for 15%

profile of v3, /device:TPU:0, one launch (start us, length us, event | category | flops | bytes accessed | tf_op | source)
XLA Modules:
  0.0 92.6 jit_solution(8144353742479959748)
XLA Ops:
  3.1 5.1 %collective-permute-start = (bf16[256,512]{1,0:T(8,128)(2,1)S(1)}, bf16[256,512]{1,0:T(8,128)(2,1)S(1)}, u32[]{:S(2)}, u32[]{:S(2)}) collective-permute-start(bf16[256,512]{1,0:T(8,128)(2,1)S(1)} %get-tuple-element.35), channel_id=1, source_target_pairs={{2,0},{3,1},{4,2},{5,3},{6,4},{7,5},{0,6},{1,7},{10,8},{11,9},{12,... | collective-permute-start | bytes 786440 | tf_op jit(solution)/shard_map/ppermute | solution.py:328
  9.4 9.3 %collective-permute-done.9.refs_0_ = bf16[128,512]{1,0:T(8,128)(2,1)S(1)} collective-permute-done((bf16[128,512]{1,0:T(8,128)(2,1)S(1)}, bf16[128,512]{1,0:T(8,128)(2,1)S(1)}, u32[]{:S(2)}, u32[]{:S(2)}) %collective-permute-start.9) | collective-permute-done | bytes 131104 | tf_op jit(solution)/shard_map/ppermute | solution.py:328
  18.7 1.5 %collective-permute-start.10 = (bf16[128,512]{1,0:T(8,128)(2,1)S(1)}, bf16[128,512]{1,0:T(8,128)(2,1)S(1)}, u32[]{:S(2)}, u32[]{:S(2)}) collective-permute-start(bf16[128,512]{1,0:T(8,128)(2,1)S(1)} %collective-permute-done.9.refs_0_), channel_id=1, source_target_pairs={{0,8},{8,0},{16,24},{24,16},{1,9},{9,1},{17,25},{25,17},{2,10},{10... | collective-permute-start | bytes 393224 | tf_op jit(solution)/shard_map/ppermute | solution.py:315
  20.2 1.5 %collective-permute-start.11 = (bf16[128,512]{1,0:T(8,128)(2,1)S(1)}, bf16[128,512]{1,0:T(8,128)(2,1)S(1)}, u32[]{:S(2)}, u32[]{:S(2)}) collective-permute-start(bf16[128,512]{1,0:T(8,128)(2,1)S(1)} %collective-permute-done.9.refs_0_), channel_id=1, source_target_pairs={{0,16},{8,24},{16,0},{24,8},{1,17},{9,25},{17,1},{25,9},{2,18},{10... | collective-permute-start | bytes 393224 | tf_op jit(solution)/shard_map/ppermute | solution.py:315
  22.3 1.5 %collective-permute-start.6 = (bf16[128,512]{1,0:T(8,128)(2,1)S(1)}, bf16[128,512]{1,0:T(8,128)(2,1)S(1)}, u32[]{:S(2)}, u32[]{:S(2)}) collective-permute-start(bf16[128,512]{1,0:T(8,128)(2,1)S(1)} %collective-permute-done.5.refs_0_), channel_id=1, source_target_pairs={{0,8},{8,0},{16,24},{24,16},{1,9},{9,1},{17,25},{25,17},{2,10},{10... | collective-permute-start | bytes 393224 | tf_op jit(solution)/shard_map/ppermute | solution.py:315
  25.1 1.5 %collective-permute-start.7 = (bf16[128,512]{1,0:T(8,128)(2,1)S(1)}, bf16[128,512]{1,0:T(8,128)(2,1)S(1)}, u32[]{:S(2)}, u32[]{:S(2)}) collective-permute-start(bf16[128,512]{1,0:T(8,128)(2,1)S(1)} %collective-permute-done.5.refs_0_), channel_id=1, source_target_pairs={{0,16},{8,24},{16,0},{24,8},{1,17},{9,25},{17,1},{25,9},{2,18},{10... | collective-permute-start | bytes 393224 | tf_op jit(solution)/shard_map/ppermute | solution.py:315
  26.7 1.8 %shard_map.69 = (f32[4,1024]{1,0:T(4,128)S(1)}, bf16[512,512]{1,0:T(8,128)(2,1)S(1)}, bf16[512,1024]{1,0:T(8,128)(2,1)S(1)}, bf16[512,1024]{1,0:T(8,128)(2,1)S(1)}) custom-call(bf16[512,512]{1,0:T(8,128)(2,1)S(1)} %copy-done.2, s32[1,1024]{1,0:T(1,128)S(1)} %bitcast.4, s32[1,1024]{1,0:T(1,128)S(1)} %collective-permute-done.3.refs_2_.refs_5_.refs_4_.p_ref.refs_1_, ...), custom_call_target="tpu_custom_call" | custom-call | flops 1073741824 | bytes 1048576 | tf_op jit(solution)/shard_map/pallas_call | solution.py:28
  28.5 1.9 %collective-permute-start.1 = (bf16[128,512]{1,0:T(8,128)(2,1)S(1)}, bf16[128,512]{1,0:T(8,128)(2,1)S(1)}, u32[]{:S(2)}, u32[]{:S(2)}) collective-permute-start(bf16[128,512]{1,0:T(8,128)(2,1)S(1)} %get-tuple-element.68), channel_id=1, source_target_pairs={{0,8},{8,0},{16,24},{24,16},{1,9},{9,1},{17,25},{25,17},{2,10},{10... | collective-permute-start | bytes 393224 | tf_op jit(solution)/shard_map/ppermute | solution.py:315
  30.5 1.5 %collective-permute-start.2 = (bf16[128,512]{1,0:T(8,128)(2,1)S(1)}, bf16[128,512]{1,0:T(8,128)(2,1)S(1)}, u32[]{:S(2)}, u32[]{:S(2)}) collective-permute-start(bf16[128,512]{1,0:T(8,128)(2,1)S(1)} %get-tuple-element.67), channel_id=1, source_target_pairs={{0,16},{8,24},{16,0},{24,8},{1,17},{9,25},{17,1},{25,9},{2,18},{10... | collective-permute-start | bytes 393224 | tf_op jit(solution)/shard_map/ppermute | solution.py:315
  34.2 1.9 %shard_map.71 = (f32[4,1024]{1,0:T(4,128)S(1)}, bf16[512,512]{1,0:T(8,128)(2,1)S(1)}, bf16[512,1024]{1,0:T(8,128)(2,1)S(1)}, bf16[512,1024]{1,0:T(8,128)(2,1)S(1)}) custom-call(bf16[128,512]{1,0:T(8,128)(2,1)S(1)} %collective-permute-done.5.refs_0_, bf16[128,512]{1,0:T(8,128)(2,1)S(1)} %collective-permute-done.6.refs_1_, ...), custom_call_target="tpu_custom_call" | custom-call | flops 1073741824 | bytes 1048576 | tf_op jit(solution)/shard_map/pallas_call | solution.py:28
  36.1 2.0 %shard_map.72 = (f32[4,1024]{1,0:T(4,128)S(1)}, bf16[512,512]{1,0:T(8,128)(2,1)S(1)}, bf16[512,1024]{1,0:T(8,128)(2,1)S(1)}, bf16[512,1024]{1,0:T(8,128)(2,1)S(1)}) custom-call(bf16[256,512]{1,0:T(8,128)(2,1)S(1)} %collective-permute-done.refs_0_, bf16[128,512]{1,0:T(8,128)(2,1)S(1)} %collective-permute-done.1.refs_1_, ...), custom_call_target="tpu_custom_call" | custom-call | flops 1073741824 | bytes 1048576 | tf_op jit(solution)/shard_map/pallas_call | solution.py:28
  39.4 2.5 %shard_map.74 = bf16[512,1024]{1,0:T(8,128)(2,1)S(1)} custom-call(s32[1,1024]{1,0:T(1,128)S(1)} %collective-permute-done.3.refs_2_.refs_5_.refs_4_.p_ref.refs_1_, f32[4,1024]{1,0:T(4,128)S(1)} %get-tuple-element.40.mine.refs_4_, f32[4,1024]{1,0:T(4,128)S(1)} %collective-permute-done.13.other.refs_5_, bf16[512,512]{1,0:T(8,128)(2,1)S(1)} %get-tuple-element.41.refs_0_, ...), custom_call_target="tpu_custom_call" | custom-call | flops 2147483648 | bytes 1048576 | tf_op jit(solution)/shard_map/pallas_call | solution.py:28
  44.9 2.5 %shard_map.79 = (f32[256,512]{1,0:T(8,128)S(1)}, bf16[256,512]{1,0:T(8,128)(2,1)S(1)}, bf16[256,512]{1,0:T(8,128)(2,1)S(1)}, bf16[256,512]{1,0:T(8,128)(2,1)S(1)}) custom-call(s32[1,1024]{1,0:T(1,128)S(1)} %bitcast.9, s32[1,1024]{1,0:T(1,128)S(1)} %collective-permute-done.3.refs_2_.refs_5_.refs_4_.p_ref.refs_1_, ...), custom_call_target="tpu_custom_call" | custom-call | flops 2147483648 | bytes 1048576 | tf_op jit(solution)/shard_map/pallas_call | solution.py:28
  47.4 1.6 %collective-permute-start.22 = (bf16[256,512]{1,0:T(8,128)(2,1)S(1)}, bf16[256,512]{1,0:T(8,128)(2,1)S(1)}, u32[]{:S(2)}, u32[]{:S(2)}) collective-permute-start(bf16[256,512]{1,0:T(8,128)(2,1)S(1)} %get-tuple-element.62), channel_id=1, source_target_pairs={{0,8},{8,0},{16,24},{24,16},{1,9},{9,1},{17,25},{25,17},{2,10},{10... | collective-permute-start | bytes 786440 | tf_op jit(solution)/shard_map/ppermute | solution.py:315
  51.0 2.1 %collective-permute-start.20 = (bf16[128,512]{1,0:T(8,128)(2,1)S(1)}, bf16[128,512]{1,0:T(8,128)(2,1)S(1)}, u32[]{:S(2)}, u32[]{:S(2)}) collective-permute-start(bf16[128,512]{1,0:T(8,128)(2,1)S(1)} %get-tuple-element.60), channel_id=1, source_target_pairs={{0,24},{8,16},{16,8},{24,0},{1,25},{9,17},{17,9},{25,1},{2,26},{10... | collective-permute-start | bytes 393224 | tf_op jit(solution)/shard_map/ppermute | solution.py:315
  54.4 10.5 %collective-permute-done.20.refs_3_ = bf16[128,512]{1,0:T(8,128)(2,1)S(1)} collective-permute-done((bf16[128,512]{1,0:T(8,128)(2,1)S(1)}, bf16[128,512]{1,0:T(8,128)(2,1)S(1)}, u32[]{:S(2)}, u32[]{:S(2)}) %collective-permute-start.20) | collective-permute-done | bytes 131104 | tf_op jit(solution)/shard_map/ppermute | solution.py:315
  67.1 1.5 %collective-permute-start.17 = (bf16[128,512]{1,0:T(8,128)(2,1)S(1)}, bf16[128,512]{1,0:T(8,128)(2,1)S(1)}, u32[]{:S(2)}, u32[]{:S(2)}) collective-permute-start(bf16[128,512]{1,0:T(8,128)(2,1)S(1)} %get-tuple-element.56), channel_id=1, source_target_pairs={{0,24},{8,16},{16,8},{24,0},{1,25},{9,17},{17,9},{25,1},{2,26},{10... | collective-permute-start | bytes 393224 | tf_op jit(solution)/shard_map/ppermute | solution.py:315
  69.3 1.9 %collective-permute-done.15.refs_1_ = bf16[128,512]{1,0:T(8,128)(2,1)S(1)} collective-permute-done((bf16[128,512]{1,0:T(8,128)(2,1)S(1)}, bf16[128,512]{1,0:T(8,128)(2,1)S(1)}, u32[]{:S(2)}, u32[]{:S(2)}) %collective-permute-start.15) | collective-permute-done | bytes 131104 | tf_op jit(solution)/shard_map/ppermute | solution.py:315
  73.5 1.6 %collective-permute-start.26 = (bf16[128,512]{1,0:T(8,128)(2,1)S(1)}, bf16[128,512]{1,0:T(8,128)(2,1)S(1)}, u32[]{:S(2)}, u32[]{:S(2)}) collective-permute-start(bf16[128,512]{1,0:T(8,128)(2,1)S(1)} %get-tuple-element.66), channel_id=1, source_target_pairs={{0,6},{1,7},{2,0},{3,1},{4,2},{5,3},{6,4},{7,5},{8,14},{9,15},{10,... | collective-permute-start | bytes 393224 | tf_op jit(solution)/shard_map/ppermute | solution.py:331
  75.0 4.6 %collective-permute-done.21.refs_4_ = bf16[128,512]{1,0:T(8,128)(2,1)S(1)} collective-permute-done((bf16[128,512]{1,0:T(8,128)(2,1)S(1)}, bf16[128,512]{1,0:T(8,128)(2,1)S(1)}, u32[]{:S(2)}, u32[]{:S(2)}) %collective-permute-start.21) | collective-permute-done | bytes 131104 | tf_op jit(solution)/shard_map/ppermute | solution.py:331
  82.5 1.5 %collective-permute-start.29 = (bf16[128,512]{1,0:T(8,128)(2,1)S(1)}, bf16[128,512]{1,0:T(8,128)(2,1)S(1)}, u32[]{:S(2)}, u32[]{:S(2)}) collective-permute-start(bf16[128,512]{1,0:T(8,128)(2,1)S(1)} %shard_map.81.refs_0_), channel_id=1, source_target_pairs={{0,24},{8,16},{16,8},{24,0},{1,25},{9,17},{17,9},{25,1},{2,26},{10... | collective-permute-start | bytes 393224 | tf_op jit(solution)/shard_map/ppermute | solution.py:315
  84.1 2.5 %shard_map.73.left = f32[512,1024]{1,0:T(8,128)S(1)} custom-call(s32[1,1024]{1,0:T(1,128)S(1)} %bitcast.11, f32[4,1024]{1,0:T(4,128)S(1)} %get-tuple-element.40.mine.refs_4_, f32[4,1024]{1,0:T(4,128)S(1)} %collective-permute-done.13.other.refs_5_, bf16[512,512]{1,0:T(8,128)(2,1)S(1)} %get-tuple-element.41.refs_0_, ...), custom_call_target="tpu_custom_call" | custom-call | flops 2147483648 | bytes 1048576 | tf_op jit(solution)/shard_map/pallas_call | solution.py:28
  86.7 1.8 %collective-permute-done.29.refs_3_ = bf16[128,512]{1,0:T(8,128)(2,1)S(1)} collective-permute-done((bf16[128,512]{1,0:T(8,128)(2,1)S(1)}, bf16[128,512]{1,0:T(8,128)(2,1)S(1)}, u32[]{:S(2)}, u32[]{:S(2)}) %collective-permute-start.29) | collective-permute-done | bytes 131104 | tf_op jit(solution)/shard_map/ppermute | solution.py:315
  89.4 3.0 %shard_map.75 = (f32[1024,512]{1,0:T(8,128)}, f32[1,1024]{1,0:T(1,128)}) custom-call(f32[4,1024]{1,0:T(4,128)S(1)} %get-tuple-element.40.mine.refs_4_, f32[4,1024]{1,0:T(4,128)S(1)} %collective-permute-done.13.other.refs_5_, bf16[1024,512]{1,0:T(8,128)(2,1)S(1)} %copy-done.1, f32[512,1024]{1,0:T(8,128)S(1)} %shard_map.73.left, ...), custom_call_target="tpu_custom_call" | custom-call | flops 4194304 | bytes 1048576 | tf_op jit(solution)/shard_map/pallas_call | solution.py:28
  (66 shorter events, 24.4 us)
Async XLA Ops:
  2.4 24.3 %collective-permute-start.4 = (bf16[1024,512]{1,0:T(8,128)(2,1)S(1)}, bf16[1024,512]{1,0:T(8,128)(2,1)S(1)}, u32[]{:S(2)}, u32[]{:S(2)}) collective-permute-start(bf16[1024,512]{1,0:T(8,128)(2,1)S(1)} %shard_map.68.refs_3_.refs_6_.refs_5_.refs_2_), channel_id=1, source_target_pairs={{0,1},{1,0},{2,3},{3,2},{4,5},{5,4},{6,7},{7,6},{8,9},{9,8},{10,11... | collective-permute-start | bytes 3145736 | tf_op jit(solution)/shard_map/ppermute | solution.py:325
  3.1 18.6 %collective-permute-start = (bf16[256,512]{1,0:T(8,128)(2,1)S(1)}, bf16[256,512]{1,0:T(8,128)(2,1)S(1)}, u32[]{:S(2)}, u32[]{:S(2)}) collective-permute-start(bf16[256,512]{1,0:T(8,128)(2,1)S(1)} %get-tuple-element.35), channel_id=1, source_target_pairs={{2,0},{3,1},{4,2},{5,3},{6,4},{7,5},{0,6},{1,7},{10,8},{11,9},{12,... | collective-permute-start | bytes 786440 | tf_op jit(solution)/shard_map/ppermute | solution.py:328
  8.2 10.5 %collective-permute-start.9 = (bf16[128,512]{1,0:T(8,128)(2,1)S(1)}, bf16[128,512]{1,0:T(8,128)(2,1)S(1)}, u32[]{:S(2)}, u32[]{:S(2)}) collective-permute-start(bf16[128,512]{1,0:T(8,128)(2,1)S(1)} %get-tuple-element.36), channel_id=1, source_target_pairs={{6,0},{7,1},{0,2},{1,3},{2,4},{3,5},{4,6},{5,7},{14,8},{15,9},{8,1... | collective-permute-start | bytes 393224 | tf_op jit(solution)/shard_map/ppermute | solution.py:328
  8.3 12.0 %collective-permute-start.3 = (s32[1,1024]{1,0:T(1,128)S(1)}, s32[1,1024]{1,0:T(1,128)S(1)}, u32[]{:S(2)}, u32[]{:S(2)}) collective-permute-start(s32[1,1024]{1,0:T(1,128)S(1)} %bitcast.3), channel_id=1, source_target_pairs={{0,1},{1,0},{2,3},{3,2},{4,5},{5,4},{6,7},{7,6},{8,9},{9,8},{10,11... | collective-permute-start | bytes 12296 | tf_op jit(solution)/shard_map/ppermute | solution.py:325
  8.3 14.0 %collective-permute-start.5 = (bf16[128,512]{1,0:T(8,128)(2,1)S(1)}, bf16[128,512]{1,0:T(8,128)(2,1)S(1)}, u32[]{:S(2)}, u32[]{:S(2)}) collective-permute-start(bf16[128,512]{1,0:T(8,128)(2,1)S(1)} %get-tuple-element.36), channel_id=1, source_target_pairs={{4,0},{5,1},{6,2},{7,3},{0,4},{1,5},{2,6},{3,7},{12,8},{13,9},{14,... | collective-permute-start | bytes 393224 | tf_op jit(solution)/shard_map/ppermute | solution.py:328
  18.7 6.4 %collective-permute-start.10 = (bf16[128,512]{1,0:T(8,128)(2,1)S(1)}, bf16[128,512]{1,0:T(8,128)(2,1)S(1)}, u32[]{:S(2)}, u32[]{:S(2)}) collective-permute-start(bf16[128,512]{1,0:T(8,128)(2,1)S(1)} %collective-permute-done.9.refs_0_), channel_id=1, source_target_pairs={{0,8},{8,0},{16,24},{24,16},{1,9},{9,1},{17,25},{25,17},{2,10},{10... | collective-permute-start | bytes 393224 | tf_op jit(solution)/shard_map/ppermute | solution.py:315
  20.2 8.3 %collective-permute-start.11 = (bf16[128,512]{1,0:T(8,128)(2,1)S(1)}, bf16[128,512]{1,0:T(8,128)(2,1)S(1)}, u32[]{:S(2)}, u32[]{:S(2)}) collective-permute-start(bf16[128,512]{1,0:T(8,128)(2,1)S(1)} %collective-permute-done.9.refs_0_), channel_id=1, source_target_pairs={{0,16},{8,24},{16,0},{24,8},{1,17},{9,25},{17,1},{25,9},{2,18},{10... | collective-permute-start | bytes 393224 | tf_op jit(solution)/shard_map/ppermute | solution.py:315
  21.8 8.7 %collective-permute-start.12 = (bf16[128,512]{1,0:T(8,128)(2,1)S(1)}, bf16[128,512]{1,0:T(8,128)(2,1)S(1)}, u32[]{:S(2)}, u32[]{:S(2)}) collective-permute-start(bf16[128,512]{1,0:T(8,128)(2,1)S(1)} %collective-permute-done.9.refs_0_), channel_id=1, source_target_pairs={{0,24},{8,16},{16,8},{24,0},{1,25},{9,17},{17,9},{25,1},{2,26},{10... | collective-permute-start | bytes 393224 | tf_op jit(solution)/shard_map/ppermute | solution.py:315
  22.3 11.0 %collective-permute-start.6 = (bf16[128,512]{1,0:T(8,128)(2,1)S(1)}, bf16[128,512]{1,0:T(8,128)(2,1)S(1)}, u32[]{:S(2)}, u32[]{:S(2)}) collective-permute-start(bf16[128,512]{1,0:T(8,128)(2,1)S(1)} %collective-permute-done.5.refs_0_), channel_id=1, source_target_pairs={{0,8},{8,0},{16,24},{24,16},{1,9},{9,1},{17,25},{25,17},{2,10},{10... | collective-permute-start | bytes 393224 | tf_op jit(solution)/shard_map/ppermute | solution.py:315
  25.1 8.4 %collective-permute-start.7 = (bf16[128,512]{1,0:T(8,128)(2,1)S(1)}, bf16[128,512]{1,0:T(8,128)(2,1)S(1)}, u32[]{:S(2)}, u32[]{:S(2)}) collective-permute-start(bf16[128,512]{1,0:T(8,128)(2,1)S(1)} %collective-permute-done.5.refs_0_), channel_id=1, source_target_pairs={{0,16},{8,24},{16,0},{24,8},{1,17},{9,25},{17,1},{25,9},{2,18},{10... | collective-permute-start | bytes 393224 | tf_op jit(solution)/shard_map/ppermute | solution.py:315
  26.6 7.6 %collective-permute-start.8 = (bf16[128,512]{1,0:T(8,128)(2,1)S(1)}, bf16[128,512]{1,0:T(8,128)(2,1)S(1)}, u32[]{:S(2)}, u32[]{:S(2)}) collective-permute-start(bf16[128,512]{1,0:T(8,128)(2,1)S(1)} %collective-permute-done.5.refs_0_), channel_id=1, source_target_pairs={{0,24},{8,16},{16,8},{24,0},{1,25},{9,17},{17,9},{25,1},{2,26},{10... | collective-permute-start | bytes 393224 | tf_op jit(solution)/shard_map/ppermute | solution.py:315
  28.5 7.5 %collective-permute-start.1 = (bf16[128,512]{1,0:T(8,128)(2,1)S(1)}, bf16[128,512]{1,0:T(8,128)(2,1)S(1)}, u32[]{:S(2)}, u32[]{:S(2)}) collective-permute-start(bf16[128,512]{1,0:T(8,128)(2,1)S(1)} %get-tuple-element.68), channel_id=1, source_target_pairs={{0,8},{8,0},{16,24},{24,16},{1,9},{9,1},{17,25},{25,17},{2,10},{10... | collective-permute-start | bytes 393224 | tf_op jit(solution)/shard_map/ppermute | solution.py:315
  41.9 47.5 %collective-permute-start.14 = (bf16[512,1024]{1,0:T(8,128)(2,1)S(1)}, bf16[512,1024]{1,0:T(8,128)(2,1)S(1)}, u32[]{:S(2)}, u32[]{:S(2)}) collective-permute-start(bf16[512,1024]{1,0:T(8,128)(2,1)S(1)} %shard_map.74), channel_id=1, source_target_pairs={{0,1},{1,0},{2,3},{3,2},{4,5},{5,4},{6,7},{7,6},{8,9},{9,8},{10,11... | collective-permute-start | bytes 3145736 | tf_op jit(solution)/shard_map/ppermute | solution.py:325
  43.5 6.7 %collective-permute-start.18 = (bf16[128,512]{1,0:T(8,128)(2,1)S(1)}, bf16[128,512]{1,0:T(8,128)(2,1)S(1)}, u32[]{:S(2)}, u32[]{:S(2)}) collective-permute-start(bf16[128,512]{1,0:T(8,128)(2,1)S(1)} %get-tuple-element.58), channel_id=1, source_target_pairs={{0,8},{8,0},{16,24},{24,16},{1,9},{9,1},{17,25},{25,17},{2,10},{10... | collective-permute-start | bytes 393224 | tf_op jit(solution)/shard_map/ppermute | solution.py:315
  44.4 6.6 %collective-permute-start.19 = (bf16[128,512]{1,0:T(8,128)(2,1)S(1)}, bf16[128,512]{1,0:T(8,128)(2,1)S(1)}, u32[]{:S(2)}, u32[]{:S(2)}) collective-permute-start(bf16[128,512]{1,0:T(8,128)(2,1)S(1)} %get-tuple-element.59), channel_id=1, source_target_pairs={{0,16},{8,24},{16,0},{24,8},{1,17},{9,25},{17,1},{25,9},{2,18},{10... | collective-permute-start | bytes 393224 | tf_op jit(solution)/shard_map/ppermute | solution.py:315
  47.4 18.6 %collective-permute-start.22 = (bf16[256,512]{1,0:T(8,128)(2,1)S(1)}, bf16[256,512]{1,0:T(8,128)(2,1)S(1)}, u32[]{:S(2)}, u32[]{:S(2)}) collective-permute-start(bf16[256,512]{1,0:T(8,128)(2,1)S(1)} %get-tuple-element.62), channel_id=1, source_target_pairs={{0,8},{8,0},{16,24},{24,16},{1,9},{9,1},{17,25},{25,17},{2,10},{10... | collective-permute-start | bytes 786440 | tf_op jit(solution)/shard_map/ppermute | solution.py:315
  49.0 18.0 %collective-permute-start.23 = (bf16[256,512]{1,0:T(8,128)(2,1)S(1)}, bf16[256,512]{1,0:T(8,128)(2,1)S(1)}, u32[]{:S(2)}, u32[]{:S(2)}) collective-permute-start(bf16[256,512]{1,0:T(8,128)(2,1)S(1)} %get-tuple-element.63), channel_id=1, source_target_pairs={{0,16},{8,24},{16,0},{24,8},{1,17},{9,25},{17,1},{25,9},{2,18},{10... | collective-permute-start | bytes 786440 | tf_op jit(solution)/shard_map/ppermute | solution.py:315
  50.2 18.4 %collective-permute-start.24 = (bf16[256,512]{1,0:T(8,128)(2,1)S(1)}, bf16[256,512]{1,0:T(8,128)(2,1)S(1)}, u32[]{:S(2)}, u32[]{:S(2)}) collective-permute-start(bf16[256,512]{1,0:T(8,128)(2,1)S(1)} %get-tuple-element.64), channel_id=1, source_target_pairs={{0,24},{8,16},{16,8},{24,0},{1,25},{9,17},{17,9},{25,1},{2,26},{10... | collective-permute-start | bytes 786440 | tf_op jit(solution)/shard_map/ppermute | solution.py:315
  51.0 14.0 %collective-permute-start.20 = (bf16[128,512]{1,0:T(8,128)(2,1)S(1)}, bf16[128,512]{1,0:T(8,128)(2,1)S(1)}, u32[]{:S(2)}, u32[]{:S(2)}) collective-permute-start(bf16[128,512]{1,0:T(8,128)(2,1)S(1)} %get-tuple-element.60), channel_id=1, source_target_pairs={{0,24},{8,16},{16,8},{24,0},{1,25},{9,17},{17,9},{25,1},{2,26},{10... | collective-permute-start | bytes 393224 | tf_op jit(solution)/shard_map/ppermute | solution.py:315
  66.0 7.4 %collective-permute-start.16 = (bf16[128,512]{1,0:T(8,128)(2,1)S(1)}, bf16[128,512]{1,0:T(8,128)(2,1)S(1)}, u32[]{:S(2)}, u32[]{:S(2)}) collective-permute-start(bf16[128,512]{1,0:T(8,128)(2,1)S(1)} %get-tuple-element.55), channel_id=1, source_target_pairs={{0,16},{8,24},{16,0},{24,8},{1,17},{9,25},{17,1},{25,9},{2,18},{10... | collective-permute-start | bytes 393224 | tf_op jit(solution)/shard_map/ppermute | solution.py:315
  67.1 8.0 %collective-permute-start.17 = (bf16[128,512]{1,0:T(8,128)(2,1)S(1)}, bf16[128,512]{1,0:T(8,128)(2,1)S(1)}, u32[]{:S(2)}, u32[]{:S(2)}) collective-permute-start(bf16[128,512]{1,0:T(8,128)(2,1)S(1)} %get-tuple-element.56), channel_id=1, source_target_pairs={{0,24},{8,16},{16,8},{24,0},{1,25},{9,17},{17,9},{25,1},{2,26},{10... | collective-permute-start | bytes 393224 | tf_op jit(solution)/shard_map/ppermute | solution.py:315
  68.6 11.0 %collective-permute-start.21 = (bf16[128,512]{1,0:T(8,128)(2,1)S(1)}, bf16[128,512]{1,0:T(8,128)(2,1)S(1)}, u32[]{:S(2)}, u32[]{:S(2)}) collective-permute-start(bf16[128,512]{1,0:T(8,128)(2,1)S(1)} %shard_map.78), channel_id=1, source_target_pairs={{0,4},{1,5},{2,6},{3,7},{4,0},{5,1},{6,2},{7,3},{8,12},{9,13},{10,... | collective-permute-start | bytes 393224 | tf_op jit(solution)/shard_map/ppermute | solution.py:331
  71.2 8.4 %collective-permute-start.25 = (bf16[128,512]{1,0:T(8,128)(2,1)S(1)}, bf16[128,512]{1,0:T(8,128)(2,1)S(1)}, u32[]{:S(2)}, u32[]{:S(2)}) collective-permute-start(bf16[128,512]{1,0:T(8,128)(2,1)S(1)} %get-tuple-element.65), channel_id=1, source_target_pairs={{0,2},{1,3},{2,4},{3,5},{4,6},{5,7},{6,0},{7,1},{8,10},{9,11},{10,... | collective-permute-start | bytes 393224 | tf_op jit(solution)/shard_map/ppermute | solution.py:331
  73.5 6.8 %collective-permute-start.26 = (bf16[128,512]{1,0:T(8,128)(2,1)S(1)}, bf16[128,512]{1,0:T(8,128)(2,1)S(1)}, u32[]{:S(2)}, u32[]{:S(2)}) collective-permute-start(bf16[128,512]{1,0:T(8,128)(2,1)S(1)} %get-tuple-element.66), channel_id=1, source_target_pairs={{0,6},{1,7},{2,0},{3,1},{4,2},{5,3},{6,4},{7,5},{8,14},{9,15},{10,... | collective-permute-start | bytes 393224 | tf_op jit(solution)/shard_map/ppermute | solution.py:331
  (11 other events, 47.9 us)

commit v4 on v2

--- a/solution.py
+++ b/solution.py
@@ -1,4 +1,5 @@
 import functools
+import math
 
 import jax
 import jax.numpy as jnp
@@ -10,6 +11,7 @@
 STEPS = 4
 DIVISOR = 0.07
 TINY = 1e-06
+SLACK = 4
 LOG2E = 1.4426950408889634
 
 
@@ -20,13 +22,16 @@
 
 
 def call(body, outs, flops, *args, scratch=(), placed=()):
+    held = sum(math.prod(x.shape) * x.dtype.itemsize for x in args)
+    held += sum(math.prod(shape) * jnp.dtype(dtype).itemsize for shape, dtype in outs)
+    held += sum(math.prod(x.shape) * 4 for x in scratch if x.memory_space == pltpu.VMEM)
     return pl.pallas_call(
         body,
         out_shape=[jax.ShapeDtypeStruct(s, d) for s, d in outs],
         in_specs=[VMEM] * len(args),
         out_specs=[ANY if i in placed else VMEM for i in range(len(outs))],
         scratch_shapes=list(scratch),
-        compiler_params=pltpu.CompilerParams(vmem_limit_bytes=48 * 1024 * 1024),
+        compiler_params=pltpu.CompilerParams(vmem_limit_bytes=held + (SLACK << 20)),
         cost_estimate=pl.CostEstimate(flops=flops, transcendentals=0, bytes_accessed=1 << 20),
     )(*args)
 
@@ -158,9 +163,7 @@
     e_own = {d: refs.pop(0) if own_neg[d] else None for d in distances}
     e_par = {d: refs.pop(0) if par_neg[d] else None for d in distances}
     grads = refs.pop()
-    outs = [refs.pop(0) for _ in range(curve)]
-    w_own = {d: refs.pop(0) if own_neg[d] else None for d in distances}
-    w_par = {d: refs.pop(0) if par_neg[d] else None for d in distances}
+    outs = refs
     bank_rows = grads.shape[0]
     rows = bank_rows // curve
     anchors = q_own.shape[0]
@@ -169,19 +172,17 @@
         base = first_key(d, bank_rows, peers)
         grads[...] = jnp.zeros_like(grads)
 
-        def side(row, q_ref, p_ref, e_ref, w_ref):
+        def side(row, q_ref, p_ref, e_ref):
             def some(index):
                 at = span(index, step)
                 inverse, coef, _, _ = scalings(mine, other, row, at)
                 weights = weights_of(e_ref, at, bank_rows, p_ref[:, at] - base, inverse, coef)
-                if w_ref is not None:
-                    w_ref[:, at] = weights
                 grads[...] += nn_dot(weights, q_ref[at, :])
 
             loop(anchors // step, some)
 
-        side(0, q_own, p_own, e_own[d], w_own[d])
-        side(2, q_par, p_par, e_par[d], w_par[d])
+        side(0, q_own, p_own, e_own[d])
+        side(2, q_par, p_par, e_par[d])
         for turn in range(curve):
             cut = grads[span(lax.axis_index("curve") ^ turn, rows), :]
             outs[turn][number * rows : (number + 1) * rows, :] = cut.astype(outs[turn].dtype)
@@ -190,7 +191,7 @@
 def query_grad_body(p_ref, mine, other, *refs, negatives, peers, row):
     refs = list(refs)
     banks = [refs.pop(0) for _ in negatives]
-    kept = [refs.pop(0) if negative else None for negative in negatives]
+    grown = [refs.pop(0) if negative else None for negative in negatives]
     out = refs.pop(0)
     bank_rows = banks[0].shape[1]
     anchors = p_ref.shape[1]
@@ -201,12 +202,8 @@
         inverse, coef, _, _ = scalings(mine, other, row, at)
         total = None
         for d, bank in enumerate(banks):
-            if kept[d] is None:
-                place = p_ref[:, at] - first_key(d, bank_rows, peers)
-                weights = weights_of(None, at, bank_rows, place, inverse, coef)
-            else:
-                weights = kept[d][:, at]
-            part = nn_dot(bank[...], weights)
+            place = p_ref[:, at] - first_key(d, bank_rows, peers)
+            part = nn_dot(bank[...], weights_of(grown[d], at, bank_rows, place, inverse, coef))
             total = part if total is None else total + part
         out[:, at] = total.astype(out.dtype)
 
@@ -320,7 +317,7 @@
 
     stats = jnp.zeros((4, anchor_rows), F32)
     banks, own_grown, par_grown = {}, {}, {}
-    for d in [0] + far:
+    for d in [0] + sorted(far):
         parts = [keys] if d == 0 else across(arrived[d])
         outs = [((4, anchor_rows), F32), ((width, bank_rows), BF16)]
         outs += [((bank_rows, anchor_rows), BF16)] * (neg_own[d] + neg_par[d])
@@ -350,7 +347,6 @@
     other = partner(stats)
 
     returned, final = [], []
-    own_kept, par_kept = {}, {}
     for group in grad_groups(pairs):
         parts = call(
             functools.partial(
@@ -362,8 +358,7 @@
                 par_neg=neg_par,
             ),
             [((len(group) * rows, width), F32)]
-            + [((len(group) * rows, width), BF16)] * (curve - 1)
-            + [((bank_rows, anchor_rows), BF16)] * sum(neg_own[d] + neg_par[d] for d in group),
+            + [((len(group) * rows, width), BF16)] * (curve - 1),
             2 * block * len(group),
             *shared,
             stats,
@@ -372,10 +367,7 @@
             *[par_grown[d] for d in group if neg_par[d]],
             scratch=[pltpu.VMEM((bank_rows, width), F32)],
         )
-        weights = list(parts[curve:])
-        own_kept.update({d: weights.pop(0) for d in group if neg_own[d]})
-        par_kept.update({d: weights.pop(0) for d in group if neg_par[d]})
-        parts = exchange(parts[:curve])
+        parts = exchange(parts)
         if group == (0,):
             final = parts
             continue
@@ -387,7 +379,7 @@
         )
         returned += [to_ahead(x, d) for x, d in zip(sums, group)]
 
-    def query_grad(dtype, row, p, kept, negatives):
+    def query_grad(dtype, row, p, grown, negatives):
         return call(
             functools.partial(query_grad_body, negatives=negatives, peers=peers, row=row),
             [((width, anchor_rows), dtype)],
@@ -396,12 +388,12 @@
             stats,
             other,
             *[banks[d] for d in range(pairs)],
-            *[kept[d] for d in range(pairs) if negatives[d]],
+            *[grown[d] for d in range(pairs) if negatives[d]],
         )[0]
 
-    sent = query_grad(F32, 2, positive_par, par_kept, neg_par)
+    sent = query_grad(BF16, 2, positive_par, par_grown, neg_par)
     received = partner(sent)
-    own_part = query_grad(F32, 0, positive, own_kept, neg_own)
+    own_part = query_grad(F32, 0, positive, own_grown, neg_own)
 
     (mine,) = call(key_body, [((rows, width), BF16)], 1 << 20, own_keys, *final, *returned)
     step = sizes(anchor_rows, 256)

time: 103 us -> 93 us (0.903)
  Pallas kernels: 28.6 us -> 22.2 us
  waiting for transfers between devices: 26.2 us -> 32.1 us
  local copies, waits for them, and re-layouts: 6.15 us -> 1.25 us
  starting transfers between devices: 40.4 us -> 36.3 us
    pallas_call x16, Pallas kernels: 28.6 us -> 22.2 us  [call(): pl.pallas_call(body, out_shape=[jax.ShapeDtypeStruct(s, d) for s, d in ou...]
    unnamed x36 -> x10, local copies, waits for them, and re-layouts: 6.14 us -> 1.24 us
    ppermute x12, waiting for transfers between devices: 1.32 us -> 5.75 us  [across(): lax.ppermute(x, 'curve', [(i, i ^ turn) for i in range(curve)])]
    ppermute x3, starting transfers between devices: 6.9 us -> 3.52 us  [to_ahead(): lax.ppermute(x, 'blk', [(i, (i + 2 * distance) % peers) for i in range(pe...]
    ppermute x3, waiting for transfers between devices: 3.94 us -> 6.23 us  [from_ahead(): lax.ppermute(x, 'blk', [((i + 2 * distance) % peers, i) for i in range(pe...]
  transfers between devices with their start and end apart: 31 -> 31, of which waited for: 11 -> 14; matrix products, arithmetic and copies ran while one was open for 0% -> 0% of each run, Pallas kernels for 10% -> 16%
where the time goes in v4:
time: 93 us; the launch traced here: 92.9 us
  starting transfers between devices  36.3 us (39%)
  waiting for transfers between devices  32.1 us (35%)
  Pallas kernels  22.2 us (24%)
  local copies, waits for them, and re-layouts  1.25 us (1%)
  between operations  1.03 us (1%)
    pallas_call x16, Pallas kernels, call(): pl.pallas_call(body, out_shape=[jax.ShapeDtypeStruct(s, d) for s, d in ou...  22.2 us
    ppermute x12, starting transfers between devices, across(): lax.ppermute(x, 'curve', [(i, i ^ turn) for i in range(curve)])  15 us
    ppermute x9, waiting for transfers between devices, exchange(): moved.append(lax.ppermute(parts[turn], 'curve', route))  14.1 us
    ppermute x9, starting transfers between devices, exchange(): moved.append(lax.ppermute(parts[turn], 'curve', route))  10.7 us
    ppermute x3, waiting for transfers between devices, from_ahead(): lax.ppermute(x, 'blk', [((i + 2 * distance) % peers, i) for i in range(pe...  6.23 us
    ppermute x3, starting transfers between devices, from_ahead(): lax.ppermute(x, 'blk', [((i + 2 * distance) % peers, i) for i in range(pe...  6.13 us
    ppermute x12, waiting for transfers between devices, across(): lax.ppermute(x, 'curve', [(i, i ^ turn) for i in range(curve)])  5.75 us
    ppermute x3, waiting for transfers between devices, to_ahead(): lax.ppermute(x, 'blk', [(i, (i + 2 * distance) % peers) for i in range(pe...  3.66 us
  transfers between devices with their start and end apart: 31, of which 14 were waited for; matrix products, arithmetic and copies ran while one was open for 0% of the time, Pallas kernels for 16%

profile of v4, /device:TPU:0, one launch (start us, length us, event | category | flops | bytes accessed | tf_op | source)
XLA Modules:
  0.0 92.9 jit_solution(5011885913450963)
XLA Ops:
  3.1 5.1 %collective-permute-start.10 = (bf16[128,512]{1,0:T(8,128)(2,1)S(1)}, bf16[128,512]{1,0:T(8,128)(2,1)S(1)}, u32[]{:S(2)}, u32[]{:S(2)}) collective-permute-start(bf16[128,512]{1,0:T(8,128)(2,1)S(1)} %shard_map.67), channel_id=1, source_target_pairs={{2,0},{3,1},{4,2},{5,3},{6,4},{7,5},{0,6},{1,7},{10,8},{11,9},{12,... | collective-permute-start | bytes 393224 | tf_op jit(solution)/shard_map/ppermute | solution.py:300
  9.2 2.9 %collective-permute-done.10.refs_0_ = bf16[128,512]{1,0:T(8,128)(2,1)S(1)} collective-permute-done((bf16[128,512]{1,0:T(8,128)(2,1)S(1)}, bf16[128,512]{1,0:T(8,128)(2,1)S(1)}, u32[]{:S(2)}, u32[]{:S(2)}) %collective-permute-start.10) | collective-permute-done | bytes 131104 | tf_op jit(solution)/shard_map/ppermute | solution.py:300
  12.1 1.5 %collective-permute-start.11 = (bf16[128,512]{1,0:T(8,128)(2,1)S(1)}, bf16[128,512]{1,0:T(8,128)(2,1)S(1)}, u32[]{:S(2)}, u32[]{:S(2)}) collective-permute-start(bf16[128,512]{1,0:T(8,128)(2,1)S(1)} %collective-permute-done.10.refs_0_), channel_id=1, source_target_pairs={{0,8},{8,0},{16,24},{24,16},{1,9},{9,1},{17,25},{25,17},{2,10},{10... | collective-permute-start | bytes 393224 | tf_op jit(solution)/shard_map/ppermute | solution.py:286
  14.9 1.5 %collective-permute-start.12 = (bf16[128,512]{1,0:T(8,128)(2,1)S(1)}, bf16[128,512]{1,0:T(8,128)(2,1)S(1)}, u32[]{:S(2)}, u32[]{:S(2)}) collective-permute-start(bf16[128,512]{1,0:T(8,128)(2,1)S(1)} %collective-permute-done.10.refs_0_), channel_id=1, source_target_pairs={{0,16},{8,24},{16,0},{24,8},{1,17},{9,25},{17,1},{25,9},{2,18},{10... | collective-permute-start | bytes 393224 | tf_op jit(solution)/shard_map/ppermute | solution.py:286
  16.4 3.3 %collective-permute-done.6.refs_0_ = bf16[128,512]{1,0:T(8,128)(2,1)S(1)} collective-permute-done((bf16[128,512]{1,0:T(8,128)(2,1)S(1)}, bf16[128,512]{1,0:T(8,128)(2,1)S(1)}, u32[]{:S(2)}, u32[]{:S(2)}) %collective-permute-start.6) | collective-permute-done | bytes 131104 | tf_op jit(solution)/shard_map/ppermute | solution.py:300
  19.7 2.4 %collective-permute-start.13 = (bf16[128,512]{1,0:T(8,128)(2,1)S(1)}, bf16[128,512]{1,0:T(8,128)(2,1)S(1)}, u32[]{:S(2)}, u32[]{:S(2)}) collective-permute-start(bf16[128,512]{1,0:T(8,128)(2,1)S(1)} %collective-permute-done.10.refs_0_), channel_id=1, source_target_pairs={{0,24},{8,16},{16,8},{24,0},{1,25},{9,17},{17,9},{25,1},{2,26},{10... | collective-permute-start | bytes 393224 | tf_op jit(solution)/shard_map/ppermute | solution.py:286
  23.2 2.4 %collective-permute-start.9 = (bf16[128,512]{1,0:T(8,128)(2,1)S(1)}, bf16[128,512]{1,0:T(8,128)(2,1)S(1)}, u32[]{:S(2)}, u32[]{:S(2)}) collective-permute-start(bf16[128,512]{1,0:T(8,128)(2,1)S(1)} %collective-permute-done.6.refs_0_), channel_id=1, source_target_pairs={{0,24},{8,16},{16,8},{24,0},{1,25},{9,17},{17,9},{25,1},{2,26},{10... | collective-permute-start | bytes 393224 | tf_op jit(solution)/shard_map/ppermute | solution.py:286
  25.6 1.8 %shard_map.69 = (f32[4,1024]{1,0:T(4,128)S(1)}, bf16[512,512]{1,0:T(8,128)(2,1)S(1)}, bf16[512,1024]{1,0:T(8,128)(2,1)S(1)}, bf16[512,1024]{1,0:T(8,128)(2,1)S(1)}) custom-call(bf16[512,512]{1,0:T(8,128)(2,1)S(1)} %copy-done.2, s32[1,1024]{1,0:T(1,128)S(1)} %bitcast.4, s32[1,1024]{1,0:T(1,128)S(1)} %collective-permute-done.4.refs_2_.refs_5_.p_ref.refs_1_, ...), custom_call_target="tpu_custom_call" | custom-call | flops 1073741824 | bytes 1048576 | tf_op jit(solution)/shard_map/pallas_call | solution.py:28
  31.3 1.9 %shard_map.70 = (f32[4,1024]{1,0:T(4,128)S(1)}, bf16[512,512]{1,0:T(8,128)(2,1)S(1)}, bf16[512,1024]{1,0:T(8,128)(2,1)S(1)}, bf16[512,1024]{1,0:T(8,128)(2,1)S(1)}) custom-call(bf16[128,512]{1,0:T(8,128)(2,1)S(1)} %collective-permute-done.10.refs_0_, bf16[128,512]{1,0:T(8,128)(2,1)S(1)} %collective-permute-done.11.refs_1_, ...), custom_call_target="tpu_custom_call" | custom-call | flops 1073741824 | bytes 1048576 | tf_op jit(solution)/shard_map/pallas_call | solution.py:28
  33.1 2.0 %shard_map.71 = (f32[4,1024]{1,0:T(4,128)S(1)}, bf16[512,512]{1,0:T(8,128)(2,1)S(1)}, bf16[512,1024]{1,0:T(8,128)(2,1)S(1)}, bf16[512,1024]{1,0:T(8,128)(2,1)S(1)}) custom-call(bf16[128,512]{1,0:T(8,128)(2,1)S(1)} %collective-permute-done.6.refs_0_, bf16[128,512]{1,0:T(8,128)(2,1)S(1)} %collective-permute-done.7.refs_1_, ...), custom_call_target="tpu_custom_call" | custom-call | flops 1073741824 | bytes 1048576 | tf_op jit(solution)/shard_map/pallas_call | solution.py:28
  35.4 1.4 %collective-permute-done.2.refs_2_ = bf16[128,512]{1,0:T(8,128)(2,1)S(1)} collective-permute-done((bf16[128,512]{1,0:T(8,128)(2,1)S(1)}, bf16[128,512]{1,0:T(8,128)(2,1)S(1)}, u32[]{:S(2)}, u32[]{:S(2)}) %collective-permute-start.2) | collective-permute-done | bytes 131104 | tf_op jit(solution)/shard_map/ppermute | solution.py:286
  39.4 2.5 %shard_map.74 = bf16[512,1024]{1,0:T(8,128)(2,1)S(1)} custom-call(s32[1,1024]{1,0:T(1,128)S(1)} %collective-permute-done.4.refs_2_.refs_5_.p_ref.refs_1_, f32[4,1024]{1,0:T(4,128)S(1)} %get-tuple-element.36.mine.refs_4_, f32[4,1024]{1,0:T(4,128)S(1)} %collective-permute-done.14.other.refs_5_, bf16[512,512]{1,0:T(8,128)(2,1)S(1)} %get-tuple-element.37.refs_0_, ...), custom_call_target="tpu_custom_call" | custom-call | flops 2147483648 | bytes 1048576 | tf_op jit(solution)/shard_map/pallas_call | solution.py:28
  43.5 1.6 %collective-permute-start.19 = (bf16[128,512]{1,0:T(8,128)(2,1)S(1)}, bf16[128,512]{1,0:T(8,128)(2,1)S(1)}, u32[]{:S(2)}, u32[]{:S(2)}) collective-permute-start(bf16[128,512]{1,0:T(8,128)(2,1)S(1)} %get-tuple-element.54), channel_id=1, source_target_pairs={{0,8},{8,0},{16,24},{24,16},{1,9},{9,1},{17,25},{25,17},{2,10},{10... | collective-permute-start | bytes 393224 | tf_op jit(solution)/shard_map/ppermute | solution.py:293
  46.4 2.5 %shard_map.79 = (f32[256,512]{1,0:T(8,128)S(1)}, bf16[256,512]{1,0:T(8,128)(2,1)S(1)}, bf16[256,512]{1,0:T(8,128)(2,1)S(1)}, bf16[256,512]{1,0:T(8,128)(2,1)S(1)}) custom-call(s32[1,1024]{1,0:T(1,128)S(1)} %bitcast.9, s32[1,1024]{1,0:T(1,128)S(1)} %collective-permute-done.4.refs_2_.refs_5_.p_ref.refs_1_, ...), custom_call_target="tpu_custom_call" | custom-call | flops 2147483648 | bytes 1048576 | tf_op jit(solution)/shard_map/pallas_call | solution.py:28
  50.2 2.3 %collective-permute-start.25 = (bf16[256,512]{1,0:T(8,128)(2,1)S(1)}, bf16[256,512]{1,0:T(8,128)(2,1)S(1)}, u32[]{:S(2)}, u32[]{:S(2)}) collective-permute-start(bf16[256,512]{1,0:T(8,128)(2,1)S(1)} %get-tuple-element.60), channel_id=1, source_target_pairs={{0,24},{8,16},{16,8},{24,0},{1,25},{9,17},{17,9},{25,1},{2,26},{10... | collective-permute-start | bytes 786440 | tf_op jit(solution)/shard_map/ppermute | solution.py:293
  54.4 11.1 %collective-permute-done.21.refs_3_ = bf16[128,512]{1,0:T(8,128)(2,1)S(1)} collective-permute-done((bf16[128,512]{1,0:T(8,128)(2,1)S(1)}, bf16[128,512]{1,0:T(8,128)(2,1)S(1)}, u32[]{:S(2)}, u32[]{:S(2)}) %collective-permute-start.21) | collective-permute-done | bytes 131104 | tf_op jit(solution)/shard_map/ppermute | solution.py:293
  67.6 1.6 %collective-permute-start.18 = (bf16[128,512]{1,0:T(8,128)(2,1)S(1)}, bf16[128,512]{1,0:T(8,128)(2,1)S(1)}, u32[]{:S(2)}, u32[]{:S(2)}) collective-permute-start(bf16[128,512]{1,0:T(8,128)(2,1)S(1)} %get-tuple-element.52), channel_id=1, source_target_pairs={{0,24},{8,16},{16,8},{24,0},{1,25},{9,17},{17,9},{25,1},{2,26},{10... | collective-permute-start | bytes 393224 | tf_op jit(solution)/shard_map/ppermute | solution.py:293
  69.3 2.1 %collective-permute-done.16.refs_1_ = bf16[128,512]{1,0:T(8,128)(2,1)S(1)} collective-permute-done((bf16[128,512]{1,0:T(8,128)(2,1)S(1)}, bf16[128,512]{1,0:T(8,128)(2,1)S(1)}, u32[]{:S(2)}, u32[]{:S(2)}) %collective-permute-start.16) | collective-permute-done | bytes 131104 | tf_op jit(solution)/shard_map/ppermute | solution.py:293
  72.3 3.5 %collective-permute-start.27 = (bf16[128,512]{1,0:T(8,128)(2,1)S(1)}, bf16[128,512]{1,0:T(8,128)(2,1)S(1)}, u32[]{:S(2)}, u32[]{:S(2)}) collective-permute-start(bf16[128,512]{1,0:T(8,128)(2,1)S(1)} %get-tuple-element.62), channel_id=1, source_target_pairs={{0,6},{1,7},{2,0},{3,1},{4,2},{5,3},{6,4},{7,5},{8,14},{9,15},{10,... | collective-permute-start | bytes 393224 | tf_op jit(solution)/shard_map/ppermute | solution.py:303
  75.8 3.1 %collective-permute-done.22.refs_4_ = bf16[128,512]{1,0:T(8,128)(2,1)S(1)} collective-permute-done((bf16[128,512]{1,0:T(8,128)(2,1)S(1)}, bf16[128,512]{1,0:T(8,128)(2,1)S(1)}, u32[]{:S(2)}, u32[]{:S(2)}) %collective-permute-start.22) | collective-permute-done | bytes 131104 | tf_op jit(solution)/shard_map/ppermute | solution.py:303
  79.8 1.6 %collective-permute-start.28 = (bf16[128,512]{1,0:T(8,128)(2,1)S(1)}, bf16[128,512]{1,0:T(8,128)(2,1)S(1)}, u32[]{:S(2)}, u32[]{:S(2)}) collective-permute-start(bf16[128,512]{1,0:T(8,128)(2,1)S(1)} %shard_map.81.refs_0_), channel_id=1, source_target_pairs={{0,8},{8,0},{16,24},{24,16},{1,9},{9,1},{17,25},{25,17},{2,10},{10... | collective-permute-start | bytes 393224 | tf_op jit(solution)/shard_map/ppermute | solution.py:286
  83.3 2.5 %shard_map.73.left = f32[512,1024]{1,0:T(8,128)S(1)} custom-call(s32[1,1024]{1,0:T(1,128)S(1)} %bitcast.11, f32[4,1024]{1,0:T(4,128)S(1)} %get-tuple-element.36.mine.refs_4_, f32[4,1024]{1,0:T(4,128)S(1)} %collective-permute-done.14.other.refs_5_, bf16[512,512]{1,0:T(8,128)(2,1)S(1)} %get-tuple-element.37.refs_0_, ...), custom_call_target="tpu_custom_call" | custom-call | flops 2147483648 | bytes 1048576 | tf_op jit(solution)/shard_map/pallas_call | solution.py:28
  86.3 2.3 %collective-permute-done.30.refs_3_ = bf16[128,512]{1,0:T(8,128)(2,1)S(1)} collective-permute-done((bf16[128,512]{1,0:T(8,128)(2,1)S(1)}, bf16[128,512]{1,0:T(8,128)(2,1)S(1)}, u32[]{:S(2)}, u32[]{:S(2)}) %collective-permute-start.30) | collective-permute-done | bytes 131104 | tf_op jit(solution)/shard_map/ppermute | solution.py:286
  89.7 3.0 %shard_map.75 = (f32[1024,512]{1,0:T(8,128)}, f32[1,1024]{1,0:T(1,128)}) custom-call(f32[4,1024]{1,0:T(4,128)S(1)} %get-tuple-element.36.mine.refs_4_, f32[4,1024]{1,0:T(4,128)S(1)} %collective-permute-done.14.other.refs_5_, bf16[1024,512]{1,0:T(8,128)(2,1)S(1)} %copy-done.1, f32[512,1024]{1,0:T(8,128)S(1)} %shard_map.73.left, ...), custom_call_target="tpu_custom_call" | custom-call | flops 4194304 | bytes 1048576 | tf_op jit(solution)/shard_map/pallas_call | solution.py:28
  (68 shorter events, 25.8 us)
Async XLA Ops:
  2.4 20.8 %collective-permute-start.5 = (bf16[1024,512]{1,0:T(8,128)(2,1)S(1)}, bf16[1024,512]{1,0:T(8,128)(2,1)S(1)}, u32[]{:S(2)}, u32[]{:S(2)}) collective-permute-start(bf16[1024,512]{1,0:T(8,128)(2,1)S(1)} %shard_map.68.refs_3_.refs_6_.refs_2_), channel_id=1, source_target_pairs={{0,1},{1,0},{2,3},{3,2},{4,5},{5,4},{6,7},{7,6},{8,9},{9,8},{10,11... | collective-permute-start | bytes 3145736 | tf_op jit(solution)/shard_map/ppermute | solution.py:297
  3.1 9.1 %collective-permute-start.10 = (bf16[128,512]{1,0:T(8,128)(2,1)S(1)}, bf16[128,512]{1,0:T(8,128)(2,1)S(1)}, u32[]{:S(2)}, u32[]{:S(2)}) collective-permute-start(bf16[128,512]{1,0:T(8,128)(2,1)S(1)} %shard_map.67), channel_id=1, source_target_pairs={{2,0},{3,1},{4,2},{5,3},{6,4},{7,5},{0,6},{1,7},{10,8},{11,9},{12,... | collective-permute-start | bytes 393224 | tf_op jit(solution)/shard_map/ppermute | solution.py:300
  8.2 11.5 %collective-permute-start.6 = (bf16[128,512]{1,0:T(8,128)(2,1)S(1)}, bf16[128,512]{1,0:T(8,128)(2,1)S(1)}, u32[]{:S(2)}, u32[]{:S(2)}) collective-permute-start(bf16[128,512]{1,0:T(8,128)(2,1)S(1)} %shard_map.67), channel_id=1, source_target_pairs={{4,0},{5,1},{6,2},{7,3},{0,4},{1,5},{2,6},{3,7},{12,8},{13,9},{14,... | collective-permute-start | bytes 393224 | tf_op jit(solution)/shard_map/ppermute | solution.py:300
  8.2 14.0 %collective-permute-start = (bf16[128,512]{1,0:T(8,128)(2,1)S(1)}, bf16[128,512]{1,0:T(8,128)(2,1)S(1)}, u32[]{:S(2)}, u32[]{:S(2)}) collective-permute-start(bf16[128,512]{1,0:T(8,128)(2,1)S(1)} %shard_map.67), channel_id=1, source_target_pairs={{6,0},{7,1},{0,2},{1,3},{2,4},{3,5},{4,6},{5,7},{14,8},{15,9},{8,1... | collective-permute-start | bytes 393224 | tf_op jit(solution)/shard_map/ppermute | solution.py:300
  12.1 10.5 %collective-permute-start.11 = (bf16[128,512]{1,0:T(8,128)(2,1)S(1)}, bf16[128,512]{1,0:T(8,128)(2,1)S(1)}, u32[]{:S(2)}, u32[]{:S(2)}) collective-permute-start(bf16[128,512]{1,0:T(8,128)(2,1)S(1)} %collective-permute-done.10.refs_0_), channel_id=1, source_target_pairs={{0,8},{8,0},{16,24},{24,16},{1,9},{9,1},{17,25},{25,17},{2,10},{10... | collective-permute-start | bytes 393224 | tf_op jit(solution)/shard_map/ppermute | solution.py:286
  14.9 12.6 %collective-permute-start.12 = (bf16[128,512]{1,0:T(8,128)(2,1)S(1)}, bf16[128,512]{1,0:T(8,128)(2,1)S(1)}, u32[]{:S(2)}, u32[]{:S(2)}) collective-permute-start(bf16[128,512]{1,0:T(8,128)(2,1)S(1)} %collective-permute-done.10.refs_0_), channel_id=1, source_target_pairs={{0,16},{8,24},{16,0},{24,8},{1,17},{9,25},{17,1},{25,9},{2,18},{10... | collective-permute-start | bytes 393224 | tf_op jit(solution)/shard_map/ppermute | solution.py:286
  19.7 8.4 %collective-permute-start.13 = (bf16[128,512]{1,0:T(8,128)(2,1)S(1)}, bf16[128,512]{1,0:T(8,128)(2,1)S(1)}, u32[]{:S(2)}, u32[]{:S(2)}) collective-permute-start(bf16[128,512]{1,0:T(8,128)(2,1)S(1)} %collective-permute-done.10.refs_0_), channel_id=1, source_target_pairs={{0,24},{8,16},{16,8},{24,0},{1,25},{9,17},{17,9},{25,1},{2,26},{10... | collective-permute-start | bytes 393224 | tf_op jit(solution)/shard_map/ppermute | solution.py:286
  22.1 7.7 %collective-permute-start.7 = (bf16[128,512]{1,0:T(8,128)(2,1)S(1)}, bf16[128,512]{1,0:T(8,128)(2,1)S(1)}, u32[]{:S(2)}, u32[]{:S(2)}) collective-permute-start(bf16[128,512]{1,0:T(8,128)(2,1)S(1)} %collective-permute-done.6.refs_0_), channel_id=1, source_target_pairs={{0,8},{8,0},{16,24},{24,16},{1,9},{9,1},{17,25},{25,17},{2,10},{10... | collective-permute-start | bytes 393224 | tf_op jit(solution)/shard_map/ppermute | solution.py:286
  22.7 10.4 %collective-permute-start.8 = (bf16[128,512]{1,0:T(8,128)(2,1)S(1)}, bf16[128,512]{1,0:T(8,128)(2,1)S(1)}, u32[]{:S(2)}, u32[]{:S(2)}) collective-permute-start(bf16[128,512]{1,0:T(8,128)(2,1)S(1)} %collective-permute-done.6.refs_0_), channel_id=1, source_target_pairs={{0,16},{8,24},{16,0},{24,8},{1,17},{9,25},{17,1},{25,9},{2,18},{10... | collective-permute-start | bytes 393224 | tf_op jit(solution)/shard_map/ppermute | solution.py:286
  23.2 9.9 %collective-permute-start.9 = (bf16[128,512]{1,0:T(8,128)(2,1)S(1)}, bf16[128,512]{1,0:T(8,128)(2,1)S(1)}, u32[]{:S(2)}, u32[]{:S(2)}) collective-permute-start(bf16[128,512]{1,0:T(8,128)(2,1)S(1)} %collective-permute-done.6.refs_0_), channel_id=1, source_target_pairs={{0,24},{8,16},{16,8},{24,0},{1,25},{9,17},{17,9},{25,1},{2,26},{10... | collective-permute-start | bytes 393224 | tf_op jit(solution)/shard_map/ppermute | solution.py:286
  27.5 7.9 %collective-permute-start.1 = (bf16[128,512]{1,0:T(8,128)(2,1)S(1)}, bf16[128,512]{1,0:T(8,128)(2,1)S(1)}, u32[]{:S(2)}, u32[]{:S(2)}) collective-permute-start(bf16[128,512]{1,0:T(8,128)(2,1)S(1)} %collective-permute-done.refs_0_), channel_id=1, source_target_pairs={{0,8},{8,0},{16,24},{24,16},{1,9},{9,1},{17,25},{25,17},{2,10},{10... | collective-permute-start | bytes 393224 | tf_op jit(solution)/shard_map/ppermute | solution.py:286
  28.1 8.8 %collective-permute-start.2 = (bf16[128,512]{1,0:T(8,128)(2,1)S(1)}, bf16[128,512]{1,0:T(8,128)(2,1)S(1)}, u32[]{:S(2)}, u32[]{:S(2)}) collective-permute-start(bf16[128,512]{1,0:T(8,128)(2,1)S(1)} %collective-permute-done.refs_0_), channel_id=1, source_target_pairs={{0,16},{8,24},{16,0},{24,8},{1,17},{9,25},{17,1},{25,9},{2,18},{10... | collective-permute-start | bytes 393224 | tf_op jit(solution)/shard_map/ppermute | solution.py:286
  29.8 7.0 %collective-permute-start.3 = (bf16[128,512]{1,0:T(8,128)(2,1)S(1)}, bf16[128,512]{1,0:T(8,128)(2,1)S(1)}, u32[]{:S(2)}, u32[]{:S(2)}) collective-permute-start(bf16[128,512]{1,0:T(8,128)(2,1)S(1)} %collective-permute-done.refs_0_), channel_id=1, source_target_pairs={{0,24},{8,16},{16,8},{24,0},{1,25},{9,17},{17,9},{25,1},{2,26},{10... | collective-permute-start | bytes 393224 | tf_op jit(solution)/shard_map/ppermute | solution.py:286
  41.9 47.8 %collective-permute-start.15 = (bf16[512,1024]{1,0:T(8,128)(2,1)S(1)}, bf16[512,1024]{1,0:T(8,128)(2,1)S(1)}, u32[]{:S(2)}, u32[]{:S(2)}) collective-permute-start(bf16[512,1024]{1,0:T(8,128)(2,1)S(1)} %shard_map.74), channel_id=1, source_target_pairs={{0,1},{1,0},{2,3},{3,2},{4,5},{5,4},{6,7},{7,6},{8,9},{9,8},{10,11... | collective-permute-start | bytes 3145736 | tf_op jit(solution)/shard_map/ppermute | solution.py:297
  43.5 6.7 %collective-permute-start.19 = (bf16[128,512]{1,0:T(8,128)(2,1)S(1)}, bf16[128,512]{1,0:T(8,128)(2,1)S(1)}, u32[]{:S(2)}, u32[]{:S(2)}) collective-permute-start(bf16[128,512]{1,0:T(8,128)(2,1)S(1)} %get-tuple-element.54), channel_id=1, source_target_pairs={{0,8},{8,0},{16,24},{24,16},{1,9},{9,1},{17,25},{25,17},{2,10},{10... | collective-permute-start | bytes 393224 | tf_op jit(solution)/shard_map/ppermute | solution.py:293
  45.0 7.5 %collective-permute-start.20 = (bf16[128,512]{1,0:T(8,128)(2,1)S(1)}, bf16[128,512]{1,0:T(8,128)(2,1)S(1)}, u32[]{:S(2)}, u32[]{:S(2)}) collective-permute-start(bf16[128,512]{1,0:T(8,128)(2,1)S(1)} %get-tuple-element.55), channel_id=1, source_target_pairs={{0,16},{8,24},{16,0},{24,8},{1,17},{9,25},{17,1},{25,9},{2,18},{10... | collective-permute-start | bytes 393224 | tf_op jit(solution)/shard_map/ppermute | solution.py:293
  49.0 17.2 %collective-permute-start.23 = (bf16[256,512]{1,0:T(8,128)(2,1)S(1)}, bf16[256,512]{1,0:T(8,128)(2,1)S(1)}, u32[]{:S(2)}, u32[]{:S(2)}) collective-permute-start(bf16[256,512]{1,0:T(8,128)(2,1)S(1)} %get-tuple-element.58), channel_id=1, source_target_pairs={{0,8},{8,0},{16,24},{24,16},{1,9},{9,1},{17,25},{25,17},{2,10},{10... | collective-permute-start | bytes 786440 | tf_op jit(solution)/shard_map/ppermute | solution.py:293
  49.6 18.1 %collective-permute-start.24 = (bf16[256,512]{1,0:T(8,128)(2,1)S(1)}, bf16[256,512]{1,0:T(8,128)(2,1)S(1)}, u32[]{:S(2)}, u32[]{:S(2)}) collective-permute-start(bf16[256,512]{1,0:T(8,128)(2,1)S(1)} %get-tuple-element.59), channel_id=1, source_target_pairs={{0,16},{8,24},{16,0},{24,8},{1,17},{9,25},{17,1},{25,9},{2,18},{10... | collective-permute-start | bytes 786440 | tf_op jit(solution)/shard_map/ppermute | solution.py:293
  50.2 19.0 %collective-permute-start.25 = (bf16[256,512]{1,0:T(8,128)(2,1)S(1)}, bf16[256,512]{1,0:T(8,128)(2,1)S(1)}, u32[]{:S(2)}, u32[]{:S(2)}) collective-permute-start(bf16[256,512]{1,0:T(8,128)(2,1)S(1)} %get-tuple-element.60), channel_id=1, source_target_pairs={{0,24},{8,16},{16,8},{24,0},{1,25},{9,17},{17,9},{25,1},{2,26},{10... | collective-permute-start | bytes 786440 | tf_op jit(solution)/shard_map/ppermute | solution.py:293
  52.5 13.1 %collective-permute-start.21 = (bf16[128,512]{1,0:T(8,128)(2,1)S(1)}, bf16[128,512]{1,0:T(8,128)(2,1)S(1)}, u32[]{:S(2)}, u32[]{:S(2)}) collective-permute-start(bf16[128,512]{1,0:T(8,128)(2,1)S(1)} %get-tuple-element.56), channel_id=1, source_target_pairs={{0,24},{8,16},{16,8},{24,0},{1,25},{9,17},{17,9},{25,1},{2,26},{10... | collective-permute-start | bytes 393224 | tf_op jit(solution)/shard_map/ppermute | solution.py:293
  67.6 8.2 %collective-permute-start.18 = (bf16[128,512]{1,0:T(8,128)(2,1)S(1)}, bf16[128,512]{1,0:T(8,128)(2,1)S(1)}, u32[]{:S(2)}, u32[]{:S(2)}) collective-permute-start(bf16[128,512]{1,0:T(8,128)(2,1)S(1)} %get-tuple-element.52), channel_id=1, source_target_pairs={{0,24},{8,16},{16,8},{24,0},{1,25},{9,17},{17,9},{25,1},{2,26},{10... | collective-permute-start | bytes 393224 | tf_op jit(solution)/shard_map/ppermute | solution.py:293
  69.2 9.7 %collective-permute-start.22 = (bf16[128,512]{1,0:T(8,128)(2,1)S(1)}, bf16[128,512]{1,0:T(8,128)(2,1)S(1)}, u32[]{:S(2)}, u32[]{:S(2)}) collective-permute-start(bf16[128,512]{1,0:T(8,128)(2,1)S(1)} %shard_map.78), channel_id=1, source_target_pairs={{0,4},{1,5},{2,6},{3,7},{4,0},{5,1},{6,2},{7,3},{8,12},{9,13},{10,... | collective-permute-start | bytes 393224 | tf_op jit(solution)/shard_map/ppermute | solution.py:303
  71.4 7.5 %collective-permute-start.26 = (bf16[128,512]{1,0:T(8,128)(2,1)S(1)}, bf16[128,512]{1,0:T(8,128)(2,1)S(1)}, u32[]{:S(2)}, u32[]{:S(2)}) collective-permute-start(bf16[128,512]{1,0:T(8,128)(2,1)S(1)} %get-tuple-element.61), channel_id=1, source_target_pairs={{0,2},{1,3},{2,4},{3,5},{4,6},{5,7},{6,0},{7,1},{8,10},{9,11},{10,... | collective-permute-start | bytes 393224 | tf_op jit(solution)/shard_map/ppermute | solution.py:303
  72.3 7.2 %collective-permute-start.27 = (bf16[128,512]{1,0:T(8,128)(2,1)S(1)}, bf16[128,512]{1,0:T(8,128)(2,1)S(1)}, u32[]{:S(2)}, u32[]{:S(2)}) collective-permute-start(bf16[128,512]{1,0:T(8,128)(2,1)S(1)} %get-tuple-element.62), channel_id=1, source_target_pairs={{0,6},{1,7},{2,0},{3,1},{4,2},{5,3},{6,4},{7,5},{8,14},{9,15},{10,... | collective-permute-start | bytes 393224 | tf_op jit(solution)/shard_map/ppermute | solution.py:303
  (12 other events, 61.1 us)
